TPU v7x, 8 devices: a whole 2x2x1 slice. The times are simulated.
8 devices in a mesh: dp: 2 (over z, y), cp: 4 (over x, core).
Axes of the slice: x: 2, y: 2, z: 1, core: 2. Of those that a mesh axis runs over, the one named last changes fastest.
Arguments:
- x_act: bfloat16 [8192, 1536], P(('dp', 'cp')), parts along dimension 0
- seg_ids: int32 [8192], P(('dp', 'cp')), parts along dimension 0
- w_q: bfloat16 [1536, 12, 128], replicated
- w_k: bfloat16 [1536, 2, 128], replicated
- w_v: bfloat16 [1536, 2, 128], replicated
- w_o: bfloat16 [1536, 12, 128], replicated
- dy_act: bfloat16 [8192, 1536], P(('dp', 'cp')), parts along dimension 0
Outputs:
- output 1: bfloat16 [8192, 1536], P(('dp', 'cp')), parts along dimension 0
- output 2: bfloat16 [8192, 1536], P(('dp', 'cp')), parts along dimension 0
- output 3: float32 [3072, 12, 128], P(('dp', 'cp')), parts along dimension 0
- output 4: float32 [3072, 2, 128], P(('dp', 'cp')), parts along dimension 0
- output 5: float32 [3072, 2, 128], P(('dp', 'cp')), parts along dimension 0
- output 6: float32 [3072, 12, 128], P(('dp', 'cp')), parts along dimension 0
There are 2 independent parts. A program takes and returns all parts, laid end to end along the dimension named above; an argument that names none is the same for every part.
All inputs are finite; a program needn't handle non-finite values.
Results may differ from a plain program's by a relative error of at most 0.02.
Values are sent between devices in bfloat16 or wider.
A program may use at most 1 GiB of HBM per device.

v0:
```python
import functools
import math

import jax
import jax.numpy as jnp
from jax import lax
from jax.experimental import pallas as pl
from jax.experimental.pallas import tpu as pltpu
from jax.sharding import PartitionSpec as P

BLK = 256
HEADS = 6
HD = 128
WIDE = HEADS * BLK
HALF = 8
VMEM_LIMIT = 60 * 1024 * 1024


def dot(a, b):
    return jnp.dot(a, b, preferred_element_type=jnp.float32)


def dot_nt(a, b):
    return lax.dot_general(a, b, (((1,), (1,)), ((), ())), preferred_element_type=jnp.float32)


def stack_heads(src, dst):
    for h in range(HEADS):
        dst[h * BLK:(h + 1) * BLK, :] = src[:, h * HD:(h + 1) * HD]


def flip_heads(src, dst):
    for h in range(HEADS):
        dst[:, h * BLK:(h + 1) * BLK] = src[:, h * HD:(h + 1) * HD].T


def store_block(p, core):
    return (p & HALF) + ((p + 4 * core) & (HALF - 1))


def first_block(seg_ref, ids_ref, step):
    chip = ids_ref[1]
    first = seg_ref[(HALF + step) * BLK]
    near = jnp.int32(0)
    far = jnp.int32(0)
    for b in range(HALF):
        far += (seg_ref[b * BLK + BLK - 1] < first).astype(jnp.int32)
        near += (seg_ref[(HALF + b) * BLK + BLK - 1] < first).astype(jnp.int32)
    far = jnp.where(chip == 0, HALF, far)
    return far + near


def spread_segments(rows_ref, dst, first, count):
    for b in range(count):
        row = jnp.broadcast_to(rows_ref[first + b], (128, BLK))
        dst[b * BLK:(b + 1) * BLK, :] = row.T


def pair_mask(segk, segq, key_block, query_block):
    segk = jnp.concatenate([segk] * (BLK // 128), axis=1)
    same = segk == segq
    rel = (lax.broadcasted_iota(jnp.int32, (BLK, BLK), 0)
           - lax.broadcasted_iota(jnp.int32, (BLK, BLK), 1))
    return same & (rel <= (query_block - key_block) * BLK)


def fwd_kernel(seg_ref, ids_ref, q_own, q_oth, kv_far, kv_near, rows_ref,
               o_own, o_oth, lse_ref, segk, kv_ref, qt, acc, m_ref, l_ref, f_ref, pm):
    step = pl.program_id(0)
    core = ids_ref[0]
    scale2 = HD ** -0.5 * math.log2(math.e)

    @pl.when(step == 0)
    def _():
        spread_segments(rows_ref, segk, 0, 2 * HALF)
        kv_ref[:HALF * BLK, :] = kv_far[...]
        kv_ref[HALF * BLK:, :] = kv_near[...]

    @pl.when(step < 4)
    def _():
        flip_heads(q_own, qt)

    @pl.when(step >= 4)
    def _():
        flip_heads(q_oth, qt)

    acc[...] = jnp.zeros_like(acc)
    m_ref[...] = jnp.full_like(m_ref, -jnp.inf)
    l_ref[...] = jnp.zeros_like(l_ref)
    hi = HALF + ((step + 4 * core) & (HALF - 1))
    count = hi - first_block(seg_ref, ids_ref, step) + 1
    segq = rows_ref[HALF + step]

    def body(it, carry):
        p = hi - it
        key_start = pl.multiple_of(store_block(p, core) * BLK, BLK)
        k_blk = kv_ref[pl.ds(key_start, BLK), :HD]
        v_t = kv_ref[pl.ds(key_start, BLK), HD:].T
        mask = pair_mask(segk[pl.ds(key_start, BLK), :], segq, p, hi)
        for h in range(HEADS):
            cols = slice(h * BLK, (h + 1) * BLK)
            s = jnp.where(mask, dot(k_blk, qt[:, cols]) * scale2, -jnp.inf)
            m_old = m_ref[:, cols]
            m_new = jnp.maximum(m_old, jnp.max(s, axis=0, keepdims=True))
            w = jnp.exp2(s - m_new)
            fac = jnp.exp2(m_old - m_new)
            m_ref[:, cols] = m_new
            l_ref[:, cols] = l_ref[:, cols] * fac + jnp.sum(w, axis=0, keepdims=True)
            f_ref[:, cols] = fac
            pm[:, cols] = w.astype(jnp.bfloat16)
        acc[...] = acc[...] * f_ref[...] + dot(v_t, pm[...])
        return carry

    lax.fori_loop(0, count, body, 0)
    total = l_ref[...]
    lse_ref[0] = m_ref[...] + jnp.log2(total)
    inv = 1.0 / total

    def put(dst):
        for h in range(HEADS):
            cols = slice(h * BLK, (h + 1) * BLK)
            dst[:, h * HD:(h + 1) * HD] = (acc[:, cols] * inv[:, cols]).T.astype(jnp.bfloat16)

    @pl.when(step < 4)
    def _():
        put(o_own)

    @pl.when(step >= 4)
    def _():
        put(o_oth)


def bwd_kernel(remote, *refs):
    if remote:
        (seg_ref, ids_ref, q_own, q_oth, do_own, do_oth, o_own, o_oth, kv_ref,
         rows_ref, lse_ref, dq_out, dkv_ref,
         segk, qs, qt, ds_, dt, delta, pm, sm, dqt) = refs
    else:
        (seg_ref, ids_ref, q_own, q_oth, do_own, do_oth, o_own, o_oth, kv_ref,
         rows_ref, lse_ref, dq_in, dq_own, dq_oth, dkv_ref,
         segk, qs, qt, ds_, dt, delta, pm, sm, dqt) = refs
    step = pl.program_id(0)
    core = ids_ref[0]
    scale = HD ** -0.5
    scale2 = scale * math.log2(math.e)

    @pl.when(step == 0)
    def _():
        dkv_ref[...] = jnp.zeros_like(dkv_ref)
        spread_segments(rows_ref, segk, 0 if remote else HALF, HALF)

    query = HALF + ((step + 4 * core) & (HALF - 1))
    first = first_block(seg_ref, ids_ref, step)
    if remote:
        lo, hi = first, jnp.int32(HALF - 1)
    else:
        lo, hi = jnp.maximum(first, HALF), query
    count = hi - lo + 1
    segq = rows_ref[HALF + step]

    def prepare(q, do, o):
        stack_heads(q, qs)
        flip_heads(q, qt)
        stack_heads(do, ds_)
        flip_heads(do, dt)
        for h in range(HEADS):
            hc = slice(h * HD, (h + 1) * HD)
            prod = do[:, hc].astype(jnp.float32) * o[:, hc].astype(jnp.float32)
            delta[:, h * BLK:(h + 1) * BLK] = jnp.sum(prod.T, axis=0, keepdims=True)

    @pl.when((step < 4) & (count > 0))
    def _():
        prepare(q_own, do_own, o_own)

    @pl.when((step >= 4) & (count > 0))
    def _():
        prepare(q_oth, do_oth, o_oth)

    if remote:
        dqt[...] = jnp.zeros_like(dqt)
    else:
        dqt[...] = dq_in[0]

    def body(it, carry):
        p = lo + it
        key_start = pl.multiple_of((store_block(p, core) & (HALF - 1)) * BLK, BLK)
        k_blk = kv_ref[pl.ds(key_start, BLK), :HD]
        v_blk = kv_ref[pl.ds(key_start, BLK), HD:]
        mask = pair_mask(segk[pl.ds(key_start, BLK), :], segq, p, query)
        for h in range(HEADS):
            cols = slice(h * BLK, (h + 1) * BLK)
            s = dot(k_blk, qt[:, cols])
            w = jnp.where(mask, jnp.exp2(s * scale2 - lse_ref[0, :, cols]), 0.0)
            dp = dot(v_blk, dt[:, cols])
            dsv = w * (dp - delta[:, cols])
            pm[:, cols] = w.astype(jnp.bfloat16)
            sm[:, cols] = dsv.astype(jnp.bfloat16)
        dkv_ref[pl.ds(key_start, BLK), HD:] += dot(pm[...], ds_[...])
        dkv_ref[pl.ds(key_start, BLK), :HD] += dot(sm[...], qs[...])
        dqt[...] += dot(k_blk.T, sm[...])
        return carry

    lax.fori_loop(0, count, body, 0)
    if remote:
        dq_out[0] = dqt[...]
    else:
        def put(dst):
            for h in range(HEADS):
                cols = slice(h * BLK, (h + 1) * BLK)
                dst[:, h * HD:(h + 1) * HD] = (dqt[:, cols] * scale).T.astype(jnp.bfloat16)

        @pl.when(step < 4)
        def _():
            put(dq_own)

        @pl.when(step >= 4)
        def _():
            put(dq_oth)


def lanes(ref, first, count):
    return jnp.concatenate([ref[first + h] for h in range(count)], axis=1)


def project_kernel(ids_ref, a_ref, w_ref, out_ref, at_ref):
    step = pl.program_id(0)
    out_ref[...] = dot(a_ref[...], lanes(w_ref, 0, 2)).astype(jnp.bfloat16)
    cols = at_ref.shape[0]
    first = pl.multiple_of(step * cols, cols)
    for t in range(0, a_ref.shape[0], BLK):
        at_ref[:, t:t + BLK] = a_ref[t:t + BLK, pl.ds(first, cols)].T


def expand_kernel(ids_ref, a_ref, b_ref, wa_ref, wb_ref, out_ref):
    out_ref[...] = (dot_nt(a_ref[...], lanes(wa_ref, 0, HEADS))
                    + dot_nt(b_ref[...], lanes(wb_ref, 0, HEADS))).astype(jnp.bfloat16)


def expand_kv_kernel(ids_ref, a_ref, b_ref, wa_ref, wb_ref, c_ref, d_ref, wc_ref, wd_ref, out_ref):
    out_ref[...] = (dot_nt(a_ref[...], lanes(wa_ref, 0, HEADS))
                    + dot_nt(b_ref[...], lanes(wb_ref, 0, HEADS))
                    + dot_nt(c_ref[...], wc_ref[...]) + dot_nt(d_ref[...], wd_ref[...])).astype(jnp.bfloat16)


def wgrad_kernel(ids_ref, a_own, a_oth, b_own, b_oth, c_own, c_oth, out_ref):
    step = pl.program_id(0)
    half = pl.num_programs(0) // 2

    def put(own, oth):
        val = dot(a_own[...], own[...]) + dot(a_oth[...], oth[...])
        for h in range(out_ref.shape[0]):
            out_ref[h] = val[:, h * HD:(h + 1) * HD]

    @pl.when(step < half)
    def _():
        put(b_own, b_oth)

    @pl.when(step >= half)
    def _():
        put(c_own, c_oth)


def own_block(i, *_):
    return (jnp.minimum(i, 3), 0)


def oth_block(i, *_):
    return (jnp.maximum(i - 4, 0), 0)


def whole(i, *_):
    return (0, 0)


def whole3(i, *_):
    return (0, 0, 0)


def lead(i, *_):
    return (i, 0, 0)


def params():
    return pltpu.CompilerParams(dimension_semantics=('arbitrary',), vmem_limit_bytes=VMEM_LIMIT)


def attend(seg, ids, q_own, q_oth, kv_far, kv_near, rows):
    keys = 2 * kv_near.shape[0]
    tok = q_own.shape[0]
    grid = 2 * tok // BLK
    qspec = [pl.BlockSpec((BLK, HEADS * HD), own_block), pl.BlockSpec((BLK, HEADS * HD), oth_block)]
    stat = pltpu.VMEM((1, WIDE), jnp.float32)
    return pl.pallas_call(
        fwd_kernel,
        grid_spec=pltpu.PrefetchScalarGridSpec(
            num_scalar_prefetch=2, grid=(grid,),
            in_specs=qspec + [pl.BlockSpec((keys // 2, 2 * HD), whole)] * 2
            + [pl.BlockSpec((keys // BLK, 1, BLK), whole3)],
            out_specs=qspec + [pl.BlockSpec((1, 1, WIDE), lead)],
            scratch_shapes=[pltpu.VMEM((keys, 128), jnp.int32), pltpu.VMEM((keys, 2 * HD), jnp.bfloat16),
                            pltpu.VMEM((HD, WIDE), jnp.bfloat16), pltpu.VMEM((HD, WIDE), jnp.float32),
                            stat, stat, stat, pltpu.VMEM((BLK, WIDE), jnp.bfloat16)]),
        out_shape=[jax.ShapeDtypeStruct((tok, HEADS * HD), jnp.bfloat16)] * 2
        + [jax.ShapeDtypeStruct((grid, 1, WIDE), jnp.float32)],
        compiler_params=params(), name='attend',
        cost_estimate=pl.CostEstimate(flops=40 * 4 * WIDE * BLK * HD, bytes_accessed=12 << 20, transcendentals=0),
    )(seg, ids, q_own, q_oth, kv_far, kv_near, rows)


def attend_grad(remote, seg, ids, q, do, o, kv, rows, lse, dq_in=None):
    keys = kv.shape[0]
    tok = q[0].shape[0]
    grid = 2 * tok // BLK
    qspec = [pl.BlockSpec((BLK, HEADS * HD), own_block), pl.BlockSpec((BLK, HEADS * HD), oth_block)]
    in_specs = qspec * 3 + [pl.BlockSpec((keys, 2 * HD), whole), pl.BlockSpec(rows.shape, whole3),
                            pl.BlockSpec((1, 1, WIDE), lead)]
    args = [seg, ids, *q, *do, *o, kv, rows, lse]
    dqt_spec = pl.BlockSpec((1, HD, WIDE), lead)
    kv_grad = [jax.ShapeDtypeStruct((keys, 2 * HD), jnp.float32)]
    kv_spec = [pl.BlockSpec((keys, 2 * HD), whole)]
    if remote:
        out_shape = [jax.ShapeDtypeStruct((grid, HD, WIDE), jnp.float32)] + kv_grad
        out_specs = [dqt_spec] + kv_spec
    else:
        in_specs.append(dqt_spec)
        args.append(dq_in)
        out_shape = [jax.ShapeDtypeStruct((tok, HEADS * HD), jnp.bfloat16)] * 2 + kv_grad
        out_specs = qspec + kv_spec
    stack = pltpu.VMEM((WIDE, HD), jnp.bfloat16)
    flip = pltpu.VMEM((HD, WIDE), jnp.bfloat16)
    tile = pltpu.VMEM((BLK, WIDE), jnp.bfloat16)
    return pl.pallas_call(
        functools.partial(bwd_kernel, remote),
        grid_spec=pltpu.PrefetchScalarGridSpec(
            num_scalar_prefetch=2, grid=(grid,), in_specs=in_specs, out_specs=out_specs,
            scratch_shapes=[pltpu.VMEM((keys, 128), jnp.int32), stack, flip, stack, flip,
                            pltpu.VMEM((1, WIDE), jnp.float32),
                            tile, tile, pltpu.VMEM((HD, WIDE), jnp.float32)]),
        out_shape=out_shape, compiler_params=params(),
        name='attend_grad_remote' if remote else 'attend_grad_local',
        cost_estimate=pl.CostEstimate(flops=20 * 10 * WIDE * BLK * HD, bytes_accessed=20 << 20, transcendentals=0),
    )(*args)


def project(ids, a, w):
    tok, dim = a.shape
    steps = HEADS // 2
    return pl.pallas_call(
        project_kernel,
        grid_spec=pltpu.PrefetchScalarGridSpec(
            num_scalar_prefetch=1, grid=(steps,),
            in_specs=[pl.BlockSpec((tok, dim), whole),
                      pl.BlockSpec((2, dim, HD), lambda i, ids: (steps * ids[0] + i, 0, 0))],
            out_specs=[pl.BlockSpec((tok, 2 * HD), lambda i, ids: (0, i)),
                       pl.BlockSpec((dim // steps, tok), lambda i, ids: (i, 0))]),
        out_shape=[jax.ShapeDtypeStruct((tok, HEADS * HD), jnp.bfloat16),
                   jax.ShapeDtypeStruct((dim, tok), jnp.bfloat16)],
        compiler_params=params(),
        cost_estimate=pl.CostEstimate(flops=2 * tok * dim * HEADS * HD, bytes_accessed=10 << 20, transcendentals=0),
    )(ids, a, w)


def expand(ids, a, b, w, extra=()):
    tok, width = a.shape
    dim = w.shape[1]
    cols = 512
    act = pl.BlockSpec((tok, width), whole)
    specs = [act, act, pl.BlockSpec((HEADS, cols, HD), lambda i, ids: (ids[0], i, 0)),
             pl.BlockSpec((HEADS, cols, HD), lambda i, ids: (1 - ids[0], i, 0))]
    args = [a, b, w, w]
    if extra:
        c, d, w_kv = extra
        act = pl.BlockSpec((tok, 2 * HD), whole)
        specs += [act, act, pl.BlockSpec((cols, 2 * HD), lambda i, ids: (i, ids[0])),
                  pl.BlockSpec((cols, 2 * HD), lambda i, ids: (i, 1 - ids[0]))]
        args += [c, d, w_kv, w_kv]
    return pl.pallas_call(
        expand_kv_kernel if extra else expand_kernel,
        grid_spec=pltpu.PrefetchScalarGridSpec(
            num_scalar_prefetch=1, grid=(dim // cols,), in_specs=specs,
            out_specs=pl.BlockSpec((tok, cols), lambda i, ids: (0, i))),
        out_shape=jax.ShapeDtypeStruct((tok, dim), jnp.bfloat16),
        compiler_params=params(), name='grad_x' if extra else 'out_y',
        cost_estimate=pl.CostEstimate(flops=4 * tok * dim * width, bytes_accessed=14 << 20, transcendentals=0),
    )(ids, *args)


def wgrad(where, core, a, b, c):
    dim, tok = a[0].shape
    width = b[0].shape[1]
    rows = dim // 4
    step = 256
    half = width // step
    heads = step // HD
    a_spec = pl.BlockSpec((rows, tok), lambda i, ids: (ids[0], 0))
    b_spec = pl.BlockSpec((tok, step), lambda i, ids: (0, jnp.minimum(i, half - 1)))
    c_spec = pl.BlockSpec((tok, step), lambda i, ids: (0, jnp.maximum(i - half, 0)))
    return pl.pallas_call(
        wgrad_kernel,
        grid_spec=pltpu.PrefetchScalarGridSpec(
            num_scalar_prefetch=1, grid=(2 * half,),
            in_specs=[a_spec] * 2 + [b_spec] * 2 + [c_spec] * 2,
            out_specs=pl.BlockSpec((heads, rows, HD), lambda i, ids: (lax.rem(i + half * ids[1], 2 * half), 0, 0))),
        out_shape=jax.ShapeDtypeStruct((2 * width // HD, rows, HD), jnp.float32),
        compiler_params=params(),
        cost_estimate=pl.CostEstimate(flops=8 * tok * rows * width, bytes_accessed=10 << 20, transcendentals=0),
    )(jnp.stack([where, core]).astype(jnp.int32), *a, *b, *c)


def after(value, *others):
    return lax.optimization_barrier((value, *others))[0]


def solution(mesh):
    row_spec = P(('dp', 'cp'), None)
    tok_spec = P(('dp', 'cp'))
    weight_spec = P(None, None, None)
    grad_spec = P(('dp', 'cp'), None, None)
    core_pairs = [(0, 1), (1, 0), (2, 3), (3, 2)]
    chip_pairs = [(0, 2), (2, 0), (1, 3), (3, 1)]
    up_pairs = [(0, 2), (1, 3)]
    down_pairs = [(2, 0), (3, 1)]

    def send(a, pairs):
        return lax.ppermute(a, 'cp', pairs)

    def layer(x, seg, w_q, w_k, w_v, w_o, dy):
        tok, dim = x.shape
        rows = dim // 4
        index = lax.axis_index('cp')
        core = index % 2
        chip = index // 2
        near_rows = index
        far_rows = 2 * (1 - chip) + core
        ids = jnp.stack([core, chip]).astype(jnp.int32)
        w_q = jnp.transpose(w_q, (1, 0, 2))
        w_o = jnp.transpose(w_o, (1, 0, 2))

        def swap(pair):
            return tuple(send(a, core_pairs) for a in pair)[::-1]

        x_o = send(x, core_pairs)
        seg_o = send(seg, core_pairs)
        dy_o = send(dy, core_pairs)
        seg_near = jnp.concatenate([seg, seg_o])
        seg_far = send(seg_near, up_pairs)
        seg_all = jnp.concatenate([seg_far, seg_near])
        seg_rows = seg_all.reshape(-1, 1, BLK)

        w_kv = jnp.stack([w_k, w_v], axis=2).reshape(dim, 4 * HD)
        w_kv = lax.optimization_barrier(w_kv)
        wkv_c = lax.dynamic_slice_in_dim(w_kv, core * 2 * HD, 2 * HD, 1)
        kv_own = dot(x, wkv_c).astype(jnp.bfloat16)
        kv_oth = dot(x_o, wkv_c).astype(jnp.bfloat16)
        kv_near = jnp.concatenate([kv_own, kv_oth], axis=0)
        kv_far = send(kv_near, up_pairs)
        q_own, xt = project(ids, after(x, kv_near), w_q)
        q_oth, xt_o = project(ids, x_o, w_q)
        do_own, dyt = project(ids, dy, w_o)
        do_oth, dyt_o = project(ids, dy_o, w_o)
        q, do, xt, dyt = (q_own, q_oth), (do_own, do_oth), (xt, xt_o), (dyt, dyt_o)

        *o, lse = attend(seg_all, ids, q[0], q[1], kv_far, kv_near, seg_rows)
        o_p = swap(o)
        dwo_far = wgrad(far_rows, core, dyt, o, o_p)
        dwo_in = send(dwo_far, chip_pairs)

        lse = after(lse, dwo_far)
        dq_part, dkv_far = attend_grad(True, seg_all, ids, q, do, o, kv_far, seg_rows, lse)
        dkv_in = send(dkv_far, down_pairs)
        dq_own, dq_oth, dkv_near = attend_grad(False, seg_all, ids, q, do, o, kv_near, seg_rows, lse, dq_part)
        dq = (dq_own, dq_oth)
        dq_p = swap(dq)
        dwq_far = wgrad(far_rows, core, xt, dq, dq_p)
        dwq_in = send(dwq_far, chip_pairs)

        y = expand(ids, after(o[0], dwq_far), o_p[0], w_o)
        dwo_near = wgrad(near_rows, core, (dyt[0], after(dyt[1], dwq_far)), o, o_p)
        dwq_near = wgrad(near_rows, core, (xt[0], after(xt[1], dwq_far)), dq, dq_p)

        dkv = dkv_near + dkv_in
        dkv = jnp.concatenate([dkv[:, :HD] * HD ** -0.5, dkv[:, HD:]], axis=1).astype(jnp.bfloat16)
        dkv = (dkv[:tok], dkv[tok:])
        dkv_p = swap(dkv)
        dwkv_far = wgrad(far_rows, core, xt, dkv, dkv_p)
        dwkv_in = send(dwkv_far, chip_pairs)
        dwkv_near = wgrad(near_rows, core, (xt[0], after(xt[1], dwkv_far)), dkv, dkv_p)
        dx = expand(ids, after(dq[0], dwkv_far), dq_p[0], w_q, (dkv[0], dkv_p[0], w_kv))

        dw_q = jnp.transpose(dwq_near + dwq_in, (1, 0, 2))
        dw_o = jnp.transpose(dwo_near + dwo_in, (1, 0, 2))
        dw_kv = jnp.transpose(dwkv_near + dwkv_in, (1, 0, 2)).reshape(rows, 2, 2, HD)
        return y, dx, dw_q, dw_kv[:, :, 0], dw_kv[:, :, 1], dw_o

    return jax.shard_map(layer, mesh=mesh,
                         in_specs=(row_spec, tok_spec, weight_spec, weight_spec, weight_spec, weight_spec, row_spec),
                         out_specs=(row_spec, row_spec, grad_spec, grad_spec, grad_spec, grad_spec),
                         check_vma=False)
```

profile of v0, /device:TPU:0, one launch (start us, length us, event | category | flops | bytes accessed | tf_op | source)
XLA Modules:
  0.0 325.3 jit_solution(14087471620238618794)
XLA Ops:
  1.5 3.6 %pad_maximum_fusion = bf16[1536,2,2,128]{3,1,0,2:T(2,128)(2,1)S(1)} fusion(bf16[1536,2,1,128]{3,1,0,2:T(2,128)(2,1)} %bitcast.31, bf16[1536,2,1,128]{3,1,0,2:T(2,128)(2,1)} %bitcast.32), kind=kLoop, calls=%fused_computation.2 | loop fusion | flops 786432 | bytes 3145728 | tf_op jit(solution)/shard_map/stack | solution.py:450
  5.1 5.0 %copy.13 = bf16[1536,2,2,128]{3,2,1,0:T(2,128)(2,1)S(1)} copy(bf16[1536,2,2,128]{3,1,0,2:T(2,128)(2,1)S(1)} %pad_maximum_fusion) | data formatting | bytes 3145728 | tf_op jit(solution)/shard_map/stack | solution.py:450
  10.8 3.4 %fusion = bf16[1024,256]{1,0:T(8,128)(2,1)S(1)} fusion(bf16[1024,1536]{1,0:T(8,128)(2,1)} %a_ref.1, bf16[1536,512]{1,0:T(8,128)(2,1)S(1)} %reshape.21.wc_ref.wd_ref, s32[]{:T(128)S(6)} %select_n.16), kind=kOutput, calls=%fused_computation.5 | convolution fusion | flops 805568512 | bytes 4456452 | tf_op jit(solution)/shard_map/dot_general | solution.py:20
  17.2 4.5 %collective-permute-start.3 = (bf16[2048,256]{1,0:T(8,128)(2,1)S(1)}, bf16[2048,256]{1,0:T(8,128)(2,1)S(1)}, u32[]{:S(2)}, u32[]{:S(2)}) collective-permute-start(bf16[2048,256]{1,0:T(8,128)(2,1)S(1)} %pad_maximum_fusion.1.kv_near.refs_8_), channel_id=1, source_target_pairs={{0,2},{1,3},{4,6},{5,7}} | collective-permute-start | bytes 3145736 | tf_op jit(solution)/shard_map/ppermute | solution.py:425
  22.3 5.5 %collective-permute-done = s32[1024]{0:T(1024)S(1)} collective-permute-done((s32[1024]{0:T(1024)S(1)}, s32[1024]{0:T(1024)S(1)}, u32[]{:S(2)}, u32[]{:S(2)}) %collective-permute-start) | collective-permute-done | bytes 4128 | tf_op jit(solution)/shard_map/ppermute | solution.py:425
  29.7 15.1 %collective-permute-done.1 = s32[2048]{0:T(1024)S(1)} collective-permute-done((s32[2048]{0:T(1024)S(1)}, s32[2048]{0:T(1024)S(1)}, u32[]{:S(2)}, u32[]{:S(2)}) %collective-permute-start.1) | collective-permute-done | bytes 8224 | tf_op jit(solution)/shard_map/ppermute | solution.py:425
  44.9 7.6 %shard_map.118 = (bf16[1024,768]{1,0:T(8,128)(2,1)}, bf16[1536,1024]{1,0:T(8,128)(2,1)}) custom-call(s32[2]{0:T(128)} %pad_add_fusion.1.ids_ref.refs_1_, bf16[1024,1536]{1,0:T(8,128)(2,1)} %a_ref.1, bf16[12,1536,128]{2,1,0:T(8,128)(2,1)} %bitcast.26), custom_call_target="tpu_custom_call" | custom-call | flops 2415919104 | bytes 10485760 | tf_op jit(solution)/shard_map/pallas_call | solution.py:348
  52.5 7.6 %shard_map.119 = (bf16[1024,768]{1,0:T(8,128)(2,1)}, bf16[1536,1024]{1,0:T(8,128)(2,1)}) custom-call(s32[2]{0:T(128)} %pad_add_fusion.1.ids_ref.refs_1_, bf16[1024,1536]{1,0:T(8,128)(2,1)} %collective-permute-done.2.a_ref, bf16[12,1536,128]{2,1,0:T(8,128)(2,1)} %bitcast.27), custom_call_target="tpu_custom_call" | custom-call | flops 2415919104 | bytes 10485760 | tf_op jit(solution)/shard_map/pallas_call | solution.py:348
  61.2 38.8 %attend.1 = (bf16[1024,768]{1,0:T(8,128)(2,1)}, bf16[1024,768]{1,0:T(8,128)(2,1)}, f32[8,1,1536]{2,1,0:T(1,128)}) custom-call(s32[4096]{0:T(1024)} %copy-done.13, s32[2]{0:T(128)} %pad_add_fusion.1.ids_ref.refs_1_, bf16[1024,768]{1,0:T(8,128)(2,1)} %get-tuple-element.30.q_own.refs_2_, bf16[1024,768]{1,0:T(8,128)(2,1)} %get-tuple-element.31.q_oth.refs_3_, ...), custom_call_target="tpu_custom_call" | custom-call | flops 8053063680 | bytes 12582912 | tf_op jit(solution)/shard_map/attend/pallas_call | solution.py:293
  101.2 7.7 %shard_map.120 = (bf16[1024,768]{1,0:T(8,128)(2,1)}, bf16[1536,1024]{1,0:T(8,128)(2,1)}) custom-call(s32[2]{0:T(128)} %pad_add_fusion.1.ids_ref.refs_1_, bf16[1024,1536]{1,0:T(8,128)(2,1)} %a_ref.2, bf16[12,1536,128]{2,1,0:T(8,128)(2,1)} %bitcast.36), custom_call_target="tpu_custom_call" | custom-call | flops 2415919104 | bytes 10485760 | tf_op jit(solution)/shard_map/pallas_call | solution.py:348
  108.8 7.7 %shard_map.121 = (bf16[1024,768]{1,0:T(8,128)(2,1)}, bf16[1536,1024]{1,0:T(8,128)(2,1)}) custom-call(s32[2]{0:T(128)} %pad_add_fusion.1.ids_ref.refs_1_, bf16[1024,1536]{1,0:T(8,128)(2,1)} %collective-permute-done.4.a_ref, bf16[12,1536,128]{2,1,0:T(8,128)(2,1)} %bitcast.37), custom_call_target="tpu_custom_call" | custom-call | flops 2415919104 | bytes 10485760 | tf_op jit(solution)/shard_map/pallas_call | solution.py:348
  117.7 8.9 %shard_map.122 = f32[12,384,128]{2,1,0:T(8,128)} custom-call(s32[2]{0:T(128)} %pad_add_fusion.2.ids_ref, bf16[1536,1024]{1,0:T(8,128)(2,1)} %get-tuple-element.39.a_own, bf16[1536,1024]{1,0:T(8,128)(2,1)} %get-tuple-element.51.a_oth, bf16[1024,768]{1,0:T(8,128)(2,1)} %get-tuple-element.45.b_own.refs_6_.a_ref, ...), custom_call_target="tpu_custom_call" | custom-call | flops 2415919104 | bytes 10485760 | tf_op jit(solution)/shard_map/pallas_call | solution.py:398
  126.6 11.4 %attend_grad_remote.1 = (f32[8,128,1536]{2,1,0:T(8,128)}, f32[2048,256]{1,0:T(8,128)}) custom-call(s32[4096]{0:T(1024)} %copy-done.13, s32[2]{0:T(128)} %pad_add_fusion.1.ids_ref.refs_1_, bf16[1024,768]{1,0:T(8,128)(2,1)} %get-tuple-element.30.q_own.refs_2_, bf16[1024,768]{1,0:T(8,128)(2,1)} %get-tuple-element.31.q_oth.refs_3_, ...), custom_call_target="tpu_custom_call" | custom-call | flops 10066329600 | bytes 20971520 | tf_op jit(solution)/shard_map/attend_grad_remote/pallas_call | solution.py:332
  139.4 53.2 %attend_grad_local.1 = (bf16[1024,768]{1,0:T(8,128)(2,1)}, bf16[1024,768]{1,0:T(8,128)(2,1)}, f32[2048,256]{1,0:T(8,128)}) custom-call(s32[4096]{0:T(1024)} %copy-done.13, s32[2]{0:T(128)} %pad_add_fusion.1.ids_ref.refs_1_, bf16[1024,768]{1,0:T(8,128)(2,1)} %get-tuple-element.30.q_own.refs_2_, bf16[1024,768]{1,0:T(8,128)(2,1)} %get-tuple-element.31.q_oth.refs_3_, ...), custom_call_target="tpu_custom_call" | custom-call | flops 10066329600 | bytes 20971520 | tf_op jit(solution)/shard_map/attend_grad_local/pallas_call | solution.py:332
  199.7 8.9 %shard_map.123 = f32[12,384,128]{2,1,0:T(8,128)} custom-call(s32[2]{0:T(128)} %pad_add_fusion.2.ids_ref, bf16[1536,1024]{1,0:T(8,128)(2,1)} %get-tuple-element.33.a_own, bf16[1536,1024]{1,0:T(8,128)(2,1)} %get-tuple-element.50.a_oth, bf16[1024,768]{1,0:T(8,128)(2,1)} %get-tuple-element.48.b_own.a_ref, bf16[1024,768]{1,0:T(8,128)(2,1)} %get-tuple-element.44.b_oth, ...), custom_call_target="tpu_custom_call" | custom-call | flops 2415919104 | bytes 10485760 | tf_op jit(solution)/shard_map/pallas_call | solution.py:398
  208.6 9.0 %shard_map.127 = f32[12,384,128]{2,1,0:T(8,128)} custom-call(s32[2]{0:T(128)} %pad_add_fusion.3.ids_ref, bf16[1536,1024]{1,0:T(8,128)(2,1)} %get-tuple-element.39.a_own, bf16[1536,1024]{1,0:T(8,128)(2,1)} %get-tuple-element.51.a_oth, bf16[1024,768]{1,0:T(8,128)(2,1)} %get-tuple-element.45.b_own.refs_6_.a_ref, ...), custom_call_target="tpu_custom_call" | custom-call | flops 2415919104 | bytes 10485760 | tf_op jit(solution)/shard_map/pallas_call | solution.py:398
  220.3 8.9 %shard_map.125 = f32[12,384,128]{2,1,0:T(8,128)} custom-call(s32[2]{0:T(128)} %pad_add_fusion.3.ids_ref, bf16[1536,1024]{1,0:T(8,128)(2,1)} %get-tuple-element.33.a_own, bf16[1536,1024]{1,0:T(8,128)(2,1)} %get-tuple-element.50.a_oth, bf16[1024,768]{1,0:T(8,128)(2,1)} %get-tuple-element.48.b_own.a_ref, bf16[1024,768]{1,0:T(8,128)(2,1)} %get-tuple-element.44.b_oth, ...), custom_call_target="tpu_custom_call" | custom-call | flops 2415919104 | bytes 10485760 | tf_op jit(solution)/shard_map/pallas_call | solution.py:398
  229.2 9.6 %out_y.1 = bf16[1024,1536]{1,0:T(8,128)(2,1)} custom-call(s32[2]{0:T(128)} %pad_add_fusion.1.ids_ref.refs_1_, bf16[1024,768]{1,0:T(8,128)(2,1)} %get-tuple-element.45.b_own.refs_6_.a_ref, bf16[1024,768]{1,0:T(8,128)(2,1)} %copy-done.5, bf16[12,1536,128]{2,1,0:T(8,128)(2,1)} %bitcast.38, bf16[12,1536,128]{2,1,0:T(8,128)(2,1)} %bitcast.39), custom_call_target="tpu_custom_call" | custom-call | flops 4831838208 | bytes 14680064 | tf_op jit(solution)/shard_map/out_y/pallas_call | solution.py:377
  239.6 4.8 %shard_map.124 = f32[4,384,128]{2,1,0:T(8,128)} custom-call(s32[2]{0:T(128)} %pad_add_fusion.2.ids_ref, bf16[1536,1024]{1,0:T(8,128)(2,1)} %get-tuple-element.33.a_own, bf16[1536,1024]{1,0:T(8,128)(2,1)} %get-tuple-element.50.a_oth, bf16[1024,256]{1,0:T(8,128)(2,1)} %copy-done.4, bf16[1024,256]{1,0:T(8,128)(2,1)} %copy-done.8, bf16[1024,256]{1,0:T(8,128)(2,1)} %copy-done.7, ...), custom_call_target="tpu_custom_call" | custom-call | flops 805306368 | bytes 10485760 | tf_op jit(solution)/shard_map/pallas_call | solution.py:398
  246.3 8.3 %collective-permute-done.14 = f32[12,384,128]{2,1,0:T(8,128)} collective-permute-done((f32[12,384,128]{2,1,0:T(8,128)}, f32[12,384,128]{2,1,0:T(8,128)}, u32[]{:S(2)}, u32[]{:S(2)}) %collective-permute-start.14) | collective-permute-done | bytes 2359328 | tf_op jit(solution)/shard_map/ppermute | solution.py:425
  257.9 4.7 %shard_map.126 = f32[4,384,128]{2,1,0:T(8,128)} custom-call(s32[2]{0:T(128)} %pad_add_fusion.3.ids_ref, bf16[1536,1024]{1,0:T(8,128)(2,1)} %get-tuple-element.33.a_own, bf16[1536,1024]{1,0:T(8,128)(2,1)} %get-tuple-element.50.a_oth, bf16[1024,256]{1,0:T(8,128)(2,1)} %copy-done.4, bf16[1024,256]{1,0:T(8,128)(2,1)} %copy-done.8, bf16[1024,256]{1,0:T(8,128)(2,1)} %copy-done.7, ...), custom_call_target="tpu_custom_call" | custom-call | flops 805306368 | bytes 10485760 | tf_op jit(solution)/shard_map/pallas_call | solution.py:398
  262.6 11.8 %grad_x.1 = bf16[1024,1536]{1,0:T(8,128)(2,1)} custom-call(s32[2]{0:T(128)} %pad_add_fusion.1.ids_ref.refs_1_, bf16[1024,768]{1,0:T(8,128)(2,1)} %get-tuple-element.48.b_own.a_ref, bf16[1024,768]{1,0:T(8,128)(2,1)} %copy-done, bf16[12,1536,128]{2,1,0:T(8,128)(2,1)} %bitcast.28, bf16[12,1536,128]{2,1,0:T(8,128)(2,1)} %bitcast.29, ...), custom_call_target="tpu_custom_call" | custom-call | flops 4831838208 | bytes 14680064 | tf_op jit(solution)/shard_map/grad_x/pallas_call | solution.py:377
  274.5 45.8 %collective-permute-done.13 = f32[4,384,128]{2,1,0:T(8,128)S(1)} collective-permute-done((f32[4,384,128]{2,1,0:T(8,128)}, f32[4,384,128]{2,1,0:T(8,128)S(1)}, u32[]{:S(2)}, u32[]{:S(2)}) %collective-permute-start.13) | collective-permute-done | bytes 786464 | tf_op jit(solution)/shard_map/ppermute | solution.py:425
  321.9 3.4 %add_bitcast_fusion.1 = f32[384,12,128]{2,0,1:T(8,128)} fusion(f32[12,384,128]{2,1,0:T(8,128)S(1)} %copy-done.2, f32[12,384,128]{2,1,0:T(8,128)} %collective-permute-done.12), kind=kLoop, calls=%fused_computation.1 | loop fusion | flops 589824 | bytes 7077888 | tf_op jit(solution)/shard_map/transpose | solution.py:490
  (73 shorter events, 29.1 us)
Async XLA Ops:
  0.6 13.6 %collective-permute-start.2 = (bf16[1024,1536]{1,0:T(8,128)(2,1)}, bf16[1024,1536]{1,0:T(8,128)(2,1)}, u32[]{:S(2)}, u32[]{:S(2)}) collective-permute-start(bf16[1024,1536]{1,0:T(8,128)(2,1)} %a_ref.1), channel_id=1, source_target_pairs={{0,1},{1,0},{2,3},{3,2},{4,5},{5,4},{6,7},{7,6}} | collective-permute-start | bytes 9437192 | tf_op jit(solution)/shard_map/ppermute | solution.py:425
  14.2 7.7 %copy-start.12 = (s32[1024]{0:T(1024)S(1)}, s32[1024]{0:T(1024)}, u32[]{:S(2)}) copy-start(s32[1024]{0:T(1024)} %param.8) | copy-start | bytes 12292
  17.2 35.2 %copy-start.11 = (bf16[2048,256]{1,0:T(8,128)(2,1)}, bf16[2048,256]{1,0:T(8,128)(2,1)S(1)}, u32[]{:S(2)}) copy-start(bf16[2048,256]{1,0:T(8,128)(2,1)S(1)} %pad_maximum_fusion.1.kv_near.refs_8_) | copy-start | bytes 3145732
  17.2 42.9 %collective-permute-start.3 = (bf16[2048,256]{1,0:T(8,128)(2,1)S(1)}, bf16[2048,256]{1,0:T(8,128)(2,1)S(1)}, u32[]{:S(2)}, u32[]{:S(2)}) collective-permute-start(bf16[2048,256]{1,0:T(8,128)(2,1)S(1)} %pad_maximum_fusion.1.kv_near.refs_8_), channel_id=1, source_target_pairs={{0,2},{1,3},{4,6},{5,7}} | collective-permute-start | bytes 3145736 | tf_op jit(solution)/shard_map/ppermute | solution.py:425
  21.7 87.1 %collective-permute-start.4 = (bf16[1024,1536]{1,0:T(8,128)(2,1)}, bf16[1024,1536]{1,0:T(8,128)(2,1)}, u32[]{:S(2)}, u32[]{:S(2)}) collective-permute-start(bf16[1024,1536]{1,0:T(8,128)(2,1)} %a_ref.2), channel_id=1, source_target_pairs={{0,1},{1,0},{2,3},{3,2},{4,5},{5,4},{6,7},{7,6}} | collective-permute-start | bytes 9437192 | tf_op jit(solution)/shard_map/ppermute | solution.py:425
  22.0 5.8 %collective-permute-start = (s32[1024]{0:T(1024)S(1)}, s32[1024]{0:T(1024)S(1)}, u32[]{:S(2)}, u32[]{:S(2)}) collective-permute-start(s32[1024]{0:T(1024)S(1)} %copy-done.12), channel_id=1, source_target_pairs={{0,1},{1,0},{2,3},{3,2},{4,5},{5,4},{6,7},{7,6}} | collective-permute-start | bytes 12296 | tf_op jit(solution)/shard_map/ppermute | solution.py:425
  27.7 17.1 %collective-permute-start.1 = (s32[2048]{0:T(1024)S(1)}, s32[2048]{0:T(1024)S(1)}, u32[]{:S(2)}, u32[]{:S(2)}) collective-permute-start(s32[2048]{0:T(1024)S(1)} %pad_add_fusion), channel_id=1, source_target_pairs={{0,2},{1,3},{4,6},{5,7}} | collective-permute-start | bytes 24584 | tf_op jit(solution)/shard_map/ppermute | solution.py:425
  44.9 7.6 %copy-start.13 = (s32[4096]{0:T(1024)}, s32[4096]{0:T(1024)S(1)}, u32[]{:S(2)}) copy-start(s32[4096]{0:T(1024)S(1)} %constant_dynamic-update-slice_fusion.seg_ref.refs_0_) | copy-start | bytes 49156
  100.0 16.5 %collective-permute-start.5 = (bf16[1024,768]{1,0:T(8,128)(2,1)}, bf16[1024,768]{1,0:T(8,128)(2,1)S(1)}, u32[]{:S(2)}, u32[]{:S(2)}) collective-permute-start(bf16[1024,768]{1,0:T(8,128)(2,1)} %get-tuple-element.37.b_oth.refs_7_), channel_id=1, source_target_pairs={{0,1},{1,0},{2,3},{3,2},{4,5},{5,4},{6,7},{7,6}} | collective-permute-start | bytes 4718600 | tf_op jit(solution)/shard_map/ppermute | solution.py:425
  100.0 16.5 %collective-permute-start.6 = (bf16[1024,768]{1,0:T(8,128)(2,1)}, bf16[1024,768]{1,0:T(8,128)(2,1)}, u32[]{:S(2)}, u32[]{:S(2)}) collective-permute-start(bf16[1024,768]{1,0:T(8,128)(2,1)} %get-tuple-element.45.b_own.refs_6_.a_ref), channel_id=1, source_target_pairs={{0,1},{1,0},{2,3},{3,2},{4,5},{5,4},{6,7},{7,6}} | collective-permute-start | bytes 4718600 | tf_op jit(solution)/shard_map/ppermute | solution.py:425
  138.0 79.7 %collective-permute-start.9 = (f32[2048,256]{1,0:T(8,128)}, f32[2048,256]{1,0:T(8,128)}, u32[]{:S(2)}, u32[]{:S(2)}) collective-permute-start(f32[2048,256]{1,0:T(8,128)} %get-tuple-element.47), channel_id=1, source_target_pairs={{2,0},{3,1},{6,4},{7,5}} | collective-permute-start | bytes 6291464 | tf_op jit(solution)/shard_map/ppermute | solution.py:425
  192.7 3.6 %collective-permute-start.7 = (bf16[1024,768]{1,0:T(8,128)(2,1)}, bf16[1024,768]{1,0:T(8,128)(2,1)S(1)}, u32[]{:S(2)}, u32[]{:S(2)}) collective-permute-start(bf16[1024,768]{1,0:T(8,128)(2,1)} %get-tuple-element.44.b_oth), channel_id=1, source_target_pairs={{0,1},{1,0},{2,3},{3,2},{4,5},{5,4},{6,7},{7,6}} | collective-permute-start | bytes 4718600 | tf_op jit(solution)/shard_map/ppermute | solution.py:425
  192.7 5.8 %collective-permute-start.8 = (bf16[1024,768]{1,0:T(8,128)(2,1)}, bf16[1024,768]{1,0:T(8,128)(2,1)S(1)}, u32[]{:S(2)}, u32[]{:S(2)}) collective-permute-start(bf16[1024,768]{1,0:T(8,128)(2,1)} %get-tuple-element.48.b_own.a_ref), channel_id=1, source_target_pairs={{0,1},{1,0},{2,3},{3,2},{4,5},{5,4},{6,7},{7,6}} | collective-permute-start | bytes 4718600 | tf_op jit(solution)/shard_map/ppermute | solution.py:425
  193.2 61.4 %collective-permute-start.14 = (f32[12,384,128]{2,1,0:T(8,128)}, f32[12,384,128]{2,1,0:T(8,128)}, u32[]{:S(2)}, u32[]{:S(2)}) collective-permute-start(f32[12,384,128]{2,1,0:T(8,128)} %shard_map.122), channel_id=1, source_target_pairs={{0,2},{2,0},{1,3},{3,1},{4,6},{6,4},{5,7},{7,5}} | collective-permute-start | bytes 7077896 | tf_op jit(solution)/shard_map/ppermute | solution.py:425
  208.6 9.0 %copy-start.10 = (f32[2048,256]{1,0:T(8,128)S(1)}, f32[2048,256]{1,0:T(8,128)}, u32[]{:S(2)}) copy-start(f32[2048,256]{1,0:T(8,128)} %get-tuple-element.46) | copy-start | bytes 6291460
  208.6 113.3 %collective-permute-start.12 = (f32[12,384,128]{2,1,0:T(8,128)}, f32[12,384,128]{2,1,0:T(8,128)}, u32[]{:S(2)}, u32[]{:S(2)}) collective-permute-start(f32[12,384,128]{2,1,0:T(8,128)} %shard_map.123), channel_id=1, source_target_pairs={{0,2},{2,0},{1,3},{3,1},{4,6},{6,4},{5,7},{7,5}} | collective-permute-start | bytes 7077896 | tf_op jit(solution)/shard_map/ppermute | solution.py:425
  219.8 9.4 %copy-start.4 = (bf16[1024,256]{1,0:T(8,128)(2,1)}, bf16[1024,256]{1,0:T(8,128)(2,1)S(1)}, u32[]{:S(2)}) copy-start(bf16[1024,256]{1,0:T(8,128)(2,1)S(1)} %get-tuple-element.53.b_own.c_ref) | copy-start | bytes 1572868
  219.8 9.4 %copy-start.8 = (bf16[1024,256]{1,0:T(8,128)(2,1)}, bf16[1024,256]{1,0:T(8,128)(2,1)S(1)}, u32[]{:S(2)}) copy-start(bf16[1024,256]{1,0:T(8,128)(2,1)S(1)} %get-tuple-element.52.b_oth) | copy-start | bytes 1572868
  219.8 19.0 %collective-permute-start.10 = (bf16[1024,256]{1,0:T(8,128)(2,1)S(1)}, bf16[1024,256]{1,0:T(8,128)(2,1)S(1)}, u32[]{:S(2)}, u32[]{:S(2)}) collective-permute-start(bf16[1024,256]{1,0:T(8,128)(2,1)S(1)} %get-tuple-element.52.b_oth), channel_id=1, source_target_pairs={{0,1},{1,0},{2,3},{3,2},{4,5},{5,4},{6,7},{7,6}} | collective-permute-start | bytes 1572872 | tf_op jit(solution)/shard_map/ppermute | solution.py:425
  220.0 18.8 %collective-permute-start.11 = (bf16[1024,256]{1,0:T(8,128)(2,1)S(1)}, bf16[1024,256]{1,0:T(8,128)(2,1)}, u32[]{:S(2)}, u32[]{:S(2)}) collective-permute-start(bf16[1024,256]{1,0:T(8,128)(2,1)S(1)} %get-tuple-element.53.b_own.c_ref), channel_id=1, source_target_pairs={{0,1},{1,0},{2,3},{3,2},{4,5},{5,4},{6,7},{7,6}} | collective-permute-start | bytes 1572872 | tf_op jit(solution)/shard_map/ppermute | solution.py:425
  238.8 15.8 %copy-start.3 = (f32[12,384,128]{2,1,0:T(8,128)S(1)}, f32[12,384,128]{2,1,0:T(8,128)}, u32[]{:S(2)}) copy-start(f32[12,384,128]{2,1,0:T(8,128)} %shard_map.127) | copy-start | bytes 7077892
  244.5 75.8 %collective-permute-start.13 = (f32[4,384,128]{2,1,0:T(8,128)}, f32[4,384,128]{2,1,0:T(8,128)S(1)}, u32[]{:S(2)}, u32[]{:S(2)}) collective-permute-start(f32[4,384,128]{2,1,0:T(8,128)} %shard_map.124), channel_id=1, source_target_pairs={{0,2},{2,0},{1,3},{3,1},{4,6},{6,4},{5,7},{7,5}} | collective-permute-start | bytes 2359304 | tf_op jit(solution)/shard_map/ppermute | solution.py:425
  262.6 57.6 %copy-start.9 = (f32[4,384,128]{2,1,0:T(8,128)S(1)}, f32[4,384,128]{2,1,0:T(8,128)}, u32[]{:S(2)}) copy-start(f32[4,384,128]{2,1,0:T(8,128)} %shard_map.126) | copy-start | bytes 2359300
  274.5 47.4 %copy-start.2 = (f32[12,384,128]{2,1,0:T(8,128)S(1)}, f32[12,384,128]{2,1,0:T(8,128)}, u32[]{:S(2)}) copy-start(f32[12,384,128]{2,1,0:T(8,128)} %shard_map.125) | copy-start | bytes 7077892
  (6 other events, 9.9 us)
where the time goes:
time: 327 us; the launch traced here: 325 us
  Pallas kernels  201 us (61%)
  waiting for transfers between devices  79.5 us (24%)
  other arithmetic  14.4 us (4%)
  starting transfers between devices  12.1 us (4%)
  local copies, waits for them, and re-layouts  11.4 us (3%)
  matrix products  6.31 us (2%)
    ppermute x15, waiting for transfers between devices, send(): return lax.ppermute(a, 'cp', pairs)  79.5 us
    pallas_call x2, Pallas kernels, attend_grad(): pl.pallas_call(functools.partial(bwd_kernel, remote), grid_spec=pltpu.Pre...  64.6 us
    pallas_call x6, Pallas kernels, wgrad(): pl.pallas_call(wgrad_kernel, grid_spec=pltpu.PrefetchScalarGridSpec(num_s...  45.2 us
    pallas_call x1, Pallas kernels, attend(): pl.pallas_call(fwd_kernel, grid_spec=pltpu.PrefetchScalarGridSpec(num_sca...  38.8 us
    pallas_call x4, Pallas kernels, project(): pl.pallas_call(project_kernel, grid_spec=pltpu.PrefetchScalarGridSpec(num...  30.6 us
    pallas_call x2, Pallas kernels, expand(): pl.pallas_call(expand_kv_kernel if extra else expand_kernel, grid_spec=pl...  21.4 us
    ppermute x15, starting transfers between devices, send(): return lax.ppermute(a, 'cp', pairs)  12.1 us
  transfers between devices with their start and end apart: 15, of which 6 were waited for; matrix products, arithmetic and copies ran while one was open for 7% of the time, Pallas kernels for 55%

commit v1 on v0

--- a/solution.py
+++ b/solution.py
@@ -13,7 +13,6 @@
 HD = 128
 WIDE = HEADS * BLK
 HALF = 8
-VMEM_LIMIT = 60 * 1024 * 1024
 
 
 def dot(a, b):
@@ -64,17 +63,27 @@
     return same & (rel <= (query_block - key_block) * BLK)
 
 
-def fwd_kernel(seg_ref, ids_ref, q_own, q_oth, kv_far, kv_near, rows_ref,
-               o_own, o_oth, lse_ref, segk, kv_ref, qt, acc, m_ref, l_ref, f_ref, pm):
+def full_blocks(seg_ref, ids_ref, step, hi):
+    last = seg_ref[(HALF + step) * BLK + BLK - 1]
+    count = jnp.int32(0)
+    for p in range(2 * HALF):
+        same = seg_ref[store_block(p, ids_ref[0]) * BLK] == last
+        count += (same & (p < hi)).astype(jnp.int32)
+    return count
+
+
+def fwd_kernel(seg_ref, ids_ref, q_own, q_oth, kv_far0, kv_far1, kv_own, kv_oth, rows_ref,
+               o_own, o_oth, lse_ref, segk, kv_ref, qt, acc, m_ref, l_ref, pm):
     step = pl.program_id(0)
     core = ids_ref[0]
     scale2 = HD ** -0.5 * math.log2(math.e)
+    tok = kv_own.shape[0]
 
     @pl.when(step == 0)
     def _():
         spread_segments(rows_ref, segk, 0, 2 * HALF)
-        kv_ref[:HALF * BLK, :] = kv_far[...]
-        kv_ref[HALF * BLK:, :] = kv_near[...]
+        for i, part in enumerate((kv_far0, kv_far1, kv_own, kv_oth)):
+            kv_ref[i * tok:(i + 1) * tok, :] = part[...]
 
     @pl.when(step < 4)
     def _():
@@ -84,35 +93,84 @@
     def _():
         flip_heads(q_oth, qt)
 
-    acc[...] = jnp.zeros_like(acc)
-    m_ref[...] = jnp.full_like(m_ref, -jnp.inf)
-    l_ref[...] = jnp.zeros_like(l_ref)
     hi = HALF + ((step + 4 * core) & (HALF - 1))
-    count = hi - first_block(seg_ref, ids_ref, step) + 1
+    lo = first_block(seg_ref, ids_ref, step)
+    full = jnp.maximum(hi - full_blocks(seg_ref, ids_ref, step, hi), lo)
     segq = rows_ref[HALF + step]
 
-    def body(it, carry):
-        p = hi - it
-        key_start = pl.multiple_of(store_block(p, core) * BLK, BLK)
-        k_blk = kv_ref[pl.ds(key_start, BLK), :HD]
-        v_t = kv_ref[pl.ds(key_start, BLK), HD:].T
-        mask = pair_mask(segk[pl.ds(key_start, BLK), :], segq, p, hi)
+    def start_of(p):
+        return pl.multiple_of(store_block(p, core) * BLK, BLK)
+
+    def fold(w):
+        return jnp.sum(w.reshape(BLK // 8, 8, BLK), axis=0)
+
+    def keys(start):
+        return kv_ref[pl.ds(start, BLK), :HD]
+
+    def values(start):
+        return kv_ref[pl.ds(pl.multiple_of(start, BLK), BLK), HD:].T
+
+    def mask_of(start, p):
+        return pair_mask(segk[pl.ds(start, BLK), :], segq, p, hi)
+
+    def diagonal():
+        start = start_of(hi)
+        mask = mask_of(start, hi)
         for h in range(HEADS):
             cols = slice(h * BLK, (h + 1) * BLK)
-            s = jnp.where(mask, dot(k_blk, qt[:, cols]) * scale2, -jnp.inf)
-            m_old = m_ref[:, cols]
-            m_new = jnp.maximum(m_old, jnp.max(s, axis=0, keepdims=True))
-            w = jnp.exp2(s - m_new)
-            fac = jnp.exp2(m_old - m_new)
-            m_ref[:, cols] = m_new
-            l_ref[:, cols] = l_ref[:, cols] * fac + jnp.sum(w, axis=0, keepdims=True)
-            f_ref[:, cols] = fac
+            s = jnp.where(mask, dot(keys(start), qt[:, cols]) * scale2, -jnp.inf)
+            top = jnp.max(s, axis=0, keepdims=True)
+            w = jnp.exp2(s - top)
+            m_ref[:, cols] = top
+            l_ref[:, cols] = fold(w)
             pm[:, cols] = w.astype(jnp.bfloat16)
-        acc[...] = acc[...] * f_ref[...] + dot(v_t, pm[...])
-        return carry
-
-    lax.fori_loop(0, count, body, 0)
-    total = l_ref[...]
+        acc[...] = jnp.zeros_like(acc)
+        return start
+
+    def weigh(p, prev, masked):
+        start = start_of(p)
+        v_t = values(prev)
+        k_blk = keys(start)
+        if masked:
+            mask = mask_of(start, p)
+        for h in range(HEADS):
+            cols = slice(h * BLK, (h + 1) * BLK)
+            s = dot(k_blk, qt[:, cols]) * scale2 - m_ref[:, cols]
+            acc[:, cols] += dot(v_t, pm[:, cols])
+            if masked:
+                s = jnp.where(mask, s, -jnp.inf)
+            w = jnp.exp2(s)
+            l_ref[:, cols] += fold(w)
+            pm[:, cols] = w.astype(jnp.bfloat16)
+        return start
+
+    prev = diagonal()
+    prev = lax.fori_loop(0, hi - full, lambda i, c: weigh(hi - 1 - i, c, False), prev)
+    prev = lax.fori_loop(0, full - lo, lambda i, c: weigh(full - 1 - i, c, True), prev)
+    acc[...] += dot(values(prev), pm[...])
+
+    @pl.when(jnp.logical_not(jnp.max(l_ref[...]) <= 2.0 ** 20))
+    def _():
+        def safe(i, carry):
+            p = hi - 1 - i
+            start = start_of(p)
+            mask = mask_of(start, p)
+            for h in range(HEADS):
+                cols = slice(h * BLK, (h + 1) * BLK)
+                s = jnp.where(mask, dot(keys(start), qt[:, cols]) * scale2, -jnp.inf)
+                top = jnp.maximum(m_ref[:, cols], jnp.max(s, axis=0, keepdims=True))
+                fac = jnp.exp2(m_ref[:, cols] - top)
+                w = jnp.exp2(s - top)
+                m_ref[:, cols] = top
+                l_ref[:, cols] = l_ref[:, cols] * fac + fold(w)
+                acc[:, cols] = acc[:, cols] * fac + dot(values(start), w.astype(jnp.bfloat16))
+            return carry
+
+        first = diagonal()
+        acc[...] += dot(values(first), pm[...])
+        lax.fori_loop(0, hi - lo, safe, 0)
+
+    total = jnp.sum(l_ref[...], axis=0, keepdims=True)
     lse_ref[0] = m_ref[...] + jnp.log2(total)
     inv = 1.0 / total
 
@@ -231,6 +289,19 @@
         at_ref[:, t:t + BLK] = a_ref[t:t + BLK, pl.ds(first, cols)].T
 
 
+def project_kv_kernel(ids_ref, a_ref, wk_ref, wv_ref, out_ref, mine_ref, other_ref, wide):
+    @pl.when(pl.program_id(0) == 0)
+    def _():
+        dim = mine_ref.shape[0]
+        for i, ref in enumerate((wk_ref, wv_ref)):
+            wide[...] = ref[...].astype(jnp.float32)
+            cols = slice(i * HD, (i + 1) * HD)
+            mine_ref[:, cols] = wide[pl.ds(ids_ref[0], dim, stride=2), :].astype(jnp.bfloat16)
+            other_ref[:, cols] = wide[pl.ds(1 - ids_ref[0], dim, stride=2), :].astype(jnp.bfloat16)
+
+    out_ref[...] = dot(a_ref[...], mine_ref[...]).astype(jnp.bfloat16)
+
+
 def expand_kernel(ids_ref, a_ref, b_ref, wa_ref, wb_ref, out_ref):
     out_ref[...] = (dot_nt(a_ref[...], lanes(wa_ref, 0, HEADS))
                     + dot_nt(b_ref[...], lanes(wb_ref, 0, HEADS))).astype(jnp.bfloat16)
@@ -280,13 +351,13 @@
     return (i, 0, 0)
 
 
-def params():
-    return pltpu.CompilerParams(dimension_semantics=('arbitrary',), vmem_limit_bytes=VMEM_LIMIT)
+def params(mib):
+    return pltpu.CompilerParams(dimension_semantics=('arbitrary',), vmem_limit_bytes=mib * 1024 * 1024)
 
 
 def attend(seg, ids, q_own, q_oth, kv_far, kv_near, rows):
-    keys = 2 * kv_near.shape[0]
     tok = q_own.shape[0]
+    keys = 4 * tok
     grid = 2 * tok // BLK
     qspec = [pl.BlockSpec((BLK, HEADS * HD), own_block), pl.BlockSpec((BLK, HEADS * HD), oth_block)]
     stat = pltpu.VMEM((1, WIDE), jnp.float32)
@@ -294,17 +365,17 @@
         fwd_kernel,
         grid_spec=pltpu.PrefetchScalarGridSpec(
             num_scalar_prefetch=2, grid=(grid,),
-            in_specs=qspec + [pl.BlockSpec((keys // 2, 2 * HD), whole)] * 2
+            in_specs=qspec + [pl.BlockSpec((tok, 2 * HD), whole)] * 4
             + [pl.BlockSpec((keys // BLK, 1, BLK), whole3)],
             out_specs=qspec + [pl.BlockSpec((1, 1, WIDE), lead)],
             scratch_shapes=[pltpu.VMEM((keys, 128), jnp.int32), pltpu.VMEM((keys, 2 * HD), jnp.bfloat16),
                             pltpu.VMEM((HD, WIDE), jnp.bfloat16), pltpu.VMEM((HD, WIDE), jnp.float32),
-                            stat, stat, stat, pltpu.VMEM((BLK, WIDE), jnp.bfloat16)]),
+                            stat, pltpu.VMEM((8, WIDE), jnp.float32), pltpu.VMEM((BLK, WIDE), jnp.bfloat16)]),
         out_shape=[jax.ShapeDtypeStruct((tok, HEADS * HD), jnp.bfloat16)] * 2
         + [jax.ShapeDtypeStruct((grid, 1, WIDE), jnp.float32)],
-        compiler_params=params(), name='attend',
+        compiler_params=params(28), name='attend',
         cost_estimate=pl.CostEstimate(flops=40 * 4 * WIDE * BLK * HD, bytes_accessed=12 << 20, transcendentals=0),
-    )(seg, ids, q_own, q_oth, kv_far, kv_near, rows)
+    )(seg, ids, q_own, q_oth, *kv_far, *kv_near, rows)
 
 
 def attend_grad(remote, seg, ids, q, do, o, kv, rows, lse, dq_in=None):
@@ -336,7 +407,7 @@
             scratch_shapes=[pltpu.VMEM((keys, 128), jnp.int32), stack, flip, stack, flip,
                             pltpu.VMEM((1, WIDE), jnp.float32),
                             tile, tile, pltpu.VMEM((HD, WIDE), jnp.float32)]),
-        out_shape=out_shape, compiler_params=params(),
+        out_shape=out_shape, compiler_params=params(36),
         name='attend_grad_remote' if remote else 'attend_grad_local',
         cost_estimate=pl.CostEstimate(flops=20 * 10 * WIDE * BLK * HD, bytes_accessed=20 << 20, transcendentals=0),
     )(*args)
@@ -355,9 +426,27 @@
                        pl.BlockSpec((dim // steps, tok), lambda i, ids: (i, 0))]),
         out_shape=[jax.ShapeDtypeStruct((tok, HEADS * HD), jnp.bfloat16),
                    jax.ShapeDtypeStruct((dim, tok), jnp.bfloat16)],
-        compiler_params=params(),
+        compiler_params=params(16),
         cost_estimate=pl.CostEstimate(flops=2 * tok * dim * HEADS * HD, bytes_accessed=10 << 20, transcendentals=0),
     )(ids, a, w)
+
+
+def project_kv(ids, a, w_k, w_v):
+    tok, dim = a.shape
+    mine = jax.ShapeDtypeStruct((dim, 2 * HD), jnp.bfloat16)
+    pack = pl.BlockSpec((2 * dim, HD), whole)
+    return pl.pallas_call(
+        project_kv_kernel,
+        grid_spec=pltpu.PrefetchScalarGridSpec(
+            num_scalar_prefetch=1, grid=(2,),
+            in_specs=[pl.BlockSpec((tok // 2, dim), lambda i, ids: (i, 0)), pack, pack],
+            out_specs=[pl.BlockSpec((tok // 2, 2 * HD), lambda i, ids: (i, 0))]
+            + [pl.BlockSpec((dim, 2 * HD), whole)] * 2,
+            scratch_shapes=[pltpu.VMEM((2 * dim, HD), jnp.float32)]),
+        out_shape=[jax.ShapeDtypeStruct((tok, 2 * HD), jnp.bfloat16), mine, mine],
+        compiler_params=params(20), name='project_kv',
+        cost_estimate=pl.CostEstimate(flops=4 * tok * dim * HD, bytes_accessed=6 << 20, transcendentals=0),
+    )(ids, a, w_k.reshape(2 * dim, HD), w_v.reshape(2 * dim, HD))
 
 
 def expand(ids, a, b, w, extra=()):
@@ -369,18 +458,16 @@
              pl.BlockSpec((HEADS, cols, HD), lambda i, ids: (1 - ids[0], i, 0))]
     args = [a, b, w, w]
     if extra:
-        c, d, w_kv = extra
         act = pl.BlockSpec((tok, 2 * HD), whole)
-        specs += [act, act, pl.BlockSpec((cols, 2 * HD), lambda i, ids: (i, ids[0])),
-                  pl.BlockSpec((cols, 2 * HD), lambda i, ids: (i, 1 - ids[0]))]
-        args += [c, d, w_kv, w_kv]
+        specs += [act, act] + [pl.BlockSpec((cols, 2 * HD), lambda i, ids: (i, 0))] * 2
+        args += extra
     return pl.pallas_call(
         expand_kv_kernel if extra else expand_kernel,
         grid_spec=pltpu.PrefetchScalarGridSpec(
             num_scalar_prefetch=1, grid=(dim // cols,), in_specs=specs,
             out_specs=pl.BlockSpec((tok, cols), lambda i, ids: (0, i))),
         out_shape=jax.ShapeDtypeStruct((tok, dim), jnp.bfloat16),
-        compiler_params=params(), name='grad_x' if extra else 'out_y',
+        compiler_params=params(20), name='grad_x' if extra else 'out_y',
         cost_estimate=pl.CostEstimate(flops=4 * tok * dim * width, bytes_accessed=14 << 20, transcendentals=0),
     )(ids, *args)
 
@@ -402,7 +489,7 @@
             in_specs=[a_spec] * 2 + [b_spec] * 2 + [c_spec] * 2,
             out_specs=pl.BlockSpec((heads, rows, HD), lambda i, ids: (lax.rem(i + half * ids[1], 2 * half), 0, 0))),
         out_shape=jax.ShapeDtypeStruct((2 * width // HD, rows, HD), jnp.float32),
-        compiler_params=params(),
+        compiler_params=params(16),
         cost_estimate=pl.CostEstimate(flops=8 * tok * rows * width, bytes_accessed=10 << 20, transcendentals=0),
     )(jnp.stack([where, core]).astype(jnp.int32), *a, *b, *c)
 
@@ -441,34 +528,32 @@
 
         x_o = send(x, core_pairs)
         seg_o = send(seg, core_pairs)
-        dy_o = send(dy, core_pairs)
+        kv_own, wkv_c, wkv_p = project_kv(ids, x, w_k, w_v)
+        kv_far0 = send(kv_own, up_pairs)
+        kv_oth = dot(x_o, wkv_c).astype(jnp.bfloat16)
+        kv_far1 = send(kv_oth, up_pairs)
+        dy_o = send(after(dy, kv_own), core_pairs)
         seg_near = jnp.concatenate([seg, seg_o])
         seg_far = send(seg_near, up_pairs)
         seg_all = jnp.concatenate([seg_far, seg_near])
         seg_rows = seg_all.reshape(-1, 1, BLK)
-
-        w_kv = jnp.stack([w_k, w_v], axis=2).reshape(dim, 4 * HD)
-        w_kv = lax.optimization_barrier(w_kv)
-        wkv_c = lax.dynamic_slice_in_dim(w_kv, core * 2 * HD, 2 * HD, 1)
-        kv_own = dot(x, wkv_c).astype(jnp.bfloat16)
-        kv_oth = dot(x_o, wkv_c).astype(jnp.bfloat16)
-        kv_near = jnp.concatenate([kv_own, kv_oth], axis=0)
-        kv_far = send(kv_near, up_pairs)
-        q_own, xt = project(ids, after(x, kv_near), w_q)
-        q_oth, xt_o = project(ids, x_o, w_q)
-        do_own, dyt = project(ids, dy, w_o)
-        do_oth, dyt_o = project(ids, dy_o, w_o)
-        q, do, xt, dyt = (q_own, q_oth), (do_own, do_oth), (xt, xt_o), (dyt, dyt_o)
+        kv_far, kv_near = (kv_far0, kv_far1), (kv_own, kv_oth)
+        q_own, xt = project(ids, after(x, kv_own), w_q)
+        q_oth, xt_o = project(ids, after(x_o, kv_oth), w_q)
+        q, xt = (q_own, q_oth), (xt, xt_o)
 
         *o, lse = attend(seg_all, ids, q[0], q[1], kv_far, kv_near, seg_rows)
         o_p = swap(o)
+        do_own, dyt = project(ids, after(dy, o[0]), w_o)
+        do_oth, dyt_o = project(ids, after(dy_o, o[0]), w_o)
+        do, dyt = (do_own, do_oth), (dyt, dyt_o)
         dwo_far = wgrad(far_rows, core, dyt, o, o_p)
         dwo_in = send(dwo_far, chip_pairs)
 
         lse = after(lse, dwo_far)
-        dq_part, dkv_far = attend_grad(True, seg_all, ids, q, do, o, kv_far, seg_rows, lse)
+        dq_part, dkv_far = attend_grad(True, seg_all, ids, q, do, o, jnp.concatenate(kv_far), seg_rows, lse)
         dkv_in = send(dkv_far, down_pairs)
-        dq_own, dq_oth, dkv_near = attend_grad(False, seg_all, ids, q, do, o, kv_near, seg_rows, lse, dq_part)
+        dq_own, dq_oth, dkv_near = attend_grad(False, seg_all, ids, q, do, o, jnp.concatenate(kv_near), seg_rows, lse, dq_part)
         dq = (dq_own, dq_oth)
         dq_p = swap(dq)
         dwq_far = wgrad(far_rows, core, xt, dq, dq_p)
@@ -485,7 +570,7 @@
         dwkv_far = wgrad(far_rows, core, xt, dkv, dkv_p)
         dwkv_in = send(dwkv_far, chip_pairs)
         dwkv_near = wgrad(near_rows, core, (xt[0], after(xt[1], dwkv_far)), dkv, dkv_p)
-        dx = expand(ids, after(dq[0], dwkv_far), dq_p[0], w_q, (dkv[0], dkv_p[0], w_kv))
+        dx = expand(ids, after(dq[0], dwkv_far), dq_p[0], w_q, (dkv[0], dkv_p[0], wkv_c, wkv_p))
 
         dw_q = jnp.transpose(dwq_near + dwq_in, (1, 0, 2))
         dw_o = jnp.transpose(dwo_near + dwo_in, (1, 0, 2))

time: 327 us -> 332 us (1.015)
  other arithmetic: 14.4 us -> 7.12 us
  Pallas kernels: 201 us -> 208 us
  local copies, waits for them, and re-layouts: 11.4 us -> 16.7 us
  matrix products: 6.31 us -> 2.87 us
    pallas_call x1, Pallas kernels: 38.8 us -> 81.5 us  [attend(): pl.pallas_call(fwd_kernel, grid_spec=pltpu.PrefetchScalarGridSpec(num_sca...]
    pallas_call x6, Pallas kernels: 45.2 us -> 28.7 us  [wgrad(): pl.pallas_call(wgrad_kernel, grid_spec=pltpu.PrefetchScalarGridSpec(num_s...]
    pallas_call x4, Pallas kernels: 30.6 us -> 18.6 us  [project(): pl.pallas_call(project_kernel, grid_spec=pltpu.PrefetchScalarGridSpec(num...]
    unnamed x32 -> x72, local copies, waits for them, and re-layouts: 4.16 us -> 15.1 us
    pallas_call x2, Pallas kernels: 64.6 us -> 58.8 us  [attend_grad(): pl.pallas_call(functools.partial(bwd_kernel, remote), grid_spec=pltpu.Pre...]
    another operation x1 -> x0, local copies, waits for them, and re-layouts: 4.97 us -> none  [layer(): w_kv = jnp.stack([w_k, w_v], axis=2).reshape(dim, 4 * HD)]
    another operation x2 -> x1, other arithmetic: 3.73 us -> 0.09 us  [the longest x1 3.64 us: layer(): w_kv = jnp.stack([w_k, w_v], axis=2).reshape(dim, 4 * HD)]
    dot_general x2 -> x1, matrix products: 6.31 us -> 2.87 us  [dot(): return jnp.dot(a, b, preferred_element_type=jnp.float32)]
  transfers between devices with their start and end apart: 15 -> 16, of which waited for: 6 -> 6; matrix products, arithmetic and copies ran while one was open for 7% -> 3% of each run, Pallas kernels for 55% -> 57%
where the time goes in v1:
time: 332 us; the launch traced here: 331 us
  Pallas kernels  208 us (63%)
  waiting for transfers between devices  81.1 us (24%)
  local copies, waits for them, and re-layouts  16.7 us (5%)
  starting transfers between devices  14.3 us (4%)
  other arithmetic  7.12 us (2%)
    pallas_call x1, Pallas kernels, attend(): pl.pallas_call(fwd_kernel, grid_spec=pltpu.PrefetchScalarGridSpec(num_sca...  81.5 us
    ppermute x16, waiting for transfers between devices, send(): return lax.ppermute(a, 'cp', pairs)  81.1 us
    pallas_call x2, Pallas kernels, attend_grad(): pl.pallas_call(functools.partial(bwd_kernel, remote), grid_spec=pltpu.Pre...  58.8 us
    pallas_call x6, Pallas kernels, wgrad(): pl.pallas_call(wgrad_kernel, grid_spec=pltpu.PrefetchScalarGridSpec(num_s...  28.7 us
    pallas_call x4, Pallas kernels, project(): pl.pallas_call(project_kernel, grid_spec=pltpu.PrefetchScalarGridSpec(num...  18.6 us
    pallas_call x2, Pallas kernels, expand(): pl.pallas_call(expand_kv_kernel if extra else expand_kernel, grid_spec=pl...  18.2 us
    unnamed x72, local copies, waits for them, and re-layouts  15.1 us
    ppermute x16, starting transfers between devices, send(): return lax.ppermute(a, 'cp', pairs)  14.3 us
  transfers between devices with their start and end apart: 16, of which 6 were waited for; matrix products, arithmetic and copies ran while one was open for 3% of the time, Pallas kernels for 57%

profile of v1, /device:TPU:0, one launch (start us, length us, event | category | flops | bytes accessed | tf_op | source)
XLA Modules:
  0.0 331.3 jit_solution(6952076568238201025)
XLA Ops:
  5.7 2.2 project_kv.1
  8.9 4.9 %collective-permute-start.3 = (bf16[1024,256]{1,0:T(8,128)(2,1)S(1)}, bf16[1024,256]{1,0:T(8,128)(2,1)S(1)}, u32[]{:S(2)}, u32[]{:S(2)}) collective-permute-start(bf16[1024,256]{1,0:T(8,128)(2,1)S(1)} %get-tuple-element.36.kv_own), channel_id=1, source_target_pairs={{0,2},{1,3},{4,6},{5,7}} | collective-permute-start | bytes 1572872 | tf_op jit(solution)/shard_map/ppermute | solution.py:512
  13.8 3.6 %shard_map.118 = (bf16[1024,768]{1,0:T(8,128)(2,1)S(1)}, bf16[1536,1024]{1,0:T(8,128)(2,1)S(1)}) custom-call(s32[2]{0:T(128)S(1)} %pad_add_fusion.1.ids_ref.refs_1_, bf16[1024,1536]{1,0:T(8,128)(2,1)S(1)} %copy-done.5, bf16[12,1536,128]{2,1,0:T(8,128)(2,1)S(1)} %bitcast.24), custom_call_target="tpu_custom_call" | custom-call | flops 2415919104 | bytes 10485760 | tf_op jit(solution)/shard_map/pallas_call | solution.py:419
  19.4 2.9 fusion.kv_oth
  23.8 2.4 collective-permute-done.1
  26.2 5.5 %shard_map.119 = (bf16[1024,768]{1,0:T(8,128)(2,1)S(1)}, bf16[1536,1024]{1,0:T(8,128)(2,1)S(1)}) custom-call(s32[2]{0:T(128)S(1)} %pad_add_fusion.1.ids_ref.refs_1_, bf16[1024,1536]{1,0:T(8,128)(2,1)} %collective-permute-done.2.a_ref, bf16[12,1536,128]{2,1,0:T(8,128)(2,1)S(1)} %bitcast.25), custom_call_target="tpu_custom_call" | custom-call | flops 2415919104 | bytes 10485760 | tf_op jit(solution)/shard_map/pallas_call | solution.py:419
  33.4 3.1 collective-permute-done.4.kv_far1
  36.5 81.5 %attend.1 = (bf16[1024,768]{1,0:T(8,128)(2,1)}, bf16[1024,768]{1,0:T(8,128)(2,1)}, f32[8,1,1536]{2,1,0:T(1,128)S(1)}) custom-call(s32[4096]{0:T(1024)S(1)} %constant_dynamic-update-slice_fusion.seg_ref.refs_0_, s32[2]{0:T(128)S(1)} %pad_add_fusion.1.ids_ref.refs_1_, bf16[1024,768]{1,0:T(8,128)(2,1)S(1)} %get-tuple-element.38.q_own.refs_2_, ...), custom_call_target="tpu_custom_call" | custom-call | flops 8053063680 | bytes 12582912 | tf_op jit(solution)/shard_map/attend/pallas_call | solution.py:364
  120.0 2.3 copy-done.18
  122.3 5.8 %shard_map.121 = (bf16[1024,768]{1,0:T(8,128)(2,1)S(1)}, bf16[1536,1024]{1,0:T(8,128)(2,1)S(1)}) custom-call(s32[2]{0:T(128)S(1)} %pad_add_fusion.1.ids_ref.refs_1_, bf16[1024,1536]{1,0:T(8,128)(2,1)} %collective-permute-done.5.a_ref, bf16[12,1536,128]{2,1,0:T(8,128)(2,1)S(1)} %bitcast.35), custom_call_target="tpu_custom_call" | custom-call | flops 2415919104 | bytes 10485760 | tf_op jit(solution)/shard_map/pallas_call | solution.py:419
  128.1 3.6 %shard_map.120 = (bf16[1024,768]{1,0:T(8,128)(2,1)S(1)}, bf16[1536,1024]{1,0:T(8,128)(2,1)S(1)}) custom-call(s32[2]{0:T(128)S(1)} %pad_add_fusion.1.ids_ref.refs_1_, bf16[1024,1536]{1,0:T(8,128)(2,1)S(1)} %copy-done.19, bf16[12,1536,128]{2,1,0:T(8,128)(2,1)S(1)} %bitcast.36), custom_call_target="tpu_custom_call" | custom-call | flops 2415919104 | bytes 10485760 | tf_op jit(solution)/shard_map/pallas_call | solution.py:419
  131.9 8.9 %shard_map.122 = f32[12,384,128]{2,1,0:T(8,128)S(1)} custom-call(s32[2]{0:T(128)S(1)} %pad_add_fusion.2.ids_ref, bf16[1536,1024]{1,0:T(8,128)(2,1)S(1)} %get-tuple-element.52.a_own, bf16[1536,1024]{1,0:T(8,128)(2,1)S(1)} %get-tuple-element.65.a_oth, bf16[1024,768]{1,0:T(8,128)(2,1)} %get-tuple-element.58.b_own.refs_6_.a_ref, ...), custom_call_target="tpu_custom_call" | custom-call | flops 2415919104 | bytes 10485760 | tf_op jit(solution)/shard_map/pallas_call | solution.py:485
  140.9 8.9 %attend_grad_remote.1 = (f32[8,128,1536]{2,1,0:T(8,128)}, f32[2048,256]{1,0:T(8,128)}) custom-call(s32[4096]{0:T(1024)S(1)} %constant_dynamic-update-slice_fusion.seg_ref.refs_0_, s32[2]{0:T(128)S(1)} %pad_add_fusion.1.ids_ref.refs_1_, bf16[1024,768]{1,0:T(8,128)(2,1)S(1)} %copy-done.21, bf16[1024,768]{1,0:T(8,128)(2,1)S(1)} %copy-done.24, ...), custom_call_target="tpu_custom_call" | custom-call | flops 10066329600 | bytes 20971520 | tf_op jit(solution)/shard_map/attend_grad_remote/pallas_call | solution.py:403
  156.9 49.9 %attend_grad_local.1 = (bf16[1024,768]{1,0:T(8,128)(2,1)S(1)}, bf16[1024,768]{1,0:T(8,128)(2,1)S(1)}, f32[2048,256]{1,0:T(8,128)S(1)}) custom-call(s32[4096]{0:T(1024)S(1)} %constant_dynamic-update-slice_fusion.seg_ref.refs_0_, s32[2]{0:T(128)S(1)} %pad_add_fusion.1.ids_ref.refs_1_, bf16[1024,768]{1,0:T(8,128)(2,1)S(1)} %copy-done.22, ...), custom_call_target="tpu_custom_call" | custom-call | flops 10066329600 | bytes 20971520 | tf_op jit(solution)/shard_map/attend_grad_local/pallas_call | solution.py:403
  207.4 2.8 collective-permute-done.8.c_own.b_ref
  210.3 2.2 collective-permute-done.9.c_oth
  212.5 4.7 %shard_map.123 = f32[12,384,128]{2,1,0:T(8,128)S(1)} custom-call(s32[2]{0:T(128)S(1)} %pad_add_fusion.2.ids_ref, bf16[1536,1024]{1,0:T(8,128)(2,1)S(1)} %get-tuple-element.43.a_own, bf16[1536,1024]{1,0:T(8,128)(2,1)S(1)} %copy-done.1, bf16[1024,768]{1,0:T(8,128)(2,1)S(1)} %get-tuple-element.61.b_own.a_ref, bf16[1024,768]{1,0:T(8,128)(2,1)S(1)} %get-tuple-element.57.b_oth, ...), custom_call_target="tpu_custom_call" | custom-call | flops 2415919104 | bytes 10485760 | tf_op jit(solution)/shard_map/pallas_call | solution.py:485
  217.2 7.0 %shard_map.127 = f32[12,384,128]{2,1,0:T(8,128)S(1)} custom-call(s32[2]{0:T(128)S(1)} %pad_add_fusion.3.ids_ref, bf16[1536,1024]{1,0:T(8,128)(2,1)S(1)} %copy-done.4, bf16[1536,1024]{1,0:T(8,128)(2,1)S(1)} %get-tuple-element.65.a_oth, bf16[1024,768]{1,0:T(8,128)(2,1)} %get-tuple-element.58.b_own.refs_6_.a_ref, ...), custom_call_target="tpu_custom_call" | custom-call | flops 2415919104 | bytes 10485760 | tf_op jit(solution)/shard_map/pallas_call | solution.py:485
  226.9 4.7 %shard_map.125 = f32[12,384,128]{2,1,0:T(8,128)S(1)} custom-call(s32[2]{0:T(128)S(1)} %pad_add_fusion.3.ids_ref, bf16[1536,1024]{1,0:T(8,128)(2,1)S(1)} %get-tuple-element.43.a_own, bf16[1536,1024]{1,0:T(8,128)(2,1)S(1)} %copy-done.1, bf16[1024,768]{1,0:T(8,128)(2,1)S(1)} %get-tuple-element.61.b_own.a_ref, bf16[1024,768]{1,0:T(8,128)(2,1)S(1)} %get-tuple-element.57.b_oth, ...), custom_call_target="tpu_custom_call" | custom-call | flops 2415919104 | bytes 10485760 | tf_op jit(solution)/shard_map/pallas_call | solution.py:485
  231.6 9.2 %out_y.1 = bf16[1024,1536]{1,0:T(8,128)(2,1)} custom-call(s32[2]{0:T(128)S(1)} %pad_add_fusion.1.ids_ref.refs_1_, bf16[1024,768]{1,0:T(8,128)(2,1)} %get-tuple-element.58.b_own.refs_6_.a_ref, bf16[1024,768]{1,0:T(8,128)(2,1)} %collective-permute-done.6.c_own.b_ref, bf16[12,1536,128]{2,1,0:T(8,128)(2,1)S(1)} %bitcast.39, bf16[12,1536,128]{2,1,0:T(8,128)(2,1)S(1)} %bitcast.40), custom_call_target="tpu_custom_call" | custom-call | flops 4831838208 | bytes 14680064 | tf_op jit(solution)/shard_map/out_y/pallas_call | solution.py:464
  242.6 2.0 collective-permute-start.14
  244.6 16.9 %collective-permute-done.15 = f32[12,384,128]{2,1,0:T(8,128)S(1)} collective-permute-done((f32[12,384,128]{2,1,0:T(8,128)S(1)}, f32[12,384,128]{2,1,0:T(8,128)S(1)}, u32[]{:S(2)}, u32[]{:S(2)}) %collective-permute-start.15) | collective-permute-done | bytes 2359328 | tf_op jit(solution)/shard_map/ppermute | solution.py:512
  265.3 9.0 %grad_x.1 = bf16[1024,1536]{1,0:T(8,128)(2,1)} custom-call(s32[2]{0:T(128)S(1)} %pad_add_fusion.1.ids_ref.refs_1_, bf16[1024,768]{1,0:T(8,128)(2,1)S(1)} %get-tuple-element.61.b_own.a_ref, bf16[1024,768]{1,0:T(8,128)(2,1)S(1)} %collective-permute-done.8.c_own.b_ref, bf16[12,1536,128]{2,1,0:T(8,128)(2,1)S(1)} %bitcast.28, ...), custom_call_target="tpu_custom_call" | custom-call | flops 4831838208 | bytes 14680064 | tf_op jit(solution)/shard_map/grad_x/pallas_call | solution.py:464
  274.3 53.6 %collective-permute-done.14 = f32[4,384,128]{2,1,0:T(8,128)S(1)} collective-permute-done((f32[4,384,128]{2,1,0:T(8,128)S(1)}, f32[4,384,128]{2,1,0:T(8,128)S(1)}, u32[]{:S(2)}, u32[]{:S(2)}) %collective-permute-start.14) | collective-permute-done | bytes 786464 | tf_op jit(solution)/shard_map/ppermute | solution.py:512
  (115 shorter events, 32.4 us)
Async XLA Ops:
  0.6 18.7 %collective-permute-start.2 = (bf16[1024,1536]{1,0:T(8,128)(2,1)}, bf16[1024,1536]{1,0:T(8,128)(2,1)}, u32[]{:S(2)}, u32[]{:S(2)}) collective-permute-start(bf16[1024,1536]{1,0:T(8,128)(2,1)} %a_ref.2), channel_id=1, source_target_pairs={{0,1},{1,0},{2,3},{3,2},{4,5},{5,4},{6,7},{7,6}} | collective-permute-start | bytes 9437192 | tf_op jit(solution)/shard_map/ppermute | solution.py:512
  8.8 27.7 %copy-start.14 = (bf16[1024,256]{1,0:T(8,128)(2,1)}, bf16[1024,256]{1,0:T(8,128)(2,1)S(1)}, u32[]{:S(2)}) copy-start(bf16[1024,256]{1,0:T(8,128)(2,1)S(1)} %get-tuple-element.36.kv_own) | copy-start | bytes 1572868
  8.8 111.1 %collective-permute-start.5 = (bf16[1024,1536]{1,0:T(8,128)(2,1)}, bf16[1024,1536]{1,0:T(8,128)(2,1)}, u32[]{:S(2)}, u32[]{:S(2)}) collective-permute-start(bf16[1024,1536]{1,0:T(8,128)(2,1)} %a_ref.3), channel_id=1, source_target_pairs={{0,1},{1,0},{2,3},{3,2},{4,5},{5,4},{6,7},{7,6}} | collective-permute-start | bytes 9437192 | tf_op jit(solution)/shard_map/ppermute | solution.py:512
  8.9 24.5 %collective-permute-start.3 = (bf16[1024,256]{1,0:T(8,128)(2,1)S(1)}, bf16[1024,256]{1,0:T(8,128)(2,1)S(1)}, u32[]{:S(2)}, u32[]{:S(2)}) collective-permute-start(bf16[1024,256]{1,0:T(8,128)(2,1)S(1)} %get-tuple-element.36.kv_own), channel_id=1, source_target_pairs={{0,2},{1,3},{4,6},{5,7}} | collective-permute-start | bytes 1572872 | tf_op jit(solution)/shard_map/ppermute | solution.py:512
  13.8 3.7 %collective-permute-start = (s32[1024]{0:T(1024)S(1)}, s32[1024]{0:T(1024)S(1)}, u32[]{:S(2)}, u32[]{:S(2)}) collective-permute-start(s32[1024]{0:T(1024)S(1)} %copy-done.30), channel_id=1, source_target_pairs={{0,1},{1,0},{2,3},{3,2},{4,5},{5,4},{6,7},{7,6}} | collective-permute-start | bytes 12296 | tf_op jit(solution)/shard_map/ppermute | solution.py:512
  17.4 19.1 %copy-start.20 = (bf16[1024,768]{1,0:T(8,128)(2,1)}, bf16[1024,768]{1,0:T(8,128)(2,1)S(1)}, u32[]{:S(2)}) copy-start(bf16[1024,768]{1,0:T(8,128)(2,1)S(1)} %get-tuple-element.38.q_own.refs_2_) | copy-start | bytes 4718596
  17.5 8.7 %collective-permute-start.1 = (s32[2048]{0:T(1024)S(1)}, s32[2048]{0:T(1024)S(1)}, u32[]{:S(2)}, u32[]{:S(2)}) collective-permute-start(s32[2048]{0:T(1024)S(1)} %pad_add_fusion), channel_id=1, source_target_pairs={{0,2},{1,3},{4,6},{5,7}} | collective-permute-start | bytes 24584 | tf_op jit(solution)/shard_map/ppermute | solution.py:512
  22.2 14.3 %copy-start.17 = (bf16[1024,256]{1,0:T(8,128)(2,1)}, bf16[1024,256]{1,0:T(8,128)(2,1)S(1)}, u32[]{:S(2)}) copy-start(bf16[1024,256]{1,0:T(8,128)(2,1)S(1)} %fusion.kv_oth) | copy-start | bytes 1572868
  22.2 14.2 %collective-permute-start.4 = (bf16[1024,256]{1,0:T(8,128)(2,1)S(1)}, bf16[1024,256]{1,0:T(8,128)(2,1)S(1)}, u32[]{:S(2)}, u32[]{:S(2)}) collective-permute-start(bf16[1024,256]{1,0:T(8,128)(2,1)S(1)} %fusion.kv_oth), channel_id=1, source_target_pairs={{0,2},{1,3},{4,6},{5,7}} | collective-permute-start | bytes 1572872 | tf_op jit(solution)/shard_map/ppermute | solution.py:512
  33.4 84.7 %copy-start.23 = (bf16[1024,768]{1,0:T(8,128)(2,1)}, bf16[1024,768]{1,0:T(8,128)(2,1)S(1)}, u32[]{:S(2)}) copy-start(bf16[1024,768]{1,0:T(8,128)(2,1)S(1)} %get-tuple-element.41.q_oth.refs_3_) | copy-start | bytes 4718596
  33.4 84.7 %copy-start.12 = (bf16[1024,256]{1,0:T(8,128)(2,1)}, bf16[1024,256]{1,0:T(8,128)(2,1)S(1)}, u32[]{:S(2)}) copy-start(bf16[1024,256]{1,0:T(8,128)(2,1)S(1)} %collective-permute-done.3.kv_far0) | copy-start | bytes 1572868
  36.5 81.6 %copy-start.15 = (bf16[1024,256]{1,0:T(8,128)(2,1)}, bf16[1024,256]{1,0:T(8,128)(2,1)S(1)}, u32[]{:S(2)}) copy-start(bf16[1024,256]{1,0:T(8,128)(2,1)S(1)} %collective-permute-done.4.kv_far1) | copy-start | bytes 1572868
  118.1 13.8 %collective-permute-start.6 = (bf16[1024,768]{1,0:T(8,128)(2,1)}, bf16[1024,768]{1,0:T(8,128)(2,1)}, u32[]{:S(2)}, u32[]{:S(2)}) collective-permute-start(bf16[1024,768]{1,0:T(8,128)(2,1)} %get-tuple-element.50.b_oth.refs_7_), channel_id=1, source_target_pairs={{0,1},{1,0},{2,3},{3,2},{4,5},{5,4},{6,7},{7,6}} | collective-permute-start | bytes 4718600 | tf_op jit(solution)/shard_map/ppermute | solution.py:512
  118.1 13.8 %collective-permute-start.7 = (bf16[1024,768]{1,0:T(8,128)(2,1)}, bf16[1024,768]{1,0:T(8,128)(2,1)}, u32[]{:S(2)}, u32[]{:S(2)}) collective-permute-start(bf16[1024,768]{1,0:T(8,128)(2,1)} %get-tuple-element.58.b_own.refs_6_.a_ref), channel_id=1, source_target_pairs={{0,1},{1,0},{2,3},{3,2},{4,5},{5,4},{6,7},{7,6}} | collective-permute-start | bytes 4718600 | tf_op jit(solution)/shard_map/ppermute | solution.py:512
  128.1 12.7 %copy-start.26 = (bf16[1024,768]{1,0:T(8,128)(2,1)}, bf16[1024,768]{1,0:T(8,128)(2,1)S(1)}, u32[]{:S(2)}) copy-start(bf16[1024,768]{1,0:T(8,128)(2,1)S(1)} %get-tuple-element.49.refs_5_) | copy-start | bytes 4718596
  149.8 74.5 %collective-permute-start.10 = (f32[2048,256]{1,0:T(8,128)}, f32[2048,256]{1,0:T(8,128)}, u32[]{:S(2)}, u32[]{:S(2)}) collective-permute-start(f32[2048,256]{1,0:T(8,128)} %get-tuple-element.60), channel_id=1, source_target_pairs={{2,0},{3,1},{6,4},{7,5}} | collective-permute-start | bytes 6291464 | tf_op jit(solution)/shard_map/ppermute | solution.py:512
  156.9 55.6 %copy-start.1 = (bf16[1536,1024]{1,0:T(8,128)(2,1)S(1)}, bf16[1536,1024]{1,0:T(8,128)(2,1)}, u32[]{:S(2)}) copy-start(bf16[1536,1024]{1,0:T(8,128)(2,1)} %copy-done) | copy-start | bytes 9437188
  206.8 3.4 %collective-permute-start.8 = (bf16[1024,768]{1,0:T(8,128)(2,1)S(1)}, bf16[1024,768]{1,0:T(8,128)(2,1)S(1)}, u32[]{:S(2)}, u32[]{:S(2)}) collective-permute-start(bf16[1024,768]{1,0:T(8,128)(2,1)S(1)} %get-tuple-element.57.b_oth), channel_id=1, source_target_pairs={{0,1},{1,0},{2,3},{3,2},{4,5},{5,4},{6,7},{7,6}} | collective-permute-start | bytes 4718600 | tf_op jit(solution)/shard_map/ppermute | solution.py:512
  206.9 5.6 %collective-permute-start.9 = (bf16[1024,768]{1,0:T(8,128)(2,1)S(1)}, bf16[1024,768]{1,0:T(8,128)(2,1)S(1)}, u32[]{:S(2)}, u32[]{:S(2)}) collective-permute-start(bf16[1024,768]{1,0:T(8,128)(2,1)S(1)} %get-tuple-element.61.b_own.a_ref), channel_id=1, source_target_pairs={{0,1},{1,0},{2,3},{3,2},{4,5},{5,4},{6,7},{7,6}} | collective-permute-start | bytes 4718600 | tf_op jit(solution)/shard_map/ppermute | solution.py:512
  207.4 54.1 %collective-permute-start.15 = (f32[12,384,128]{2,1,0:T(8,128)S(1)}, f32[12,384,128]{2,1,0:T(8,128)S(1)}, u32[]{:S(2)}, u32[]{:S(2)}) collective-permute-start(f32[12,384,128]{2,1,0:T(8,128)S(1)} %shard_map.122), channel_id=1, source_target_pairs={{0,2},{2,0},{1,3},{3,1},{4,6},{6,4},{5,7},{7,5}} | collective-permute-start | bytes 7077896 | tf_op jit(solution)/shard_map/ppermute | solution.py:512
  217.2 112.4 %collective-permute-start.13 = (f32[12,384,128]{2,1,0:T(8,128)S(1)}, f32[12,384,128]{2,1,0:T(8,128)S(1)}, u32[]{:S(2)}, u32[]{:S(2)}) collective-permute-start(f32[12,384,128]{2,1,0:T(8,128)S(1)} %shard_map.123), channel_id=1, source_target_pairs={{0,2},{2,0},{1,3},{3,1},{4,6},{6,4},{5,7},{7,5}} | collective-permute-start | bytes 7077896 | tf_op jit(solution)/shard_map/ppermute | solution.py:512
  226.4 14.4 %collective-permute-start.11 = (bf16[1024,256]{1,0:T(8,128)(2,1)S(1)}, bf16[1024,256]{1,0:T(8,128)(2,1)S(1)}, u32[]{:S(2)}, u32[]{:S(2)}) collective-permute-start(bf16[1024,256]{1,0:T(8,128)(2,1)S(1)} %get-tuple-element.66.b_oth), channel_id=1, source_target_pairs={{0,1},{1,0},{2,3},{3,2},{4,5},{5,4},{6,7},{7,6}} | collective-permute-start | bytes 1572872 | tf_op jit(solution)/shard_map/ppermute | solution.py:512
  226.6 14.2 %collective-permute-start.12 = (bf16[1024,256]{1,0:T(8,128)(2,1)S(1)}, bf16[1024,256]{1,0:T(8,128)(2,1)S(1)}, u32[]{:S(2)}, u32[]{:S(2)}) collective-permute-start(bf16[1024,256]{1,0:T(8,128)(2,1)S(1)} %get-tuple-element.67.b_own.c_ref), channel_id=1, source_target_pairs={{0,1},{1,0},{2,3},{3,2},{4,5},{5,4},{6,7},{7,6}} | collective-permute-start | bytes 1572872 | tf_op jit(solution)/shard_map/ppermute | solution.py:512
  242.6 85.4 %collective-permute-start.14 = (f32[4,384,128]{2,1,0:T(8,128)S(1)}, f32[4,384,128]{2,1,0:T(8,128)S(1)}, u32[]{:S(2)}, u32[]{:S(2)}) collective-permute-start(f32[4,384,128]{2,1,0:T(8,128)S(1)} %shard_map.124), channel_id=1, source_target_pairs={{0,2},{2,0},{1,3},{3,1},{4,6},{6,4},{5,7},{7,5}} | collective-permute-start | bytes 2359304 | tf_op jit(solution)/shard_map/ppermute | solution.py:512
  (27 other events, 118.8 us)

commit v2 on v1

v2 whole, which is shorter than its diff:
```python
import functools
import math

import jax
import jax.numpy as jnp
from jax import lax
from jax.experimental import pallas as pl
from jax.experimental.pallas import tpu as pltpu
from jax.sharding import PartitionSpec as P

BLK = 256
HEADS = 6
HD = 128
WIDE = HEADS * BLK
HALF = 8


def dot(a, b):
    return jnp.dot(a, b, preferred_element_type=jnp.float32)


def dot_nt(a, b):
    return lax.dot_general(a, b, (((1,), (1,)), ((), ())), preferred_element_type=jnp.float32)


def stack_heads(src, dst):
    for h in range(HEADS):
        dst[h * BLK:(h + 1) * BLK, :] = src[:, h * HD:(h + 1) * HD]


def flip_heads(src, dst):
    for h in range(HEADS):
        dst[:, h * BLK:(h + 1) * BLK] = src[:, h * HD:(h + 1) * HD].T


def store_block(p, core):
    return (p & HALF) + ((p + 4 * core) & (HALF - 1))


def first_block(seg_ref, ids_ref, step):
    chip = ids_ref[1]
    first = seg_ref[(HALF + step) * BLK]
    near = jnp.int32(0)
    far = jnp.int32(0)
    for b in range(HALF):
        far += (seg_ref[b * BLK + BLK - 1] < first).astype(jnp.int32)
        near += (seg_ref[(HALF + b) * BLK + BLK - 1] < first).astype(jnp.int32)
    far = jnp.where(chip == 0, HALF, far)
    return far + near


def spread_segments(rows_ref, dst, first, count):
    for b in range(count):
        row = jnp.broadcast_to(rows_ref[first + b], (128, BLK))
        dst[b * BLK:(b + 1) * BLK, :] = row.T


def pair_mask(segk, segq, key_block, query_block):
    segk = jnp.concatenate([segk] * (BLK // 128), axis=1)
    same = segk == segq
    rel = (lax.broadcasted_iota(jnp.int32, (BLK, BLK), 0)
           - lax.broadcasted_iota(jnp.int32, (BLK, BLK), 1))
    return same & (rel <= (query_block - key_block) * BLK)


def full_blocks(seg_ref, ids_ref, step, hi):
    last = seg_ref[(HALF + step) * BLK + BLK - 1]
    count = jnp.int32(0)
    for p in range(2 * HALF):
        same = seg_ref[store_block(p, ids_ref[0]) * BLK] == last
        count += (same & (p < hi)).astype(jnp.int32)
    return count


def fwd_kernel(seg_ref, ids_ref, q_ref, kv_far0, kv_far1, kv_own, kv_oth, rows_ref, o_ref, lse_ref,
               segk, kv_ref, qt, acc, m_ref, l_ref, pm):
    step = pl.program_id(0)
    core = ids_ref[0]
    scale2 = HD ** -0.5 * math.log2(math.e)
    tok = kv_own.shape[0]

    @pl.when(step == 0)
    def _():
        spread_segments(rows_ref, segk, 0, 2 * HALF)
        for i, part in enumerate((kv_far0, kv_far1, kv_own, kv_oth)):
            kv_ref[i * tok:(i + 1) * tok, :] = part[...]

    flip_heads(q_ref, qt)
    hi = HALF + ((step + 4 * core) & (HALF - 1))
    lo = first_block(seg_ref, ids_ref, step)
    full = jnp.maximum(hi - full_blocks(seg_ref, ids_ref, step, hi), lo)
    segq = rows_ref[HALF + step]

    def start_of(p):
        return pl.multiple_of(store_block(p, core) * BLK, BLK)

    def fold(w):
        return jnp.sum(w.reshape(BLK // 8, 8, BLK), axis=0)

    def keys(start):
        return kv_ref[pl.ds(start, BLK), :HD]

    def values(start):
        return kv_ref[pl.ds(pl.multiple_of(start, BLK), BLK), HD:].T

    def mask_of(start, p):
        return pair_mask(segk[pl.ds(start, BLK), :], segq, p, hi)

    def diagonal():
        start = start_of(hi)
        mask = mask_of(start, hi)
        for h in range(HEADS):
            cols = slice(h * BLK, (h + 1) * BLK)
            s = jnp.where(mask, dot(keys(start), qt[:, cols]) * scale2, -jnp.inf)
            top = jnp.max(s, axis=0, keepdims=True)
            w = jnp.exp2(s - top)
            m_ref[:, cols] = top
            l_ref[:, cols] = fold(w)
            pm[:, cols] = w.astype(jnp.bfloat16)
        acc[...] = jnp.zeros_like(acc)
        return start

    def weigh(p, prev, masked):
        start = start_of(p)
        v_t = values(prev)
        k_blk = keys(start)
        if masked:
            mask = mask_of(start, p)
        for h in range(HEADS):
            cols = slice(h * BLK, (h + 1) * BLK)
            s = dot(k_blk, qt[:, cols]) * scale2 - m_ref[:, cols]
            acc[:, cols] += dot(v_t, pm[:, cols])
            if masked:
                s = jnp.where(mask, s, -jnp.inf)
            w = jnp.exp2(s)
            l_ref[:, cols] += fold(w)
            pm[:, cols] = w.astype(jnp.bfloat16)
        return start

    prev = diagonal()
    prev = lax.fori_loop(0, hi - full, lambda i, c: weigh(hi - 1 - i, c, False), prev)
    prev = lax.fori_loop(0, full - lo, lambda i, c: weigh(full - 1 - i, c, True), prev)
    acc[...] += dot(values(prev), pm[...])

    @pl.when(jnp.logical_not(jnp.max(l_ref[...]) <= 2.0 ** 20))
    def _():
        def safe(i, carry):
            p = hi - 1 - i
            start = start_of(p)
            mask = mask_of(start, p)
            for h in range(HEADS):
                cols = slice(h * BLK, (h + 1) * BLK)
                s = jnp.where(mask, dot(keys(start), qt[:, cols]) * scale2, -jnp.inf)
                top = jnp.maximum(m_ref[:, cols], jnp.max(s, axis=0, keepdims=True))
                fac = jnp.exp2(m_ref[:, cols] - top)
                w = jnp.exp2(s - top)
                m_ref[:, cols] = top
                l_ref[:, cols] = l_ref[:, cols] * fac + fold(w)
                acc[:, cols] = acc[:, cols] * fac + dot(values(start), w.astype(jnp.bfloat16))
            return carry

        first = diagonal()
        acc[...] += dot(values(first), pm[...])
        lax.fori_loop(0, hi - lo, safe, 0)

    total = jnp.sum(l_ref[...], axis=0, keepdims=True)
    lse_ref[0] = m_ref[...] + jnp.log2(total)
    inv = 1.0 / total

    for h in range(HEADS):
        cols = slice(h * BLK, (h + 1) * BLK)
        o_ref[:, h * HD:(h + 1) * HD] = (acc[:, cols] * inv[:, cols]).T.astype(jnp.bfloat16)


def bwd_kernel(remote, *refs):
    if remote:
        (seg_ref, ids_ref, q_ref, do_ref, o_ref, kv_own, kv_oth,
         rows_ref, lse_ref, dq_out, dkv_ref,
         segk, kv_ref, qs, qt, ds_, dt, delta, pm, sm, dqt) = refs
    else:
        (seg_ref, ids_ref, q_ref, do_ref, o_ref, kv_own, kv_oth,
         rows_ref, lse_ref, dq_in, dq_out, dkv_ref,
         segk, kv_ref, qs, qt, ds_, dt, delta, pm, sm, dqt) = refs
    step = pl.program_id(0)
    core = ids_ref[0]
    scale = HD ** -0.5
    scale2 = scale * math.log2(math.e)

    @pl.when(step == 0)
    def _():
        dkv_ref[...] = jnp.zeros_like(dkv_ref)
        spread_segments(rows_ref, segk, 0 if remote else HALF, HALF)
        tok = kv_own.shape[0]
        kv_ref[:tok, :] = kv_own[...]
        kv_ref[tok:, :] = kv_oth[...]

    query = HALF + ((step + 4 * core) & (HALF - 1))
    first = first_block(seg_ref, ids_ref, step)
    if remote:
        lo, hi = first, jnp.int32(HALF - 1)
    else:
        lo, hi = jnp.maximum(first, HALF), query
    count = hi - lo + 1
    segq = rows_ref[HALF + step]

    @pl.when(count > 0)
    def _():
        stack_heads(q_ref, qs)
        flip_heads(q_ref, qt)
        stack_heads(do_ref, ds_)
        flip_heads(do_ref, dt)
        for h in range(HEADS):
            hc = slice(h * HD, (h + 1) * HD)
            prod = do_ref[:, hc].astype(jnp.float32) * o_ref[:, hc].astype(jnp.float32)
            delta[:, h * BLK:(h + 1) * BLK] = jnp.sum(prod.T, axis=0, keepdims=True)

    if remote:
        dqt[...] = jnp.zeros_like(dqt)
    else:
        dqt[...] = dq_in[0]

    def body(it, carry):
        p = lo + it
        key_start = pl.multiple_of((store_block(p, core) & (HALF - 1)) * BLK, BLK)
        k_blk = kv_ref[pl.ds(key_start, BLK), :HD]
        v_blk = kv_ref[pl.ds(key_start, BLK), HD:]
        mask = pair_mask(segk[pl.ds(key_start, BLK), :], segq, p, query)
        for h in range(HEADS):
            cols = slice(h * BLK, (h + 1) * BLK)
            s = dot(k_blk, qt[:, cols])
            w = jnp.where(mask, jnp.exp2(s * scale2 - lse_ref[0, :, cols]), 0.0)
            dp = dot(v_blk, dt[:, cols])
            dsv = w * (dp - delta[:, cols])
            pm[:, cols] = w.astype(jnp.bfloat16)
            sm[:, cols] = dsv.astype(jnp.bfloat16)
        dkv_ref[pl.ds(key_start, BLK), HD:] += dot(pm[...], ds_[...])
        dkv_ref[pl.ds(key_start, BLK), :HD] += dot(sm[...], qs[...])
        dqt[...] += dot(k_blk.T, sm[...])
        return carry

    lax.fori_loop(0, count, body, 0)
    if remote:
        dq_out[0] = dqt[...]
    else:
        for h in range(HEADS):
            cols = slice(h * BLK, (h + 1) * BLK)
            dq_out[:, h * HD:(h + 1) * HD] = (dqt[:, cols] * scale).T.astype(jnp.bfloat16)


def lanes(ref, first, count):
    return jnp.concatenate([ref[first + h] for h in range(count)], axis=1)


def project_kernel(ids_ref, a_own, a_oth, w_ref, out_ref):
    weight = lanes(w_ref, 0, 2)
    half = out_ref.shape[0] // 2

    def put(src):
        for t in (0, half):
            out_ref[t:t + half, :] = dot(src[t:t + half, :], weight).astype(jnp.bfloat16)

    @pl.when(pl.program_id(0) == 0)
    def _():
        put(a_own)

    @pl.when(pl.program_id(0) == 1)
    def _():
        put(a_oth)


def project_kv_kernel(ids_ref, a_ref, wk_ref, wv_ref, out_ref, pass_ref, mine_ref, other_ref, wide):
    @pl.when(pl.program_id(0) == 0)
    def _():
        dim = mine_ref.shape[0]
        for i, ref in enumerate((wk_ref, wv_ref)):
            wide[...] = ref[...].astype(jnp.float32)
            cols = slice(i * HD, (i + 1) * HD)
            mine_ref[:, cols] = wide[pl.ds(ids_ref[0], dim, stride=2), :].astype(jnp.bfloat16)
            other_ref[:, cols] = wide[pl.ds(1 - ids_ref[0], dim, stride=2), :].astype(jnp.bfloat16)

    out_ref[...] = dot(a_ref[...], mine_ref[...]).astype(jnp.bfloat16)
    pass_ref[...] = dot(a_ref[...], other_ref[...]).astype(jnp.bfloat16)


def expand_kernel(ids_ref, a_ref, b_ref, wa_ref, wb_ref, out_ref):
    out_ref[...] = (dot_nt(a_ref[...], lanes(wa_ref, 0, HEADS))
                    + dot_nt(b_ref[...], lanes(wb_ref, 0, HEADS))).astype(jnp.bfloat16)


def expand_kv_kernel(ids_ref, a_ref, b_ref, wa_ref, wb_ref, c_ref, d_ref, wc_ref, wd_ref, out_ref):
    out_ref[...] = (dot_nt(a_ref[...], lanes(wa_ref, 0, HEADS))
                    + dot_nt(b_ref[...], lanes(wb_ref, 0, HEADS))
                    + dot_nt(c_ref[...], wc_ref[...]) + dot_nt(d_ref[...], wd_ref[...])).astype(jnp.bfloat16)


def turn_kernel(ids_ref, a_ref, b_ref, out_ref):
    half = pl.num_programs(0) // 2

    @pl.when(pl.program_id(0) < half)
    def _():
        out_ref[...] = a_ref[...].T

    @pl.when(pl.program_id(0) >= half)
    def _():
        out_ref[...] = b_ref[...].T


def wgrad_kernel(ids_ref, a_ref, b_ref, c_ref, out_ref):
    step = pl.program_id(0)
    half = pl.num_programs(0) // 2
    tok = a_ref.shape[1] // 2

    def put(own, oth):
        val = dot(a_ref[:, :tok], own) + dot(a_ref[:, tok:], oth)
        for h in range(out_ref.shape[0]):
            out_ref[h] = val[:, h * HD:(h + 1) * HD]

    @pl.when(step < half)
    def _():
        put(b_ref[:tok, :], b_ref[tok:, :])

    @pl.when(step >= half)
    def _():
        put(c_ref[tok:, :], c_ref[:tok, :])


def whole(i, *_):
    return (0, 0)


def whole3(i, *_):
    return (0, 0, 0)


def lead(i, *_):
    return (i, 0, 0)


def params(mib, axes=1):
    return pltpu.CompilerParams(dimension_semantics=('arbitrary',) * axes, vmem_limit_bytes=mib * 1024 * 1024)


def attend(seg, ids, q, kv_far, kv_near, rows):
    tok = q.shape[0]
    keys = 2 * tok
    grid = tok // BLK
    block = pl.BlockSpec((BLK, HEADS * HD), lambda i, *_: (i, 0))
    return pl.pallas_call(
        fwd_kernel,
        grid_spec=pltpu.PrefetchScalarGridSpec(
            num_scalar_prefetch=2, grid=(grid,),
            in_specs=[block] + [pl.BlockSpec((tok // 2, 2 * HD), whole)] * 4
            + [pl.BlockSpec((keys // BLK, 1, BLK), whole3)],
            out_specs=[block, pl.BlockSpec((1, 1, WIDE), lead)],
            scratch_shapes=[pltpu.VMEM((keys, 128), jnp.int32), pltpu.VMEM((keys, 2 * HD), jnp.bfloat16),
                            pltpu.VMEM((HD, WIDE), jnp.bfloat16), pltpu.VMEM((HD, WIDE), jnp.float32),
                            pltpu.VMEM((1, WIDE), jnp.float32), pltpu.VMEM((8, WIDE), jnp.float32),
                            pltpu.VMEM((BLK, WIDE), jnp.bfloat16)]),
        out_shape=[jax.ShapeDtypeStruct((tok, HEADS * HD), jnp.bfloat16),
                   jax.ShapeDtypeStruct((grid, 1, WIDE), jnp.float32)],
        compiler_params=params(24), name='attend',
        cost_estimate=pl.CostEstimate(flops=40 * 4 * WIDE * BLK * HD, bytes_accessed=12 << 20, transcendentals=0),
    )(seg, ids, q, *kv_far, *kv_near, rows)


def attend_grad(remote, seg, ids, q, do, o, kv, rows, lse, dq_in=None):
    tok = q.shape[0]
    grid = tok // BLK
    block = pl.BlockSpec((BLK, HEADS * HD), lambda i, *_: (i, 0))
    in_specs = [block] * 3 + [pl.BlockSpec((tok // 2, 2 * HD), whole)] * 2 + [
        pl.BlockSpec(rows.shape, whole3), pl.BlockSpec((1, 1, WIDE), lead)]
    args = [seg, ids, q, do, o, *kv, rows, lse]
    dqt_spec = pl.BlockSpec((1, HD, WIDE), lead)
    kv_grad = jax.ShapeDtypeStruct((tok, 2 * HD), jnp.float32)
    kv_spec = pl.BlockSpec((tok, 2 * HD), whole)
    if remote:
        out_shape = [jax.ShapeDtypeStruct((grid, HD, WIDE), jnp.float32), kv_grad]
        out_specs = [dqt_spec, kv_spec]
    else:
        in_specs.append(dqt_spec)
        args.append(dq_in)
        out_shape = [jax.ShapeDtypeStruct((tok, HEADS * HD), jnp.bfloat16), kv_grad]
        out_specs = [block, kv_spec]
    stack = pltpu.VMEM((WIDE, HD), jnp.bfloat16)
    flip = pltpu.VMEM((HD, WIDE), jnp.bfloat16)
    tile = pltpu.VMEM((BLK, WIDE), jnp.bfloat16)
    return pl.pallas_call(
        functools.partial(bwd_kernel, remote),
        grid_spec=pltpu.PrefetchScalarGridSpec(
            num_scalar_prefetch=2, grid=(grid,), in_specs=in_specs, out_specs=out_specs,
            scratch_shapes=[pltpu.VMEM((tok, 128), jnp.int32), pltpu.VMEM((tok, 2 * HD), jnp.bfloat16),
                            stack, flip, stack, flip, pltpu.VMEM((1, WIDE), jnp.float32),
                            tile, tile, pltpu.VMEM((HD, WIDE), jnp.float32)]),
        out_shape=out_shape, compiler_params=params(28),
        name='attend_grad_remote' if remote else 'attend_grad_local',
        cost_estimate=pl.CostEstimate(flops=20 * 10 * WIDE * BLK * HD, bytes_accessed=20 << 20, transcendentals=0),
    )(*args)


def project(ids, a, b, w):
    tok, dim = a.shape
    steps = HEADS // 2
    return pl.pallas_call(
        project_kernel,
        grid_spec=pltpu.PrefetchScalarGridSpec(
            num_scalar_prefetch=1, grid=(2, steps),
            in_specs=[pl.BlockSpec((tok, dim), whole)] * 2
            + [pl.BlockSpec((2, dim, HD), lambda t, i, ids: (steps * ids[0] + i, 0, 0))],
            out_specs=pl.BlockSpec((tok, 2 * HD), lambda t, i, ids: (t, i))),
        out_shape=jax.ShapeDtypeStruct((2 * tok, HEADS * HD), jnp.bfloat16),
        compiler_params=params(20, 2),
        cost_estimate=pl.CostEstimate(flops=4 * tok * dim * HEADS * HD, bytes_accessed=12 << 20, transcendentals=0),
    )(ids, a, b, w)


def project_kv(ids, a, w_k, w_v):
    tok, dim = a.shape
    mine = jax.ShapeDtypeStruct((dim, 2 * HD), jnp.bfloat16)
    pack = pl.BlockSpec((2 * dim, HD), whole)
    return pl.pallas_call(
        project_kv_kernel,
        grid_spec=pltpu.PrefetchScalarGridSpec(
            num_scalar_prefetch=1, grid=(2,),
            in_specs=[pl.BlockSpec((tok // 2, dim), lambda i, ids: (i, 0)), pack, pack],
            out_specs=[pl.BlockSpec((tok // 2, 2 * HD), lambda i, ids: (i, 0))] * 2
            + [pl.BlockSpec((dim, 2 * HD), whole)] * 2,
            scratch_shapes=[pltpu.VMEM((2 * dim, HD), jnp.float32)]),
        out_shape=[jax.ShapeDtypeStruct((tok, 2 * HD), jnp.bfloat16)] * 2 + [mine, mine],
        compiler_params=params(60), name='project_kv',
        cost_estimate=pl.CostEstimate(flops=4 * tok * dim * HD, bytes_accessed=6 << 20, transcendentals=0),
    )(ids, a, w_k.reshape(2 * dim, HD), w_v.reshape(2 * dim, HD))


def expand(ids, a, b, w, extra=()):
    tok, width = a.shape[0] // 2, a.shape[1]
    dim = w.shape[1]
    cols = 512

    def first(i, ids):
        return (0, 0)

    def second(i, ids):
        return (1, 0)

    specs = [pl.BlockSpec((tok, width), first), pl.BlockSpec((tok, width), second),
             pl.BlockSpec((HEADS, cols, HD), lambda i, ids: (ids[0], i, 0)),
             pl.BlockSpec((HEADS, cols, HD), lambda i, ids: (1 - ids[0], i, 0))]
    args = [a, b, w, w]
    if extra:
        specs += [pl.BlockSpec((tok, 2 * HD), first), pl.BlockSpec((tok, 2 * HD), second)]
        specs += [pl.BlockSpec((cols, 2 * HD), lambda i, ids: (i, 0))] * 2
        args += extra
    return pl.pallas_call(
        expand_kv_kernel if extra else expand_kernel,
        grid_spec=pltpu.PrefetchScalarGridSpec(
            num_scalar_prefetch=1, grid=(dim // cols,), in_specs=specs,
            out_specs=pl.BlockSpec((tok, cols), lambda i, ids: (0, i))),
        out_shape=jax.ShapeDtypeStruct((tok, dim), jnp.bfloat16),
        compiler_params=params(20), name='grad_x' if extra else 'out_y',
        cost_estimate=pl.CostEstimate(flops=4 * tok * dim * width, bytes_accessed=14 << 20, transcendentals=0),
    )(ids, *args)


def turn(where, a, b):
    tok, dim = a.shape
    rows = dim // 4
    part = tok // 2
    return pl.pallas_call(
        turn_kernel,
        grid_spec=pltpu.PrefetchScalarGridSpec(
            num_scalar_prefetch=1, grid=(4,),
            in_specs=[pl.BlockSpec((part, rows), lambda i, ids: (jnp.minimum(i, 1), ids[0])),
                      pl.BlockSpec((part, rows), lambda i, ids: (jnp.maximum(i - 2, 0), ids[0]))],
            out_specs=pl.BlockSpec((rows, part), lambda i, ids: (0, i))),
        out_shape=jax.ShapeDtypeStruct((rows, 2 * tok), jnp.bfloat16),
        compiler_params=params(12),
        cost_estimate=pl.CostEstimate(flops=2 << 30, bytes_accessed=4 * rows * tok * 2, transcendentals=0),
    )(where.reshape(1).astype(jnp.int32), a, b)


def wgrad(core, a, b, c):
    rows, tok = a.shape
    width = b.shape[1]
    step = 256
    half = width // step
    heads = step // HD
    return pl.pallas_call(
        wgrad_kernel,
        grid_spec=pltpu.PrefetchScalarGridSpec(
            num_scalar_prefetch=1, grid=(2 * half,),
            in_specs=[pl.BlockSpec((rows, tok), whole),
                      pl.BlockSpec((tok, step), lambda i, ids: (0, jnp.minimum(i, half - 1))),
                      pl.BlockSpec((tok, step), lambda i, ids: (0, jnp.maximum(i - half, 0)))],
            out_specs=pl.BlockSpec((heads, rows, HD), lambda i, ids: (lax.rem(i + half * ids[0], 2 * half), 0, 0))),
        out_shape=jax.ShapeDtypeStruct((2 * width // HD, rows, HD), jnp.float32),
        compiler_params=params(16),
        cost_estimate=pl.CostEstimate(flops=4 * tok * rows * width, bytes_accessed=10 << 20, transcendentals=0),
    )(core.reshape(1).astype(jnp.int32), a, b, c)


def after(value, *others):
    return lax.optimization_barrier((value, *others))[0]


def solution(mesh):
    row_spec = P(('dp', 'cp'), None)
    tok_spec = P(('dp', 'cp'))
    weight_spec = P(None, None, None)
    grad_spec = P(('dp', 'cp'), None, None)
    core_pairs = [(0, 1), (1, 0), (2, 3), (3, 2)]
    chip_pairs = [(0, 2), (2, 0), (1, 3), (3, 1)]
    up_pairs = [(0, 2), (1, 3)]
    up_cross = [(0, 3), (1, 2)]
    down_pairs = [(2, 0), (3, 1)]

    def send(a, pairs):
        return lax.ppermute(a, 'cp', pairs)

    def layer(x, seg, w_q, w_k, w_v, w_o, dy):
        _, dim = x.shape
        rows = dim // 4
        index = lax.axis_index('cp')
        core = index % 2
        chip = index // 2
        near_rows = index
        far_rows = 2 * (1 - chip) + core
        ids = jnp.stack([core, chip]).astype(jnp.int32)
        w_q = jnp.transpose(w_q, (1, 0, 2))
        w_o = jnp.transpose(w_o, (1, 0, 2))

        x_o = send(x, core_pairs)
        kv_own, kv_pass, wkv_c, wkv_p = project_kv(ids, x, w_k, w_v)
        kv_far0 = send(kv_own, up_pairs)
        kv_far1 = send(kv_pass, up_cross)
        kv_oth = send(kv_pass, core_pairs)
        seg_o = send(after(seg, kv_own), core_pairs)
        dy_o = send(after(dy, kv_own), core_pairs)
        seg_far0 = send(after(seg, kv_own), up_pairs)
        seg_far1 = send(after(seg, kv_own), up_cross)
        seg_all = jnp.concatenate([seg_far0, seg_far1, seg, seg_o])
        seg_rows = seg_all.reshape(-1, 1, BLK)
        kv_far, kv_near = (kv_far0, kv_far1), (kv_own, kv_oth)
        q = project(ids, after(x, kv_own), x_o, w_q)
        do = project(ids, after(dy, kv_own), dy_o, w_o)
        dy_far = turn(far_rows, dy, dy_o)
        x_far = turn(far_rows, x, x_o)

        o, lse = attend(seg_all, ids, q, kv_far, kv_near, seg_rows)
        o_p = send(o, core_pairs)
        dwo_far = wgrad(core, dy_far, o, o_p)
        dwo_in = send(dwo_far, chip_pairs)

        lse = after(lse, dwo_far)
        dq_part, dkv_far = attend_grad(True, seg_all, ids, q, do, o, kv_far, seg_rows, lse)
        dkv_in = send(dkv_far, down_pairs)
        dq, dkv_near = attend_grad(False, seg_all, ids, q, do, o, kv_near, seg_rows, lse, dq_part)
        dq_p = send(dq, core_pairs)
        dwq_far = wgrad(core, x_far, dq, dq_p)
        dwq_in = send(dwq_far, chip_pairs)

        y = expand(ids, after(o, dwq_far), o_p, w_o)
        x_near = turn(near_rows, after(x, dwq_far), x_o)
        dy_near = turn(near_rows, after(dy, dwq_far), dy_o)
        dwo_near = wgrad(core, dy_near, o, o_p)
        dwq_near = wgrad(core, x_near, dq, dq_p)

        dkv = dkv_near + dkv_in
        dkv = jnp.concatenate([dkv[:, :HD] * HD ** -0.5, dkv[:, HD:]], axis=1).astype(jnp.bfloat16)
        dkv_p = send(dkv, core_pairs)
        dwkv_far = wgrad(core, x_far, dkv, dkv_p)
        dwkv_in = send(dwkv_far, chip_pairs)
        dwkv_near = wgrad(core, x_near, after(dkv, dwkv_far), dkv_p)
        dx = expand(ids, after(dq, dwkv_far), dq_p, w_q, (dkv, dkv_p, wkv_c, wkv_p))

        dw_q = jnp.transpose(dwq_near + dwq_in, (1, 0, 2))
        dw_o = jnp.transpose(dwo_near + dwo_in, (1, 0, 2))
        dw_kv = jnp.transpose(dwkv_near + dwkv_in, (1, 0, 2)).reshape(rows, 2, 2, HD)
        return y, dx, dw_q, dw_kv[:, :, 0], dw_kv[:, :, 1], dw_o

    return jax.shard_map(layer, mesh=mesh,
                         in_specs=(row_spec, tok_spec, weight_spec, weight_spec, weight_spec, weight_spec, row_spec),
                         out_specs=(row_spec, row_spec, grad_spec, grad_spec, grad_spec, grad_spec),
                         check_vma=False)
```

time: 332 us -> 328 us (0.988)
  waiting for transfers between devices: 81.1 us -> 91.4 us
  local copies, waits for them, and re-layouts: 16.7 us -> 9.78 us
    pallas_call x0 -> x4, Pallas kernels: none -> 10.9 us  [turn(): pl.pallas_call(turn_kernel, grid_spec=pltpu.PrefetchScalarGridSpec(num_sc...]
    ppermute x16 -> x15, waiting for transfers between devices: 81.1 us -> 91.4 us  [send(): return lax.ppermute(a, 'cp', pairs)]
    pallas_call x2, Pallas kernels: 58.8 us -> 51.1 us  [attend_grad(): pl.pallas_call(functools.partial(bwd_kernel, remote), grid_spec=pltpu.Pre...]
    unnamed x72 -> x51, local copies, waits for them, and re-layouts: 15.1 us -> 8.17 us
    pallas_call x6, Pallas kernels: 28.7 us -> 22.4 us  [wgrad(): pl.pallas_call(wgrad_kernel, grid_spec=pltpu.PrefetchScalarGridSpec(num_s...]
    pallas_call x1, Pallas kernels: 2.2 us -> 6.2 us  [project_kv(): pl.pallas_call(project_kv_kernel, grid_spec=pltpu.PrefetchScalarGridSpec(...]
    ppermute x16 -> x15, starting transfers between devices: 14.3 us -> 15.1 us  [send(): return lax.ppermute(a, 'cp', pairs)]
    pallas_call x4 -> x2, Pallas kernels: 18.6 us -> 17.8 us  [project(): pl.pallas_call(project_kernel, grid_spec=pltpu.PrefetchScalarGridSpec(num...]
  transfers between devices with their start and end apart: 16 -> 15, of which waited for: 6 -> 5; matrix products, arithmetic and copies ran while one was open for 3% -> 1% of each run, Pallas kernels for 57% -> 60%
where the time goes in v2:
time: 328 us; the launch traced here: 327 us
  Pallas kernels  206 us (63%)
  waiting for transfers between devices  91.4 us (28%)
  starting transfers between devices  15.1 us (5%)
  local copies, waits for them, and re-layouts  9.78 us (3%)
  other arithmetic  4.44 us (1%)
    ppermute x15, waiting for transfers between devices, send(): return lax.ppermute(a, 'cp', pairs)  91.4 us
    pallas_call x1, Pallas kernels, attend(): pl.pallas_call(fwd_kernel, grid_spec=pltpu.PrefetchScalarGridSpec(num_sca...  79.5 us
    pallas_call x2, Pallas kernels, attend_grad(): pl.pallas_call(functools.partial(bwd_kernel, remote), grid_spec=pltpu.Pre...  51.1 us
    pallas_call x6, Pallas kernels, wgrad(): pl.pallas_call(wgrad_kernel, grid_spec=pltpu.PrefetchScalarGridSpec(num_s...  22.4 us
    pallas_call x2, Pallas kernels, project(): pl.pallas_call(project_kernel, grid_spec=pltpu.PrefetchScalarGridSpec(num...  17.8 us
    pallas_call x2, Pallas kernels, expand(): pl.pallas_call(expand_kv_kernel if extra else expand_kernel, grid_spec=pl...  17.7 us
    ppermute x15, starting transfers between devices, send(): return lax.ppermute(a, 'cp', pairs)  15.1 us
    pallas_call x4, Pallas kernels, turn(): pl.pallas_call(turn_kernel, grid_spec=pltpu.PrefetchScalarGridSpec(num_sc...  10.9 us
  transfers between devices with their start and end apart: 15, of which 5 were waited for; matrix products, arithmetic and copies ran while one was open for 1% of the time, Pallas kernels for 60%

profile of v2, /device:TPU:0, one launch (start us, length us, event | category | flops | bytes accessed | tf_op | source)
XLA Modules:
  0.0 327.4 jit_solution(14196208323253809979)
XLA Ops:
  2.1 6.2 %project_kv.1 = (bf16[1024,256]{1,0:T(8,128)(2,1)}, bf16[1024,256]{1,0:T(8,128)(2,1)}, bf16[1536,256]{1,0:T(8,128)(2,1)}, bf16[1536,256]{1,0:T(8,128)(2,1)}) custom-call(s32[2]{0:T(128)} %pad_add_fusion.1.ids_ref.refs_1_, bf16[1024,1536]{1,0:T(8,128)(2,1)} %a_ref.6, bf16[3072,128]{1,0:T(8,128)(2,1)} %bitcast.34, bf16[3072,128]{1,0:T(8,128)(2,1)} %bitcast.35), custom_call_target="tpu_custom_call" | custom-call | flops 805306368 | bytes 6291456 | tf_op jit(solution)/shard_map/project_kv/pallas_call | solution.py:420
  8.3 4.4 %collective-permute-start = (s32[1024]{0:T(1024)S(1)}, s32[1024]{0:T(1024)S(1)}, u32[]{:S(2)}, u32[]{:S(2)}) collective-permute-start(s32[1024]{0:T(1024)S(1)} %copy-done.19), channel_id=1, source_target_pairs={{0,2},{1,3},{4,6},{5,7}} | collective-permute-start | bytes 12296 | tf_op jit(solution)/shard_map/ppermute | solution.py:517
  18.5 2.3 copy-done.1
  20.8 8.9 %shard_map.118.q_ref.refs_2_ = bf16[2048,768]{1,0:T(8,128)(2,1)S(1)} custom-call(s32[2]{0:T(128)S(1)} %copy-done.6, bf16[1024,1536]{1,0:T(8,128)(2,1)S(1)} %copy-done.2, bf16[1024,1536]{1,0:T(8,128)(2,1)} %collective-permute-done.3.a_oth.b_ref, bf16[12,1536,128]{2,1,0:T(8,128)(2,1)S(1)} %bitcast.28), custom_call_target="tpu_custom_call" | custom-call | flops 4831838208 | bytes 12582912 | tf_op jit(solution)/shard_map/pallas_call | solution.py:403
  29.8 9.3 %collective-permute-done.5.kv_far1.refs_6_ = bf16[1024,256]{1,0:T(8,128)(2,1)S(1)} collective-permute-done((bf16[1024,256]{1,0:T(8,128)(2,1)}, bf16[1024,256]{1,0:T(8,128)(2,1)S(1)}, u32[]{:S(2)}, u32[]{:S(2)}) %collective-permute-start.5) | collective-permute-done | bytes 524320 | tf_op jit(solution)/shard_map/ppermute | solution.py:517
  39.1 79.5 %attend.1 = (bf16[2048,768]{1,0:T(8,128)(2,1)S(1)}, f32[8,1,1536]{2,1,0:T(1,128)S(1)}) custom-call(s32[4096]{0:T(1024)S(1)} %constant_dynamic-update-slice_fusion.seg_ref.refs_0_, s32[2]{0:T(128)S(1)} %copy-done.6, bf16[2048,768]{1,0:T(8,128)(2,1)S(1)} %shard_map.118.q_ref.refs_2_, bf16[1024,256]{1,0:T(8,128)(2,1)S(1)} %collective-permute-done.4.kv_far0.refs_5_, ...), custom_call_target="tpu_custom_call" | custom-call | flops 8053063680 | bytes 12582912 | tf_op jit(solution)/shard_map/attend/pallas_call | solution.py:348
  120.6 2.8 shard_map.121.a_ref
  123.4 2.3 copy-done
  125.7 8.9 %shard_map.120.refs_3_ = bf16[2048,768]{1,0:T(8,128)(2,1)S(1)} custom-call(s32[2]{0:T(128)S(1)} %copy-done.6, bf16[1024,1536]{1,0:T(8,128)(2,1)S(1)} %copy-done.8, bf16[1024,1536]{1,0:T(8,128)(2,1)} %collective-permute-done.7.a_oth.b_ref, bf16[12,1536,128]{2,1,0:T(8,128)(2,1)S(1)} %bitcast.23), custom_call_target="tpu_custom_call" | custom-call | flops 4831838208 | bytes 12582912 | tf_op jit(solution)/shard_map/pallas_call | solution.py:403
  134.7 5.9 %shard_map.122 = f32[12,384,128]{2,1,0:T(8,128)S(1)} custom-call(s32[1]{0:T(128)} %bitcast.ids_ref, bf16[384,2048]{1,0:T(8,128)(2,1)S(1)} %shard_map.121.a_ref, bf16[2048,768]{1,0:T(8,128)(2,1)S(1)} %get-tuple-element.35.b_ref.refs_4_.a_ref, bf16[2048,768]{1,0:T(8,128)(2,1)} %collective-permute-done.8.c_ref.b_ref), custom_call_target="tpu_custom_call" | custom-call | flops 2415919104 | bytes 10485760 | tf_op jit(solution)/shard_map/pallas_call | solution.py:487
  140.7 2.5 attend_grad_remote.1
  144.7 48.6 %attend_grad_local.1 = (bf16[2048,768]{1,0:T(8,128)(2,1)S(1)}, f32[2048,256]{1,0:T(8,128)S(1)}) custom-call(s32[4096]{0:T(1024)S(1)} %constant_dynamic-update-slice_fusion.seg_ref.refs_0_, s32[2]{0:T(128)S(1)} %copy-done.6, bf16[2048,768]{1,0:T(8,128)(2,1)S(1)} %copy-done.18, bf16[2048,768]{1,0:T(8,128)(2,1)S(1)} %shard_map.120.refs_3_, ...), custom_call_target="tpu_custom_call" | custom-call | flops 10066329600 | bytes 20971520 | tf_op jit(solution)/shard_map/attend_grad_local/pallas_call | solution.py:387
  193.8 10.4 %collective-permute-done.10 = f32[2048,256]{1,0:T(8,128)S(1)} collective-permute-done((f32[2048,256]{1,0:T(8,128)S(1)}, f32[2048,256]{1,0:T(8,128)S(1)}, u32[]{:S(2)}, u32[]{:S(2)}) %collective-permute-start.10) | collective-permute-done | bytes 2097184 | tf_op jit(solution)/shard_map/ppermute | solution.py:517
  206.3 2.7 shard_map.119.a_ref
  210.7 4.1 %shard_map.123 = f32[12,384,128]{2,1,0:T(8,128)S(1)} custom-call(s32[1]{0:T(128)} %bitcast.ids_ref, bf16[384,2048]{1,0:T(8,128)(2,1)S(1)} %shard_map.119.a_ref, bf16[2048,768]{1,0:T(8,128)(2,1)S(1)} %get-tuple-element.38.b_ref.a_ref, bf16[2048,768]{1,0:T(8,128)(2,1)S(1)} %collective-permute-done.9.c_ref.b_ref), custom_call_target="tpu_custom_call" | custom-call | flops 2415919104 | bytes 10485760 | tf_op jit(solution)/shard_map/pallas_call | solution.py:487
  216.4 2.7 shard_map.128.a_ref
  219.0 2.7 shard_map.125.a_ref
  223.0 4.1 %shard_map.126 = f32[12,384,128]{2,1,0:T(8,128)S(1)} custom-call(s32[1]{0:T(128)} %bitcast.ids_ref, bf16[384,2048]{1,0:T(8,128)(2,1)S(1)} %shard_map.125.a_ref, bf16[2048,768]{1,0:T(8,128)(2,1)S(1)} %get-tuple-element.38.b_ref.a_ref, bf16[2048,768]{1,0:T(8,128)(2,1)S(1)} %collective-permute-done.9.c_ref.b_ref), custom_call_target="tpu_custom_call" | custom-call | flops 2415919104 | bytes 10485760 | tf_op jit(solution)/shard_map/pallas_call | solution.py:487
  227.1 5.9 %shard_map.129 = f32[12,384,128]{2,1,0:T(8,128)S(1)} custom-call(s32[1]{0:T(128)} %bitcast.ids_ref, bf16[384,2048]{1,0:T(8,128)(2,1)S(1)} %shard_map.128.a_ref, bf16[2048,768]{1,0:T(8,128)(2,1)S(1)} %get-tuple-element.35.b_ref.refs_4_.a_ref, bf16[2048,768]{1,0:T(8,128)(2,1)} %collective-permute-done.8.c_ref.b_ref), custom_call_target="tpu_custom_call" | custom-call | flops 2415919104 | bytes 10485760 | tf_op jit(solution)/shard_map/pallas_call | solution.py:487
  233.1 8.7 %out_y.1 = bf16[1024,1536]{1,0:T(8,128)(2,1)} custom-call(s32[2]{0:T(128)S(1)} %copy-done.6, bf16[2048,768]{1,0:T(8,128)(2,1)S(1)} %get-tuple-element.35.b_ref.refs_4_.a_ref, bf16[2048,768]{1,0:T(8,128)(2,1)} %collective-permute-done.8.c_ref.b_ref, bf16[12,1536,128]{2,1,0:T(8,128)(2,1)S(1)} %bitcast.26, bf16[12,1536,128]{2,1,0:T(8,128)(2,1)S(1)} %bitcast.27), custom_call_target="tpu_custom_call" | custom-call | flops 4831838208 | bytes 14680064 | tf_op jit(solution)/shard_map/out_y/pallas_call | solution.py:453
  241.8 17.1 %collective-permute-done.14 = f32[12,384,128]{2,1,0:T(8,128)S(1)} collective-permute-done((f32[12,384,128]{2,1,0:T(8,128)S(1)}, f32[12,384,128]{2,1,0:T(8,128)S(1)}, u32[]{:S(2)}, u32[]{:S(2)}) %collective-permute-start.14) | collective-permute-done | bytes 2359328 | tf_op jit(solution)/shard_map/ppermute | solution.py:517
  260.5 9.0 %grad_x.1 = bf16[1024,1536]{1,0:T(8,128)(2,1)} custom-call(s32[2]{0:T(128)S(1)} %copy-done.6, bf16[2048,768]{1,0:T(8,128)(2,1)S(1)} %get-tuple-element.38.b_ref.a_ref, bf16[2048,768]{1,0:T(8,128)(2,1)S(1)} %collective-permute-done.9.c_ref.b_ref, bf16[12,1536,128]{2,1,0:T(8,128)(2,1)S(1)} %bitcast.31, bf16[12,1536,128]{2,1,0:T(8,128)(2,1)S(1)} %bitcast.32, ...), custom_call_target="tpu_custom_call" | custom-call | flops 4831838208 | bytes 14680064 | tf_op jit(solution)/shard_map/grad_x/pallas_call | solution.py:453
  269.6 6.2 %collective-permute-done.13 = f32[4,384,128]{2,1,0:T(8,128)S(1)} collective-permute-done((f32[4,384,128]{2,1,0:T(8,128)S(1)}, f32[4,384,128]{2,1,0:T(8,128)S(1)}, u32[]{:S(2)}, u32[]{:S(2)}) %collective-permute-start.13) | collective-permute-done | bytes 786464 | tf_op jit(solution)/shard_map/ppermute | solution.py:517
  277.4 48.4 %collective-permute-done.12 = f32[12,384,128]{2,1,0:T(8,128)S(1)} collective-permute-done((f32[12,384,128]{2,1,0:T(8,128)S(1)}, f32[12,384,128]{2,1,0:T(8,128)S(1)}, u32[]{:S(2)}, u32[]{:S(2)}) %collective-permute-start.12) | collective-permute-done | bytes 2359328 | tf_op jit(solution)/shard_map/ppermute | solution.py:517
  (89 shorter events, 22.7 us)
Async XLA Ops:
  0.6 17.8 %collective-permute-start.3 = (bf16[1024,1536]{1,0:T(8,128)(2,1)}, bf16[1024,1536]{1,0:T(8,128)(2,1)}, u32[]{:S(2)}, u32[]{:S(2)}) collective-permute-start(bf16[1024,1536]{1,0:T(8,128)(2,1)} %a_ref.6), channel_id=1, source_target_pairs={{0,1},{1,0},{2,3},{3,2},{4,5},{5,4},{6,7},{7,6}} | collective-permute-start | bytes 9437192 | tf_op jit(solution)/shard_map/ppermute | solution.py:517
  8.3 7.5 %collective-permute-start = (s32[1024]{0:T(1024)S(1)}, s32[1024]{0:T(1024)S(1)}, u32[]{:S(2)}, u32[]{:S(2)}) collective-permute-start(s32[1024]{0:T(1024)S(1)} %copy-done.19), channel_id=1, source_target_pairs={{0,2},{1,3},{4,6},{5,7}} | collective-permute-start | bytes 12296 | tf_op jit(solution)/shard_map/ppermute | solution.py:517
  12.7 4.5 %collective-permute-start.1 = (s32[1024]{0:T(1024)S(1)}, s32[1024]{0:T(1024)S(1)}, u32[]{:S(2)}, u32[]{:S(2)}) collective-permute-start(s32[1024]{0:T(1024)S(1)} %copy-done.19), channel_id=1, source_target_pairs={{0,3},{1,2},{4,7},{5,6}} | collective-permute-start | bytes 12296 | tf_op jit(solution)/shard_map/ppermute | solution.py:517
  14.1 4.3 %collective-permute-start.2 = (s32[1024]{0:T(1024)S(1)}, s32[1024]{0:T(1024)S(1)}, u32[]{:S(2)}, u32[]{:S(2)}) collective-permute-start(s32[1024]{0:T(1024)S(1)} %copy-done.19), channel_id=1, source_target_pairs={{0,1},{1,0},{2,3},{3,2},{4,5},{5,4},{6,7},{7,6}} | collective-permute-start | bytes 12296 | tf_op jit(solution)/shard_map/ppermute | solution.py:517
  14.2 15.6 %collective-permute-start.4 = (bf16[1024,256]{1,0:T(8,128)(2,1)}, bf16[1024,256]{1,0:T(8,128)(2,1)S(1)}, u32[]{:S(2)}, u32[]{:S(2)}) collective-permute-start(bf16[1024,256]{1,0:T(8,128)(2,1)} %get-tuple-element.25.kv_own.refs_5_), channel_id=1, source_target_pairs={{0,2},{1,3},{4,6},{5,7}} | collective-permute-start | bytes 1572872 | tf_op jit(solution)/shard_map/ppermute | solution.py:517
  15.8 23.2 %collective-permute-start.5 = (bf16[1024,256]{1,0:T(8,128)(2,1)}, bf16[1024,256]{1,0:T(8,128)(2,1)S(1)}, u32[]{:S(2)}, u32[]{:S(2)}) collective-permute-start(bf16[1024,256]{1,0:T(8,128)(2,1)} %get-tuple-element.28), channel_id=1, source_target_pairs={{0,3},{1,2},{4,7},{5,6}} | collective-permute-start | bytes 1572872 | tf_op jit(solution)/shard_map/ppermute | solution.py:517
  17.2 21.9 %collective-permute-start.6 = (bf16[1024,256]{1,0:T(8,128)(2,1)}, bf16[1024,256]{1,0:T(8,128)(2,1)S(1)}, u32[]{:S(2)}, u32[]{:S(2)}) collective-permute-start(bf16[1024,256]{1,0:T(8,128)(2,1)} %get-tuple-element.28), channel_id=1, source_target_pairs={{0,1},{1,0},{2,3},{3,2},{4,5},{5,4},{6,7},{7,6}} | collective-permute-start | bytes 1572872 | tf_op jit(solution)/shard_map/ppermute | solution.py:517
  18.4 100.3 %collective-permute-start.7 = (bf16[1024,1536]{1,0:T(8,128)(2,1)}, bf16[1024,1536]{1,0:T(8,128)(2,1)}, u32[]{:S(2)}, u32[]{:S(2)}) collective-permute-start(bf16[1024,1536]{1,0:T(8,128)(2,1)} %a_ref.7), channel_id=1, source_target_pairs={{0,1},{1,0},{2,3},{3,2},{4,5},{5,4},{6,7},{7,6}} | collective-permute-start | bytes 9437192 | tf_op jit(solution)/shard_map/ppermute | solution.py:517
  20.8 18.2 %copy-start.9 = (bf16[1024,256]{1,0:T(8,128)(2,1)S(1)}, bf16[1024,256]{1,0:T(8,128)(2,1)}, u32[]{:S(2)}) copy-start(bf16[1024,256]{1,0:T(8,128)(2,1)} %get-tuple-element.25.kv_own.refs_5_) | copy-start | bytes 1572868
  29.7 88.8 %copy-start.17 = (bf16[2048,768]{1,0:T(8,128)(2,1)}, bf16[2048,768]{1,0:T(8,128)(2,1)S(1)}, u32[]{:S(2)}) copy-start(bf16[2048,768]{1,0:T(8,128)(2,1)S(1)} %shard_map.118.q_ref.refs_2_) | copy-start | bytes 9437188
  29.8 88.8 %copy-start.11 = (bf16[1024,256]{1,0:T(8,128)(2,1)}, bf16[1024,256]{1,0:T(8,128)(2,1)S(1)}, u32[]{:S(2)}) copy-start(bf16[1024,256]{1,0:T(8,128)(2,1)S(1)} %collective-permute-done.4.kv_far0.refs_5_) | copy-start | bytes 1572868
  39.0 79.5 %copy-start.15 = (bf16[1024,256]{1,0:T(8,128)(2,1)}, bf16[1024,256]{1,0:T(8,128)(2,1)S(1)}, u32[]{:S(2)}) copy-start(bf16[1024,256]{1,0:T(8,128)(2,1)S(1)} %collective-permute-done.5.kv_far1.refs_6_) | copy-start | bytes 1572868
  39.1 79.5 %copy-start.13 = (bf16[1024,256]{1,0:T(8,128)(2,1)}, bf16[1024,256]{1,0:T(8,128)(2,1)S(1)}, u32[]{:S(2)}) copy-start(bf16[1024,256]{1,0:T(8,128)(2,1)S(1)} %collective-permute-done.6.kv_oth.refs_6_) | copy-start | bytes 1572868
  118.6 16.1 %collective-permute-start.8 = (bf16[2048,768]{1,0:T(8,128)(2,1)S(1)}, bf16[2048,768]{1,0:T(8,128)(2,1)}, u32[]{:S(2)}, u32[]{:S(2)}) collective-permute-start(bf16[2048,768]{1,0:T(8,128)(2,1)S(1)} %get-tuple-element.35.b_ref.refs_4_.a_ref), channel_id=1, source_target_pairs={{0,1},{1,0},{2,3},{3,2},{4,5},{5,4},{6,7},{7,6}} | collective-permute-start | bytes 9437192 | tf_op jit(solution)/shard_map/ppermute | solution.py:517
  143.2 60.9 %collective-permute-start.10 = (f32[2048,256]{1,0:T(8,128)S(1)}, f32[2048,256]{1,0:T(8,128)S(1)}, u32[]{:S(2)}, u32[]{:S(2)}) collective-permute-start(f32[2048,256]{1,0:T(8,128)S(1)} %get-tuple-element.37), channel_id=1, source_target_pairs={{2,0},{3,1},{6,4},{7,5}} | collective-permute-start | bytes 6291464 | tf_op jit(solution)/shard_map/ppermute | solution.py:517
  193.3 17.5 %collective-permute-start.9 = (bf16[2048,768]{1,0:T(8,128)(2,1)S(1)}, bf16[2048,768]{1,0:T(8,128)(2,1)S(1)}, u32[]{:S(2)}, u32[]{:S(2)}) collective-permute-start(bf16[2048,768]{1,0:T(8,128)(2,1)S(1)} %get-tuple-element.38.b_ref.a_ref), channel_id=1, source_target_pairs={{0,1},{1,0},{2,3},{3,2},{4,5},{5,4},{6,7},{7,6}} | collective-permute-start | bytes 9437192 | tf_op jit(solution)/shard_map/ppermute | solution.py:517
  204.7 4.3 %collective-permute-start.11 = (bf16[2048,256]{1,0:T(8,128)(2,1)S(1)}, bf16[2048,256]{1,0:T(8,128)(2,1)S(1)}, u32[]{:S(2)}, u32[]{:S(2)}) collective-permute-start(bf16[2048,256]{1,0:T(8,128)(2,1)S(1)} %pad_maximum_fusion.b_ref.c_ref), channel_id=1, source_target_pairs={{0,1},{1,0},{2,3},{3,2},{4,5},{5,4},{6,7},{7,6}} | collective-permute-start | bytes 3145736 | tf_op jit(solution)/shard_map/ppermute | solution.py:517
  204.7 54.1 %collective-permute-start.14 = (f32[12,384,128]{2,1,0:T(8,128)S(1)}, f32[12,384,128]{2,1,0:T(8,128)S(1)}, u32[]{:S(2)}, u32[]{:S(2)}) collective-permute-start(f32[12,384,128]{2,1,0:T(8,128)S(1)} %shard_map.122), channel_id=1, source_target_pairs={{0,2},{2,0},{1,3},{3,1},{4,6},{6,4},{5,7},{7,5}} | collective-permute-start | bytes 7077896 | tf_op jit(solution)/shard_map/ppermute | solution.py:517
  210.2 65.5 %collective-permute-start.13 = (f32[4,384,128]{2,1,0:T(8,128)S(1)}, f32[4,384,128]{2,1,0:T(8,128)S(1)}, u32[]{:S(2)}, u32[]{:S(2)}) collective-permute-start(f32[4,384,128]{2,1,0:T(8,128)S(1)} %shard_map.124), channel_id=1, source_target_pairs={{0,2},{2,0},{1,3},{3,1},{4,6},{6,4},{5,7},{7,5}} | collective-permute-start | bytes 2359304 | tf_op jit(solution)/shard_map/ppermute | solution.py:517
  214.8 111.0 %collective-permute-start.12 = (f32[12,384,128]{2,1,0:T(8,128)S(1)}, f32[12,384,128]{2,1,0:T(8,128)S(1)}, u32[]{:S(2)}, u32[]{:S(2)}) collective-permute-start(f32[12,384,128]{2,1,0:T(8,128)S(1)} %shard_map.123), channel_id=1, source_target_pairs={{0,2},{2,0},{1,3},{3,1},{4,6},{6,4},{5,7},{7,5}} | collective-permute-start | bytes 7077896 | tf_op jit(solution)/shard_map/ppermute | solution.py:517
  227.1 33.4 %slice-start.2 = ((s8[4718592]{0:T(1024)(128)(4,1)}), s8[4194304]{0:T(1024)(128)(4,1)S(1)}, s32[]{:S(2)}) async-start(s8[4718592]{0:T(1024)(128)(4,1)} %bitcast.29), calls=%async_computation.2 | async-start | bytes 8388608
  233.1 27.5 %slice-start.3 = ((s8[4718592]{0:T(1024)(128)(4,1)}), s8[524288]{0:T(1024)(128)(4,1)S(1)}, s32[]{:S(2)}) async-start(s8[4718592]{0:T(1024)(128)(4,1)} %bitcast.29), calls=%async_computation.3 | async-start | bytes 1048576
  241.8 18.8 %copy-start.4 = (bf16[1536,256]{1,0:T(8,128)(2,1)S(1)}, bf16[1536,256]{1,0:T(8,128)(2,1)}, u32[]{:S(2)}) copy-start(bf16[1536,256]{1,0:T(8,128)(2,1)} %get-tuple-element.39.wc_ref) | copy-start | bytes 2359300
  241.8 18.8 %copy-start.5 = (bf16[1536,256]{1,0:T(8,128)(2,1)S(1)}, bf16[1536,256]{1,0:T(8,128)(2,1)}, u32[]{:S(2)}) copy-start(bf16[1536,256]{1,0:T(8,128)(2,1)} %get-tuple-element.40.wd_ref) | copy-start | bytes 2359300
  (15 other events, 92.1 us)

commit v3 on v2

--- a/solution.py
+++ b/solution.py
@@ -252,12 +252,13 @@
 
 
 def project_kernel(ids_ref, a_own, a_oth, w_ref, out_ref):
-    weight = lanes(w_ref, 0, 2)
     half = out_ref.shape[0] // 2
 
     def put(src):
-        for t in (0, half):
-            out_ref[t:t + half, :] = dot(src[t:t + half, :], weight).astype(jnp.bfloat16)
+        for n in range(0, HEADS, 2):
+            weight = jnp.concatenate([w_ref[n], w_ref[n + 1]], axis=1)
+            for t in (0, half):
+                out_ref[t:t + half, n * HD:(n + 2) * HD] = dot(src[t:t + half, :], weight).astype(jnp.bfloat16)
 
     @pl.when(pl.program_id(0) == 0)
     def _():
@@ -305,6 +306,14 @@
         out_ref[...] = b_ref[...].T
 
 
+def wgrad_one_kernel(partner, a_ref, b_ref, out_ref):
+    tok = a_ref.shape[1] // 2
+    first, second = (b_ref[tok:, :], b_ref[:tok, :]) if partner else (b_ref[:tok, :], b_ref[tok:, :])
+    val = dot(a_ref[:, :tok], first) + dot(a_ref[:, tok:], second)
+    for h in range(out_ref.shape[0]):
+        out_ref[h] = val[:, h * HD:(h + 1) * HD]
+
+
 def wgrad_kernel(ids_ref, a_ref, b_ref, c_ref, out_ref):
     step = pl.program_id(0)
     half = pl.num_programs(0) // 2
@@ -336,8 +345,8 @@
     return (i, 0, 0)
 
 
-def params(mib, axes=1):
-    return pltpu.CompilerParams(dimension_semantics=('arbitrary',) * axes, vmem_limit_bytes=mib * 1024 * 1024)
+def params(mib):
+    return pltpu.CompilerParams(dimension_semantics=('arbitrary',), vmem_limit_bytes=mib * 1024 * 1024)
 
 
 def attend(seg, ids, q, kv_far, kv_near, rows):
@@ -399,16 +408,15 @@
 
 def project(ids, a, b, w):
     tok, dim = a.shape
-    steps = HEADS // 2
     return pl.pallas_call(
         project_kernel,
         grid_spec=pltpu.PrefetchScalarGridSpec(
-            num_scalar_prefetch=1, grid=(2, steps),
+            num_scalar_prefetch=1, grid=(2,),
             in_specs=[pl.BlockSpec((tok, dim), whole)] * 2
-            + [pl.BlockSpec((2, dim, HD), lambda t, i, ids: (steps * ids[0] + i, 0, 0))],
-            out_specs=pl.BlockSpec((tok, 2 * HD), lambda t, i, ids: (t, i))),
+            + [pl.BlockSpec((HEADS, dim, HD), lambda t, ids: (ids[0], 0, 0))],
+            out_specs=pl.BlockSpec((tok, HEADS * HD), lambda t, ids: (t, 0))),
         out_shape=jax.ShapeDtypeStruct((2 * tok, HEADS * HD), jnp.bfloat16),
-        compiler_params=params(20, 2),
+        compiler_params=params(24),
         cost_estimate=pl.CostEstimate(flops=4 * tok * dim * HEADS * HD, bytes_accessed=12 << 20, transcendentals=0),
     )(ids, a, b, w)
 
@@ -496,6 +504,22 @@
         compiler_params=params(16),
         cost_estimate=pl.CostEstimate(flops=4 * tok * rows * width, bytes_accessed=10 << 20, transcendentals=0),
     )(core.reshape(1).astype(jnp.int32), a, b, c)
+
+
+def wgrad_one(a, b, partner):
+    rows, tok = a.shape
+    width = b.shape[1]
+    step = 256
+    heads = step // HD
+    return pl.pallas_call(
+        functools.partial(wgrad_one_kernel, partner),
+        grid=(width // step,),
+        in_specs=[pl.BlockSpec((rows, tok), whole), pl.BlockSpec((tok, step), lambda i: (0, i))],
+        out_specs=pl.BlockSpec((heads, rows, HD), lambda i: (i, 0, 0)),
+        out_shape=jax.ShapeDtypeStruct((width // HD, rows, HD), jnp.float32),
+        compiler_params=params(16),
+        cost_estimate=pl.CostEstimate(flops=2 * tok * rows * width, bytes_accessed=6 << 20, transcendentals=0),
+    )(a, b)
 
 
 def after(value, *others):
@@ -547,16 +571,20 @@
 
         o, lse = attend(seg_all, ids, q, kv_far, kv_near, seg_rows)
         o_p = send(o, core_pairs)
-        dwo_far = wgrad(core, dy_far, o, o_p)
+        dwo_far = wgrad_one(dy_far, o, False)
         dwo_in = send(dwo_far, chip_pairs)
-
-        lse = after(lse, dwo_far)
+        dwo_far2 = wgrad_one(dy_far, o_p, True)
+        dwo_in2 = send(dwo_far2, chip_pairs)
+
+        lse = after(lse, dwo_far2)
         dq_part, dkv_far = attend_grad(True, seg_all, ids, q, do, o, kv_far, seg_rows, lse)
         dkv_in = send(dkv_far, down_pairs)
         dq, dkv_near = attend_grad(False, seg_all, ids, q, do, o, kv_near, seg_rows, lse, dq_part)
         dq_p = send(dq, core_pairs)
-        dwq_far = wgrad(core, x_far, dq, dq_p)
-        dwq_in = send(dwq_far, chip_pairs)
+        dwq_far1 = wgrad_one(x_far, dq, False)
+        dwq_in = send(dwq_far1, chip_pairs)
+        dwq_far = wgrad_one(x_far, dq_p, True)
+        dwq_in2 = send(dwq_far, chip_pairs)
 
         y = expand(ids, after(o, dwq_far), o_p, w_o)
         x_near = turn(near_rows, after(x, dwq_far), x_o)
@@ -572,8 +600,12 @@
         dwkv_near = wgrad(core, x_near, after(dkv, dwkv_far), dkv_p)
         dx = expand(ids, after(dq, dwkv_far), dq_p, w_q, (dkv, dkv_p, wkv_c, wkv_p))
 
-        dw_q = jnp.transpose(dwq_near + dwq_in, (1, 0, 2))
-        dw_o = jnp.transpose(dwo_near + dwo_in, (1, 0, 2))
+        def total(near, mine, other):
+            far = jnp.where(core == 0, jnp.concatenate([mine, other]), jnp.concatenate([other, mine]))
+            return jnp.transpose(near + far, (1, 0, 2))
+
+        dw_o = total(dwo_near, dwo_in, dwo_in2)
+        dw_q = total(dwq_near, dwq_in, dwq_in2)
         dw_kv = jnp.transpose(dwkv_near + dwkv_in, (1, 0, 2)).reshape(rows, 2, 2, HD)
         return y, dx, dw_q, dw_kv[:, :, 0], dw_kv[:, :, 1], dw_o
 

time: 328 us -> 333 us (1.015)
  waiting for transfers between devices: 91.4 us -> 80.4 us
  local copies, waits for them, and re-layouts: 9.78 us -> 16.1 us
  Pallas kernels: 206 us -> 212 us
    pallas_call x0 -> x4, Pallas kernels: none -> 11.4 us  [wgrad_one(): pl.pallas_call(functools.partial(wgrad_one_kernel, partner), grid=(width...]
    ppermute x15 -> x17, waiting for transfers between devices: 91.4 us -> 80.4 us  [send(): return lax.ppermute(a, 'cp', pairs)]
    unnamed x51 -> x69, local copies, waits for them, and re-layouts: 8.17 us -> 14.5 us
    pallas_call x6 -> x4, Pallas kernels: 22.4 us -> 17.3 us  [wgrad(): pl.pallas_call(wgrad_kernel, grid_spec=pltpu.PrefetchScalarGridSpec(num_s...]
    ppermute x15 -> x17, starting transfers between devices: 15.1 us -> 16.9 us  [send(): return lax.ppermute(a, 'cp', pairs)]
  transfers between devices with their start and end apart: 15 -> 17, of which waited for: 5 -> 5; matrix products, arithmetic and copies ran while one was open for 1% -> 2% of each run, Pallas kernels for 60% -> 62%
where the time goes in v3:
time: 333 us; the launch traced here: 332 us
  Pallas kernels  212 us (64%)
  waiting for transfers between devices  80.4 us (24%)
  starting transfers between devices  16.9 us (5%)
  local copies, waits for them, and re-layouts  16.1 us (5%)
  other arithmetic  5.41 us (2%)
    ppermute x17, waiting for transfers between devices, send(): return lax.ppermute(a, 'cp', pairs)  80.4 us
    pallas_call x1, Pallas kernels, attend(): pl.pallas_call(fwd_kernel, grid_spec=pltpu.PrefetchScalarGridSpec(num_sca...  79.5 us
    pallas_call x2, Pallas kernels, attend_grad(): pl.pallas_call(functools.partial(bwd_kernel, remote), grid_spec=pltpu.Pre...  51.3 us
    pallas_call x2, Pallas kernels, expand(): pl.pallas_call(expand_kv_kernel if extra else expand_kernel, grid_spec=pl...  19.5 us
    pallas_call x4, Pallas kernels, wgrad(): pl.pallas_call(wgrad_kernel, grid_spec=pltpu.PrefetchScalarGridSpec(num_s...  17.3 us
    ppermute x17, starting transfers between devices, send(): return lax.ppermute(a, 'cp', pairs)  16.9 us
    pallas_call x2, Pallas kernels, project(): pl.pallas_call(project_kernel, grid_spec=pltpu.PrefetchScalarGridSpec(num...  15.4 us
    unnamed x69, local copies, waits for them, and re-layouts  14.5 us
  transfers between devices with their start and end apart: 17, of which 5 were waited for; matrix products, arithmetic and copies ran while one was open for 2% of the time, Pallas kernels for 62%

profile of v3, /device:TPU:0, one launch (start us, length us, event | category | flops | bytes accessed | tf_op | source)
XLA Modules:
  0.0 332.4 jit_solution(3989646587824317923)
XLA Ops:
  2.1 6.2 %project_kv.1 = (bf16[1024,256]{1,0:T(8,128)(2,1)}, bf16[1024,256]{1,0:T(8,128)(2,1)}, bf16[1536,256]{1,0:T(8,128)(2,1)}, bf16[1536,256]{1,0:T(8,128)(2,1)}) custom-call(s32[2]{0:T(128)} %pad_add_fusion.1.ids_ref.refs_1_, bf16[1024,1536]{1,0:T(8,128)(2,1)} %a_ref.6, bf16[3072,128]{1,0:T(8,128)(2,1)} %bitcast.34, bf16[3072,128]{1,0:T(8,128)(2,1)} %bitcast.35), custom_call_target="tpu_custom_call" | custom-call | flops 805306368 | bytes 6291456 | tf_op jit(solution)/shard_map/project_kv/pallas_call | solution.py:428
  8.3 4.4 %collective-permute-start = (s32[1024]{0:T(1024)S(1)}, s32[1024]{0:T(1024)S(1)}, u32[]{:S(2)}, u32[]{:S(2)}) collective-permute-start(s32[1024]{0:T(1024)S(1)} %copy-done.28), channel_id=1, source_target_pairs={{0,2},{1,3},{4,6},{5,7}} | collective-permute-start | bytes 12296 | tf_op jit(solution)/shard_map/ppermute | solution.py:541
  20.8 7.7 %shard_map.118.q_ref.refs_2_ = bf16[2048,768]{1,0:T(8,128)(2,1)S(1)} custom-call(s32[2]{0:T(128)S(1)} %copy-done.14, bf16[1024,1536]{1,0:T(8,128)(2,1)S(1)} %copy-done.8, bf16[1024,1536]{1,0:T(8,128)(2,1)} %collective-permute-done.3.a_oth.b_ref, bf16[12,1536,128]{2,1,0:T(8,128)(2,1)S(1)} %bitcast.28), custom_call_target="tpu_custom_call" | custom-call | flops 4831838208 | bytes 12582912 | tf_op jit(solution)/shard_map/pallas_call | solution.py:411
  28.5 10.5 %collective-permute-done.5.kv_far1.refs_6_ = bf16[1024,256]{1,0:T(8,128)(2,1)S(1)} collective-permute-done((bf16[1024,256]{1,0:T(8,128)(2,1)}, bf16[1024,256]{1,0:T(8,128)(2,1)S(1)}, u32[]{:S(2)}, u32[]{:S(2)}) %collective-permute-start.5) | collective-permute-done | bytes 524320 | tf_op jit(solution)/shard_map/ppermute | solution.py:541
  39.1 79.5 %attend.1 = (bf16[2048,768]{1,0:T(8,128)(2,1)S(1)}, f32[8,1,1536]{2,1,0:T(1,128)S(1)}) custom-call(s32[4096]{0:T(1024)S(1)} %constant_dynamic-update-slice_fusion.seg_ref.refs_0_, s32[2]{0:T(128)S(1)} %copy-done.14, bf16[2048,768]{1,0:T(8,128)(2,1)S(1)} %shard_map.118.q_ref.refs_2_, bf16[1024,256]{1,0:T(8,128)(2,1)S(1)} %collective-permute-done.4.kv_far0.refs_5_, ...), custom_call_target="tpu_custom_call" | custom-call | flops 8053063680 | bytes 12582912 | tf_op jit(solution)/shard_map/attend/pallas_call | solution.py:357
  118.7 3.0 copy-done.15
  121.6 2.8 shard_map.121.a_ref
  124.5 2.9 copy-done.4
  127.4 7.7 %shard_map.120.refs_3_ = bf16[2048,768]{1,0:T(8,128)(2,1)S(1)} custom-call(s32[2]{0:T(128)S(1)} %copy-done.14, bf16[1024,1536]{1,0:T(8,128)(2,1)S(1)} %copy-done.16, bf16[1024,1536]{1,0:T(8,128)(2,1)} %collective-permute-done.7.a_oth.b_ref, bf16[12,1536,128]{2,1,0:T(8,128)(2,1)S(1)} %bitcast.23), custom_call_target="tpu_custom_call" | custom-call | flops 4831838208 | bytes 12582912 | tf_op jit(solution)/shard_map/pallas_call | solution.py:411
  135.2 3.8 %shard_map.122 = f32[6,384,128]{2,1,0:T(8,128)S(1)} custom-call(bf16[384,2048]{1,0:T(8,128)(2,1)S(1)} %shard_map.121.a_ref, bf16[2048,768]{1,0:T(8,128)(2,1)} %collective-permute-done.8.b_ref.c_ref), custom_call_target="tpu_custom_call" | custom-call | flops 1207959552 | bytes 6291456 | tf_op jit(solution)/shard_map/pallas_call | solution.py:514
  145.9 48.6 %attend_grad_local.1 = (bf16[2048,768]{1,0:T(8,128)(2,1)S(1)}, f32[2048,256]{1,0:T(8,128)S(1)}) custom-call(s32[4096]{0:T(1024)S(1)} %constant_dynamic-update-slice_fusion.seg_ref.refs_0_, s32[2]{0:T(128)S(1)} %copy-done.14, bf16[2048,768]{1,0:T(8,128)(2,1)S(1)} %copy-done.27, bf16[2048,768]{1,0:T(8,128)(2,1)S(1)} %shard_map.120.refs_3_, ...), custom_call_target="tpu_custom_call" | custom-call | flops 10066329600 | bytes 20971520 | tf_op jit(solution)/shard_map/attend_grad_local/pallas_call | solution.py:396
  194.5 8.3 %collective-permute-done.10 = f32[2048,256]{1,0:T(8,128)S(1)} collective-permute-done((f32[2048,256]{1,0:T(8,128)S(1)}, f32[2048,256]{1,0:T(8,128)S(1)}, u32[]{:S(2)}, u32[]{:S(2)}) %collective-permute-start.10) | collective-permute-done | bytes 2097184 | tf_op jit(solution)/shard_map/ppermute | solution.py:541
  209.9 2.8 shard_map.119.a_ref
  216.8 2.8 shard_map.124
  221.5 3.6 %shard_map.123 = f32[6,384,128]{2,1,0:T(8,128)S(1)} custom-call(bf16[384,2048]{1,0:T(8,128)(2,1)S(1)} %shard_map.119.a_ref, bf16[2048,768]{1,0:T(8,128)(2,1)} %collective-permute-done.9.b_ref.c_ref), custom_call_target="tpu_custom_call" | custom-call | flops 1207959552 | bytes 6291456 | tf_op jit(solution)/shard_map/pallas_call | solution.py:514
  225.5 3.5 %shard_map.129.a_ref = bf16[384,2048]{1,0:T(8,128)(2,1)S(1)} custom-call(s32[1]{0:T(128)} %bitcast.11.ids_ref, bf16[1024,1536]{1,0:T(8,128)(2,1)S(1)} %copy-done.17, bf16[1024,1536]{1,0:T(8,128)(2,1)} %collective-permute-done.7.a_oth.b_ref), custom_call_target="tpu_custom_call" | custom-call | flops 2147483648 | bytes 3145728 | tf_op jit(solution)/shard_map/pallas_call | solution.py:476
  229.0 5.8 %shard_map.130 = f32[12,384,128]{2,1,0:T(8,128)S(1)} custom-call(s32[1]{0:T(128)} %bitcast.ids_ref, bf16[384,2048]{1,0:T(8,128)(2,1)S(1)} %shard_map.129.a_ref, bf16[2048,768]{1,0:T(8,128)(2,1)S(1)} %copy-done.3, bf16[2048,768]{1,0:T(8,128)(2,1)} %collective-permute-done.8.b_ref.c_ref), custom_call_target="tpu_custom_call" | custom-call | flops 2415919104 | bytes 10485760 | tf_op jit(solution)/shard_map/pallas_call | solution.py:495
  234.8 8.7 %out_y.1 = bf16[1024,1536]{1,0:T(8,128)(2,1)} custom-call(s32[2]{0:T(128)S(1)} %copy-done.14, bf16[2048,768]{1,0:T(8,128)(2,1)S(1)} %copy-done.3, bf16[2048,768]{1,0:T(8,128)(2,1)} %collective-permute-done.8.b_ref.c_ref, bf16[12,1536,128]{2,1,0:T(8,128)(2,1)S(1)} %bitcast.26, bf16[12,1536,128]{2,1,0:T(8,128)(2,1)S(1)} %bitcast.27), custom_call_target="tpu_custom_call" | custom-call | flops 4831838208 | bytes 14680064 | tf_op jit(solution)/shard_map/out_y/pallas_call | solution.py:461
  243.5 20.6 %collective-permute-done.16 = f32[6,384,128]{2,1,0:T(8,128)S(1)} collective-permute-done((f32[6,384,128]{2,1,0:T(8,128)S(1)}, f32[6,384,128]{2,1,0:T(8,128)S(1)}, u32[]{:S(2)}, u32[]{:S(2)}) %collective-permute-start.16) | collective-permute-done | bytes 1179680 | tf_op jit(solution)/shard_map/ppermute | solution.py:541
  268.4 2.9 shard_map.128
  271.4 5.9 %shard_map.126 = f32[12,384,128]{2,1,0:T(8,128)S(1)} custom-call(s32[1]{0:T(128)} %bitcast.ids_ref, bf16[384,2048]{1,0:T(8,128)(2,1)S(1)} %shard_map.125.a_ref, bf16[2048,768]{1,0:T(8,128)(2,1)S(1)} %get-tuple-element.38.a_ref.b_ref, bf16[2048,768]{1,0:T(8,128)(2,1)} %collective-permute-done.9.b_ref.c_ref), custom_call_target="tpu_custom_call" | custom-call | flops 2415919104 | bytes 10485760 | tf_op jit(solution)/shard_map/pallas_call | solution.py:495
  277.3 10.8 %grad_x.1 = bf16[1024,1536]{1,0:T(8,128)(2,1)} custom-call(s32[2]{0:T(128)S(1)} %copy-done.14, bf16[2048,768]{1,0:T(8,128)(2,1)S(1)} %get-tuple-element.38.a_ref.b_ref, bf16[2048,768]{1,0:T(8,128)(2,1)} %collective-permute-done.9.b_ref.c_ref, bf16[12,1536,128]{2,1,0:T(8,128)(2,1)S(1)} %bitcast.31, bf16[12,1536,128]{2,1,0:T(8,128)(2,1)S(1)} %bitcast.32, ...), custom_call_target="tpu_custom_call" | custom-call | flops 4831838208 | bytes 14680064 | tf_op jit(solution)/shard_map/grad_x/pallas_call | solution.py:461
  288.1 18.1 %collective-permute-done.14 = f32[4,384,128]{2,1,0:T(8,128)S(1)} collective-permute-done((f32[4,384,128]{2,1,0:T(8,128)S(1)}, f32[4,384,128]{2,1,0:T(8,128)S(1)}, u32[]{:S(2)}, u32[]{:S(2)}) %collective-permute-start.14) | collective-permute-done | bytes 786464 | tf_op jit(solution)/shard_map/ppermute | solution.py:541
  307.8 22.9 %collective-permute-done.13 = f32[6,384,128]{2,1,0:T(8,128)S(1)} collective-permute-done((f32[6,384,128]{2,1,0:T(8,128)S(1)}, f32[6,384,128]{2,1,0:T(8,128)S(1)}, u32[]{:S(2)}, u32[]{:S(2)}) %collective-permute-start.13) | collective-permute-done | bytes 1179680 | tf_op jit(solution)/shard_map/ppermute | solution.py:541
  (113 shorter events, 37.5 us)
Async XLA Ops:
  0.6 17.8 %collective-permute-start.3 = (bf16[1024,1536]{1,0:T(8,128)(2,1)}, bf16[1024,1536]{1,0:T(8,128)(2,1)}, u32[]{:S(2)}, u32[]{:S(2)}) collective-permute-start(bf16[1024,1536]{1,0:T(8,128)(2,1)} %a_ref.6), channel_id=1, source_target_pairs={{0,1},{1,0},{2,3},{3,2},{4,5},{5,4},{6,7},{7,6}} | collective-permute-start | bytes 9437192 | tf_op jit(solution)/shard_map/ppermute | solution.py:541
  2.1 16.4 %copy-start.14 = (s32[2]{0:T(128)S(1)}, s32[2]{0:T(128)}, u32[]{:S(2)}) copy-start(s32[2]{0:T(128)} %pad_add_fusion.1.ids_ref.refs_1_) | copy-start | bytes 28
  8.3 7.5 %collective-permute-start = (s32[1024]{0:T(1024)S(1)}, s32[1024]{0:T(1024)S(1)}, u32[]{:S(2)}, u32[]{:S(2)}) collective-permute-start(s32[1024]{0:T(1024)S(1)} %copy-done.28), channel_id=1, source_target_pairs={{0,2},{1,3},{4,6},{5,7}} | collective-permute-start | bytes 12296 | tf_op jit(solution)/shard_map/ppermute | solution.py:541
  12.7 4.5 %collective-permute-start.1 = (s32[1024]{0:T(1024)S(1)}, s32[1024]{0:T(1024)S(1)}, u32[]{:S(2)}, u32[]{:S(2)}) collective-permute-start(s32[1024]{0:T(1024)S(1)} %copy-done.28), channel_id=1, source_target_pairs={{0,3},{1,2},{4,7},{5,6}} | collective-permute-start | bytes 12296 | tf_op jit(solution)/shard_map/ppermute | solution.py:541
  14.1 4.3 %collective-permute-start.2 = (s32[1024]{0:T(1024)S(1)}, s32[1024]{0:T(1024)S(1)}, u32[]{:S(2)}, u32[]{:S(2)}) collective-permute-start(s32[1024]{0:T(1024)S(1)} %copy-done.28), channel_id=1, source_target_pairs={{0,1},{1,0},{2,3},{3,2},{4,5},{5,4},{6,7},{7,6}} | collective-permute-start | bytes 12296 | tf_op jit(solution)/shard_map/ppermute | solution.py:541
  14.2 14.3 %collective-permute-start.4 = (bf16[1024,256]{1,0:T(8,128)(2,1)}, bf16[1024,256]{1,0:T(8,128)(2,1)S(1)}, u32[]{:S(2)}, u32[]{:S(2)}) collective-permute-start(bf16[1024,256]{1,0:T(8,128)(2,1)} %get-tuple-element.25.kv_own.refs_5_), channel_id=1, source_target_pairs={{0,2},{1,3},{4,6},{5,7}} | collective-permute-start | bytes 1572872 | tf_op jit(solution)/shard_map/ppermute | solution.py:541
  15.8 23.2 %collective-permute-start.5 = (bf16[1024,256]{1,0:T(8,128)(2,1)}, bf16[1024,256]{1,0:T(8,128)(2,1)S(1)}, u32[]{:S(2)}, u32[]{:S(2)}) collective-permute-start(bf16[1024,256]{1,0:T(8,128)(2,1)} %get-tuple-element.28), channel_id=1, source_target_pairs={{0,3},{1,2},{4,7},{5,6}} | collective-permute-start | bytes 1572872 | tf_op jit(solution)/shard_map/ppermute | solution.py:541
  17.2 21.9 %collective-permute-start.6 = (bf16[1024,256]{1,0:T(8,128)(2,1)}, bf16[1024,256]{1,0:T(8,128)(2,1)S(1)}, u32[]{:S(2)}, u32[]{:S(2)}) collective-permute-start(bf16[1024,256]{1,0:T(8,128)(2,1)} %get-tuple-element.28), channel_id=1, source_target_pairs={{0,1},{1,0},{2,3},{3,2},{4,5},{5,4},{6,7},{7,6}} | collective-permute-start | bytes 1572872 | tf_op jit(solution)/shard_map/ppermute | solution.py:541
  18.4 100.3 %collective-permute-start.7 = (bf16[1024,1536]{1,0:T(8,128)(2,1)}, bf16[1024,1536]{1,0:T(8,128)(2,1)}, u32[]{:S(2)}, u32[]{:S(2)}) collective-permute-start(bf16[1024,1536]{1,0:T(8,128)(2,1)} %a_ref.7), channel_id=1, source_target_pairs={{0,1},{1,0},{2,3},{3,2},{4,5},{5,4},{6,7},{7,6}} | collective-permute-start | bytes 9437192 | tf_op jit(solution)/shard_map/ppermute | solution.py:541
  20.8 18.2 %copy-start.18 = (bf16[1024,256]{1,0:T(8,128)(2,1)S(1)}, bf16[1024,256]{1,0:T(8,128)(2,1)}, u32[]{:S(2)}) copy-start(bf16[1024,256]{1,0:T(8,128)(2,1)} %get-tuple-element.25.kv_own.refs_5_) | copy-start | bytes 1572868
  28.5 90.0 %copy-start.26 = (bf16[2048,768]{1,0:T(8,128)(2,1)}, bf16[2048,768]{1,0:T(8,128)(2,1)S(1)}, u32[]{:S(2)}) copy-start(bf16[2048,768]{1,0:T(8,128)(2,1)S(1)} %shard_map.118.q_ref.refs_2_) | copy-start | bytes 9437188
  28.5 90.0 %copy-start.20 = (bf16[1024,256]{1,0:T(8,128)(2,1)}, bf16[1024,256]{1,0:T(8,128)(2,1)S(1)}, u32[]{:S(2)}) copy-start(bf16[1024,256]{1,0:T(8,128)(2,1)S(1)} %collective-permute-done.4.kv_far0.refs_5_) | copy-start | bytes 1572868
  39.0 79.5 %copy-start.24 = (bf16[1024,256]{1,0:T(8,128)(2,1)}, bf16[1024,256]{1,0:T(8,128)(2,1)S(1)}, u32[]{:S(2)}) copy-start(bf16[1024,256]{1,0:T(8,128)(2,1)S(1)} %collective-permute-done.5.kv_far1.refs_6_) | copy-start | bytes 1572868
  39.1 79.5 %copy-start.22 = (bf16[1024,256]{1,0:T(8,128)(2,1)}, bf16[1024,256]{1,0:T(8,128)(2,1)S(1)}, u32[]{:S(2)}) copy-start(bf16[1024,256]{1,0:T(8,128)(2,1)S(1)} %collective-permute-done.6.kv_oth.refs_6_) | copy-start | bytes 1572868
  118.6 21.4 %copy-start = (bf16[2048,768]{1,0:T(8,128)(2,1)}, bf16[2048,768]{1,0:T(8,128)(2,1)S(1)}, u32[]{:S(2)}) copy-start(bf16[2048,768]{1,0:T(8,128)(2,1)S(1)} %get-tuple-element.35.refs_4_.a_ref.b_ref) | copy-start | bytes 9437188
  118.6 16.5 %collective-permute-start.8 = (bf16[2048,768]{1,0:T(8,128)(2,1)S(1)}, bf16[2048,768]{1,0:T(8,128)(2,1)}, u32[]{:S(2)}, u32[]{:S(2)}) collective-permute-start(bf16[2048,768]{1,0:T(8,128)(2,1)S(1)} %get-tuple-element.35.refs_4_.a_ref.b_ref), channel_id=1, source_target_pairs={{0,1},{1,0},{2,3},{3,2},{4,5},{5,4},{6,7},{7,6}} | collective-permute-start | bytes 9437192 | tf_op jit(solution)/shard_map/ppermute | solution.py:541
  142.7 60.1 %collective-permute-start.10 = (f32[2048,256]{1,0:T(8,128)S(1)}, f32[2048,256]{1,0:T(8,128)S(1)}, u32[]{:S(2)}, u32[]{:S(2)}) collective-permute-start(f32[2048,256]{1,0:T(8,128)S(1)} %get-tuple-element.37), channel_id=1, source_target_pairs={{2,0},{3,1},{6,4},{7,5}} | collective-permute-start | bytes 6291464 | tf_op jit(solution)/shard_map/ppermute | solution.py:541
  194.5 27.0 %collective-permute-start.9 = (bf16[2048,768]{1,0:T(8,128)(2,1)S(1)}, bf16[2048,768]{1,0:T(8,128)(2,1)}, u32[]{:S(2)}, u32[]{:S(2)}) collective-permute-start(bf16[2048,768]{1,0:T(8,128)(2,1)S(1)} %get-tuple-element.38.a_ref.b_ref), channel_id=1, source_target_pairs={{0,1},{1,0},{2,3},{3,2},{4,5},{5,4},{6,7},{7,6}} | collective-permute-start | bytes 9437192 | tf_op jit(solution)/shard_map/ppermute | solution.py:541
  204.3 12.5 %collective-permute-start.11 = (bf16[2048,256]{1,0:T(8,128)(2,1)}, bf16[2048,256]{1,0:T(8,128)(2,1)}, u32[]{:S(2)}, u32[]{:S(2)}) collective-permute-start(bf16[2048,256]{1,0:T(8,128)(2,1)} %pad_maximum_fusion.b_ref.c_ref), channel_id=1, source_target_pairs={{0,1},{1,0},{2,3},{3,2},{4,5},{5,4},{6,7},{7,6}} | collective-permute-start | bytes 3145736 | tf_op jit(solution)/shard_map/ppermute | solution.py:541
  209.9 33.6 %collective-permute-start.15 = (f32[6,384,128]{2,1,0:T(8,128)S(1)}, f32[6,384,128]{2,1,0:T(8,128)S(1)}, u32[]{:S(2)}, u32[]{:S(2)}) collective-permute-start(f32[6,384,128]{2,1,0:T(8,128)S(1)} %shard_map.131), channel_id=1, source_target_pairs={{0,2},{2,0},{1,3},{3,1},{4,6},{6,4},{5,7},{7,5}} | collective-permute-start | bytes 3538952 | tf_op jit(solution)/shard_map/ppermute | solution.py:541
  212.7 51.3 %collective-permute-start.16 = (f32[6,384,128]{2,1,0:T(8,128)S(1)}, f32[6,384,128]{2,1,0:T(8,128)S(1)}, u32[]{:S(2)}, u32[]{:S(2)}) collective-permute-start(f32[6,384,128]{2,1,0:T(8,128)S(1)} %copy-done.11), channel_id=1, source_target_pairs={{0,2},{2,0},{1,3},{3,1},{4,6},{6,4},{5,7},{7,5}} | collective-permute-start | bytes 3538952 | tf_op jit(solution)/shard_map/ppermute | solution.py:541
  216.7 91.1 %collective-permute-start.12 = (f32[6,384,128]{2,1,0:T(8,128)S(1)}, f32[6,384,128]{2,1,0:T(8,128)S(1)}, u32[]{:S(2)}, u32[]{:S(2)}) collective-permute-start(f32[6,384,128]{2,1,0:T(8,128)S(1)} %shard_map.127), channel_id=1, source_target_pairs={{0,2},{2,0},{1,3},{3,1},{4,6},{6,4},{5,7},{7,5}} | collective-permute-start | bytes 3538952 | tf_op jit(solution)/shard_map/ppermute | solution.py:541
  219.6 86.6 %collective-permute-start.14 = (f32[4,384,128]{2,1,0:T(8,128)S(1)}, f32[4,384,128]{2,1,0:T(8,128)S(1)}, u32[]{:S(2)}, u32[]{:S(2)}) collective-permute-start(f32[4,384,128]{2,1,0:T(8,128)S(1)} %shard_map.124), channel_id=1, source_target_pairs={{0,2},{2,0},{1,3},{3,1},{4,6},{6,4},{5,7},{7,5}} | collective-permute-start | bytes 2359304 | tf_op jit(solution)/shard_map/ppermute | solution.py:541
  225.2 105.6 %collective-permute-start.13 = (f32[6,384,128]{2,1,0:T(8,128)S(1)}, f32[6,384,128]{2,1,0:T(8,128)S(1)}, u32[]{:S(2)}, u32[]{:S(2)}) collective-permute-start(f32[6,384,128]{2,1,0:T(8,128)S(1)} %shard_map.123), channel_id=1, source_target_pairs={{0,2},{2,0},{1,3},{3,1},{4,6},{6,4},{5,7},{7,5}} | collective-permute-start | bytes 3538952 | tf_op jit(solution)/shard_map/ppermute | solution.py:541
  (26 other events, 129.1 us)

commit v4 on v3

--- a/solution.py
+++ b/solution.py
@@ -72,7 +72,7 @@
     return count
 
 
-def fwd_kernel(seg_ref, ids_ref, q_ref, kv_far0, kv_far1, kv_own, kv_oth, rows_ref, o_ref, lse_ref,
+def fwd_kernel(seg_ref, ids_ref, q_ref, kv_far0, kv_far1, kv_own, kv_oth, rows_ref, o_ref, lse_ref, reach_ref,
                segk, kv_ref, qt, acc, m_ref, l_ref, pm):
     step = pl.program_id(0)
     core = ids_ref[0]
@@ -82,6 +82,10 @@
     @pl.when(step == 0)
     def _():
         spread_segments(rows_ref, segk, 0, 2 * HALF)
+        first = jnp.where(ids_ref[1] == 0, HALF, 0)
+        ends = [seg_ref[store_block(first + p, core) * BLK + BLK - 1] for p in (HALF // 2 - 1, HALF - 1)]
+        reach_ref[0] = (ends[0] == ends[1]).astype(jnp.int32)
+
         for i, part in enumerate((kv_far0, kv_far1, kv_own, kv_oth)):
             kv_ref[i * tok:(i + 1) * tok, :] = part[...]
 
@@ -175,8 +179,8 @@
 def bwd_kernel(remote, *refs):
     if remote:
         (seg_ref, ids_ref, q_ref, do_ref, o_ref, kv_own, kv_oth,
-         rows_ref, lse_ref, dq_out, dkv_ref,
-         segk, kv_ref, qs, qt, ds_, dt, delta, pm, sm, dqt) = refs
+         rows_ref, lse_ref, dq_out, dkv_first, dkv_second,
+         segk, kv_ref, qs, qt, ds_, dt, delta, pm, sm, dqt, dkv_ref) = refs
     else:
         (seg_ref, ids_ref, q_ref, do_ref, o_ref, kv_own, kv_oth,
          rows_ref, lse_ref, dq_in, dq_out, dkv_ref,
@@ -233,14 +237,21 @@
             dsv = w * (dp - delta[:, cols])
             pm[:, cols] = w.astype(jnp.bfloat16)
             sm[:, cols] = dsv.astype(jnp.bfloat16)
-        dkv_ref[pl.ds(key_start, BLK), HD:] += dot(pm[...], ds_[...])
-        dkv_ref[pl.ds(key_start, BLK), :HD] += dot(sm[...], qs[...])
+        put = pl.multiple_of(p * BLK, BLK) if remote else key_start
+        dkv_ref[pl.ds(put, BLK), HD:] += dot(pm[...], ds_[...])
+        dkv_ref[pl.ds(put, BLK), :HD] += dot(sm[...], qs[...])
         dqt[...] += dot(k_blk.T, sm[...])
         return carry
 
     lax.fori_loop(0, count, body, 0)
     if remote:
         dq_out[0] = dqt[...]
+
+        @pl.when(step == pl.num_programs(0) - 1)
+        def _():
+            tok = dkv_first.shape[0]
+            dkv_first[...] = dkv_ref[:tok, :]
+            dkv_second[...] = dkv_ref[tok:, :]
     else:
         for h in range(HEADS):
             cols = slice(h * BLK, (h + 1) * BLK)
@@ -360,13 +371,13 @@
             num_scalar_prefetch=2, grid=(grid,),
             in_specs=[block] + [pl.BlockSpec((tok // 2, 2 * HD), whole)] * 4
             + [pl.BlockSpec((keys // BLK, 1, BLK), whole3)],
-            out_specs=[block, pl.BlockSpec((1, 1, WIDE), lead)],
+            out_specs=[block, pl.BlockSpec((1, 1, WIDE), lead), pl.BlockSpec(memory_space=pltpu.SMEM)],
             scratch_shapes=[pltpu.VMEM((keys, 128), jnp.int32), pltpu.VMEM((keys, 2 * HD), jnp.bfloat16),
                             pltpu.VMEM((HD, WIDE), jnp.bfloat16), pltpu.VMEM((HD, WIDE), jnp.float32),
                             pltpu.VMEM((1, WIDE), jnp.float32), pltpu.VMEM((8, WIDE), jnp.float32),
                             pltpu.VMEM((BLK, WIDE), jnp.bfloat16)]),
         out_shape=[jax.ShapeDtypeStruct((tok, HEADS * HD), jnp.bfloat16),
-                   jax.ShapeDtypeStruct((grid, 1, WIDE), jnp.float32)],
+                   jax.ShapeDtypeStruct((grid, 1, WIDE), jnp.float32), jax.ShapeDtypeStruct((1,), jnp.int32)],
         compiler_params=params(24), name='attend',
         cost_estimate=pl.CostEstimate(flops=40 * 4 * WIDE * BLK * HD, bytes_accessed=12 << 20, transcendentals=0),
     )(seg, ids, q, *kv_far, *kv_near, rows)
@@ -382,9 +393,12 @@
     dqt_spec = pl.BlockSpec((1, HD, WIDE), lead)
     kv_grad = jax.ShapeDtypeStruct((tok, 2 * HD), jnp.float32)
     kv_spec = pl.BlockSpec((tok, 2 * HD), whole)
+    extra = []
     if remote:
-        out_shape = [jax.ShapeDtypeStruct((grid, HD, WIDE), jnp.float32), kv_grad]
-        out_specs = [dqt_spec, kv_spec]
+        shard = jax.ShapeDtypeStruct((tok // 2, 2 * HD), jnp.float32)
+        out_shape = [jax.ShapeDtypeStruct((grid, HD, WIDE), jnp.float32), shard, shard]
+        out_specs = [dqt_spec] + [pl.BlockSpec((tok // 2, 2 * HD), whole)] * 2
+        extra = [pltpu.VMEM((tok, 2 * HD), jnp.float32)]
     else:
         in_specs.append(dqt_spec)
         args.append(dq_in)
@@ -399,7 +413,7 @@
             num_scalar_prefetch=2, grid=(grid,), in_specs=in_specs, out_specs=out_specs,
             scratch_shapes=[pltpu.VMEM((tok, 128), jnp.int32), pltpu.VMEM((tok, 2 * HD), jnp.bfloat16),
                             stack, flip, stack, flip, pltpu.VMEM((1, WIDE), jnp.float32),
-                            tile, tile, pltpu.VMEM((HD, WIDE), jnp.float32)]),
+                            tile, tile, pltpu.VMEM((HD, WIDE), jnp.float32)] + extra),
         out_shape=out_shape, compiler_params=params(28),
         name='attend_grad_remote' if remote else 'attend_grad_local',
         cost_estimate=pl.CostEstimate(flops=20 * 10 * WIDE * BLK * HD, bytes_accessed=20 << 20, transcendentals=0),
@@ -565,21 +579,30 @@
         seg_rows = seg_all.reshape(-1, 1, BLK)
         kv_far, kv_near = (kv_far0, kv_far1), (kv_own, kv_oth)
         q = project(ids, after(x, kv_own), x_o, w_q)
-        do = project(ids, after(dy, kv_own), dy_o, w_o)
         dy_far = turn(far_rows, dy, dy_o)
         x_far = turn(far_rows, x, x_o)
 
-        o, lse = attend(seg_all, ids, q, kv_far, kv_near, seg_rows)
+        o, lse, reach = attend(seg_all, ids, q, kv_far, kv_near, seg_rows)
         o_p = send(o, core_pairs)
         dwo_far = wgrad_one(dy_far, o, False)
         dwo_in = send(dwo_far, chip_pairs)
         dwo_far2 = wgrad_one(dy_far, o_p, True)
         dwo_in2 = send(dwo_far2, chip_pairs)
 
-        lse = after(lse, dwo_far2)
-        dq_part, dkv_far = attend_grad(True, seg_all, ids, q, do, o, kv_far, seg_rows, lse)
-        dkv_in = send(dkv_far, down_pairs)
-        dq, dkv_near = attend_grad(False, seg_all, ids, q, do, o, kv_near, seg_rows, lse, dq_part)
+        do = project(ids, after(dy, dwo_far), dy_o, w_o)
+        dq_part, dkv_far0, dkv_far1 = attend_grad(True, seg_all, ids, q, do, o, kv_far, seg_rows, lse)
+        dkv_in1 = send(dkv_far1, down_pairs)
+
+        local = (seg_all, ids, q, do, o, kv_near, seg_rows, lse, dq_part)
+
+        def sent(first, args):
+            got = send(first, down_pairs)
+            return *attend_grad(False, *args), got
+
+        def kept(first, args):
+            return *attend_grad(False, *args), jnp.zeros_like(first)
+
+        dq, dkv_near, dkv_in0 = lax.cond(reach[0] != 0, sent, kept, dkv_far0, local)
         dq_p = send(dq, core_pairs)
         dwq_far1 = wgrad_one(x_far, dq, False)
         dwq_in = send(dwq_far1, chip_pairs)
@@ -592,7 +615,8 @@
         dwo_near = wgrad(core, dy_near, o, o_p)
         dwq_near = wgrad(core, x_near, dq, dq_p)
 
-        dkv = dkv_near + dkv_in
+        dkv = dkv_near + jnp.where(core == 0, jnp.concatenate([dkv_in0, dkv_in1]),
+                                   jnp.concatenate([dkv_in1, dkv_in0]))
         dkv = jnp.concatenate([dkv[:, :HD] * HD ** -0.5, dkv[:, HD:]], axis=1).astype(jnp.bfloat16)
         dkv_p = send(dkv, core_pairs)
         dwkv_far = wgrad(core, x_far, dkv, dkv_p)

time: 333 us -> 328 us (0.985)
  local copies, waits for them, and re-layouts: 16.1 us -> 5.82 us
  starting transfers between devices: 16.9 us -> 23.5 us
    unnamed x69 -> x47, local copies, waits for them, and re-layouts: 14.5 us -> 4.21 us
    ppermute x17 -> x18, starting transfers between devices: 16.9 us -> 23.5 us  [send(): return lax.ppermute(a, 'cp', pairs)]
    pallas_call x4, Pallas kernels: 17.3 us -> 14 us  [wgrad(): pl.pallas_call(wgrad_kernel, grid_spec=pltpu.PrefetchScalarGridSpec(num_s...]
    ppermute x17 -> x18, waiting for transfers between devices: 80.4 us -> 77.9 us  [send(): return lax.ppermute(a, 'cp', pairs)]
  transfers between devices with their start and end apart: 17 -> 18, of which waited for: 5 -> 5; matrix products, arithmetic and copies ran while one was open for 2% -> 2% of each run, Pallas kernels for 62% -> 34%
where the time goes in v4:
time: 328 us
  Pallas kernels  212 us (65%)
  waiting for transfers between devices  77.9 us (24%)
  starting transfers between devices  23.5 us (7%)
  other arithmetic  6.86 us (2%)
  local copies, waits for them, and re-layouts  5.82 us (2%)
    pallas_call x1, Pallas kernels, attend(): pl.pallas_call(fwd_kernel, grid_spec=pltpu.PrefetchScalarGridSpec(num_sca...  79.7 us
    ppermute x18, waiting for transfers between devices, send(): return lax.ppermute(a, 'cp', pairs)  77.9 us
    pallas_call x2, Pallas kernels, attend_grad(): pl.pallas_call(functools.partial(bwd_kernel, remote), grid_spec=pltpu.Pre...  53.7 us
    ppermute x18, starting transfers between devices, send(): return lax.ppermute(a, 'cp', pairs)  23.5 us
    pallas_call x2, Pallas kernels, expand(): pl.pallas_call(expand_kv_kernel if extra else expand_kernel, grid_spec=pl...  19 us
    pallas_call x2, Pallas kernels, project(): pl.pallas_call(project_kernel, grid_spec=pltpu.PrefetchScalarGridSpec(num...  16.2 us
    pallas_call x4, Pallas kernels, wgrad(): pl.pallas_call(wgrad_kernel, grid_spec=pltpu.PrefetchScalarGridSpec(num_s...  14 us
    pallas_call x4, Pallas kernels, turn(): pl.pallas_call(turn_kernel, grid_spec=pltpu.PrefetchScalarGridSpec(num_sc...  12.3 us
  transfers between devices with their start and end apart: 18, of which 5 were waited for; matrix products, arithmetic and copies ran while one was open for 2% of the time, Pallas kernels for 34%

profile of v4, /device:TPU:0, one launch (start us, length us, event | category | flops | bytes accessed | tf_op | source)
XLA Modules:
  0.0 327.6 jit_solution(2046760904647470471)
XLA Ops:
  0.7 5.7 %project_kv.1 = (bf16[1024,256]{1,0:T(8,128)(2,1)S(1)}, bf16[1024,256]{1,0:T(8,128)(2,1)}, bf16[1536,256]{1,0:T(8,128)(2,1)}, bf16[1536,256]{1,0:T(8,128)(2,1)}) custom-call(s32[2]{0:T(128)S(1)} %pad_add_fusion.1.ids_ref.refs_1_, bf16[1024,1536]{1,0:T(8,128)(2,1)} %a_ref.6, bf16[3072,128]{1,0:T(8,128)(2,1)} %bitcast.39, bf16[3072,128]{1,0:T(8,128)(2,1)} %bitcast.40), custom_call_target="tpu_custom_call" | custom-call | flops 805306368 | bytes 6291456 | tf_op jit(solution)/shard_map/project_kv/pallas_call | solution.py:442
  7.3 4.9 %collective-permute-start.1 = (s32[1024]{0:T(1024)S(1)}, s32[1024]{0:T(1024)S(1)}, u32[]{:S(2)}, u32[]{:S(2)}) collective-permute-start(s32[1024]{0:T(1024)S(1)} %copy-done.13), channel_id=1, source_target_pairs={{0,2},{1,3},{4,6},{5,7}} | collective-permute-start | bytes 12296 | tf_op jit(solution)/shard_map/ppermute | solution.py:555
  13.6 4.1 %collective-permute-start.5 = (bf16[1024,256]{1,0:T(8,128)(2,1)S(1)}, bf16[1024,256]{1,0:T(8,128)(2,1)S(1)}, u32[]{:S(2)}, u32[]{:S(2)}) collective-permute-start(bf16[1024,256]{1,0:T(8,128)(2,1)S(1)} %get-tuple-element.95.kv_own), channel_id=1, source_target_pairs={{0,2},{1,3},{4,6},{5,7}} | collective-permute-start | bytes 1572872 | tf_op jit(solution)/shard_map/ppermute | solution.py:555
  21.1 3.5 %shard_map.120.a_ref = bf16[384,2048]{1,0:T(8,128)(2,1)S(1)} custom-call(s32[1]{0:T(128)} %bitcast.9.ids_ref, bf16[1024,1536]{1,0:T(8,128)(2,1)S(1)} %copy-done.8, bf16[1024,1536]{1,0:T(8,128)(2,1)} %collective-permute-done.8.b_ref.a_oth), custom_call_target="tpu_custom_call" | custom-call | flops 2147483648 | bytes 3145728 | tf_op jit(solution)/shard_map/pallas_call | solution.py:490
  24.6 8.5 %shard_map.118.q_ref.refs_2_ = bf16[2048,768]{1,0:T(8,128)(2,1)S(1)} custom-call(s32[2]{0:T(128)S(1)} %pad_add_fusion.1.ids_ref.refs_1_, bf16[1024,1536]{1,0:T(8,128)(2,1)S(1)} %copy-done.2, bf16[1024,1536]{1,0:T(8,128)(2,1)} %collective-permute-done.4.a_oth.b_ref, bf16[12,1536,128]{2,1,0:T(8,128)(2,1)S(1)} %bitcast.33), custom_call_target="tpu_custom_call" | custom-call | flops 4831838208 | bytes 12582912 | tf_op jit(solution)/shard_map/pallas_call | solution.py:425
  33.1 6.0 %collective-permute-done.6.kv_far1.refs_6_ = bf16[1024,256]{1,0:T(8,128)(2,1)S(1)} collective-permute-done((bf16[1024,256]{1,0:T(8,128)(2,1)}, bf16[1024,256]{1,0:T(8,128)(2,1)S(1)}, u32[]{:S(2)}, u32[]{:S(2)}) %collective-permute-start.6) | collective-permute-done | bytes 524320 | tf_op jit(solution)/shard_map/ppermute | solution.py:555
  39.2 79.7 %attend.1 = (bf16[2048,768]{1,0:T(8,128)(2,1)S(1)}, f32[8,1,1536]{2,1,0:T(1,128)S(1)}, s32[1]{0:T(128)}) custom-call(s32[4096]{0:T(1024)S(1)} %constant_dynamic-update-slice_fusion.seg_ref.refs_0_, s32[2]{0:T(128)S(1)} %pad_add_fusion.1.ids_ref.refs_1_, bf16[2048,768]{1,0:T(8,128)(2,1)S(1)} %shard_map.118.q_ref.refs_2_, ...), custom_call_target="tpu_custom_call" | custom-call | flops 8053063680 | bytes 12582912 | tf_op jit(solution)/shard_map/attend/pallas_call | solution.py:368
  122.0 7.7 %shard_map.122.refs_3_ = bf16[2048,768]{1,0:T(8,128)(2,1)S(1)} custom-call(s32[2]{0:T(128)S(1)} %pad_add_fusion.1.ids_ref.refs_1_, bf16[1024,1536]{1,0:T(8,128)(2,1)S(1)} %copy-done.9, bf16[1024,1536]{1,0:T(8,128)(2,1)} %collective-permute-done.8.b_ref.a_oth, bf16[12,1536,128]{2,1,0:T(8,128)(2,1)S(1)} %bitcast.26), custom_call_target="tpu_custom_call" | custom-call | flops 4831838208 | bytes 12582912 | tf_op jit(solution)/shard_map/pallas_call | solution.py:425
  129.7 3.8 %attend_grad_remote.1 = (f32[8,128,1536]{2,1,0:T(8,128)S(1)}, f32[1024,256]{1,0:T(8,128)S(1)}, f32[1024,256]{1,0:T(8,128)}) custom-call(s32[4096]{0:T(1024)S(1)} %constant_dynamic-update-slice_fusion.seg_ref.refs_0_, s32[2]{0:T(128)S(1)} %pad_add_fusion.1.ids_ref.refs_1_, bf16[2048,768]{1,0:T(8,128)(2,1)S(1)} %shard_map.118.q_ref.refs_2_, ...), custom_call_target="tpu_custom_call" | custom-call | flops 10066329600 | bytes 20971520 | tf_op jit(solution)/shard_map/attend_grad_remote/pallas_call | solution.py:410
  135.5 51.6 %conditional.1 = (bf16[2048,768]{1,0:T(8,128)(2,1)}, f32[2048,256]{1,0:T(8,128)}, f32[1024,256]{1,0:T(8,128)}) conditional(s32[]{:T(128)} %bitcast.10, (s32[4096]{0:T(1024)S(1)}, s32[2]{0:T(128)S(1)}, bf16[2048,768]{1,0:T(8,128)(2,1)S(1)}, bf16[2048,768]{1,0:T(8,128)(2,1)S(1)}, bf16[2048,768]{1,0:T(8,128)(2,1)S(1)}, ...), branch_computations={%region_0.1_spmd, %region_1.2_spmd} | conditional | flops 10066329600 | bytes 25165888 | solution.py:605
  136.8 49.9 %attend_grad_local.3 = (bf16[2048,768]{1,0:T(8,128)(2,1)}, f32[2048,256]{1,0:T(8,128)}) custom-call(s32[4096]{0:T(1024)S(1)} %get-tuple-element.54.refs_0_, s32[2]{0:T(128)S(1)} %get-tuple-element.55.refs_1_, bf16[2048,768]{1,0:T(8,128)(2,1)S(1)} %get-tuple-element.56.refs_2_, bf16[2048,768]{1,0:T(8,128)(2,1)S(1)} %get-tuple-element.57.refs_3_, ...), custom_call_target="tpu_custom_call" | custom-call | flops 10066329600 | bytes 20971520 | tf_op jit(solution)/shard_map/cond/branch_1_fun/attend_grad_local/pallas_call | solution.py:410
  187.0 3.6 %collective-permute-start.9 = (bf16[2048,768]{1,0:T(8,128)(2,1)}, bf16[2048,768]{1,0:T(8,128)(2,1)S(1)}, u32[]{:S(2)}, u32[]{:S(2)}) collective-permute-start(bf16[2048,768]{1,0:T(8,128)(2,1)} %get-tuple-element.111.a_ref.b_ref), channel_id=1, source_target_pairs={{0,1},{1,0},{2,3},{3,2},{4,5},{5,4},{6,7},{7,6}} | collective-permute-start | bytes 9437192 | tf_op jit(solution)/shard_map/ppermute | solution.py:555
  190.6 3.2 fusion.4
  198.4 3.7 %collective-permute-done.12.c_ref.d_ref = bf16[2048,256]{1,0:T(8,128)(2,1)S(1)} collective-permute-done((bf16[2048,256]{1,0:T(8,128)(2,1)S(1)}, bf16[2048,256]{1,0:T(8,128)(2,1)S(1)}, u32[]{:S(2)}, u32[]{:S(2)}) %collective-permute-start.12) | collective-permute-done | bytes 1048608 | tf_op jit(solution)/shard_map/ppermute | solution.py:555
  205.3 3.6 %shard_map.127 = f32[6,384,128]{2,1,0:T(8,128)S(1)} custom-call(bf16[384,2048]{1,0:T(8,128)(2,1)S(1)} %shard_map.119.a_ref, bf16[2048,768]{1,0:T(8,128)(2,1)} %get-tuple-element.111.a_ref.b_ref), custom_call_target="tpu_custom_call" | custom-call | flops 1207959552 | bytes 6291456 | tf_op jit(solution)/shard_map/pallas_call | solution.py:528
  213.0 3.6 %shard_map.131 = f32[6,384,128]{2,1,0:T(8,128)S(1)} custom-call(bf16[384,2048]{1,0:T(8,128)(2,1)S(1)} %copy-done.1, bf16[2048,768]{1,0:T(8,128)(2,1)} %collective-permute-done.10.b_ref.c_ref), custom_call_target="tpu_custom_call" | custom-call | flops 1207959552 | bytes 6291456 | tf_op jit(solution)/shard_map/pallas_call | solution.py:528
  216.7 2.7 shard_map.125.a_ref
  220.6 3.1 collective-permute-done.15
  223.9 5.8 %shard_map.126 = f32[12,384,128]{2,1,0:T(8,128)S(1)} custom-call(s32[1]{0:T(128)} %bitcast.ids_ref, bf16[384,2048]{1,0:T(8,128)(2,1)S(1)} %shard_map.125.a_ref, bf16[2048,768]{1,0:T(8,128)(2,1)} %get-tuple-element.111.a_ref.b_ref, bf16[2048,768]{1,0:T(8,128)(2,1)S(1)} %collective-permute-done.9.b_ref.c_ref), custom_call_target="tpu_custom_call" | custom-call | flops 2415919104 | bytes 10485760 | tf_op jit(solution)/shard_map/pallas_call | solution.py:509
  229.7 3.4 %shard_map.129.a_ref = bf16[384,2048]{1,0:T(8,128)(2,1)S(1)} custom-call(s32[1]{0:T(128)} %bitcast.12.ids_ref, bf16[1024,1536]{1,0:T(8,128)(2,1)S(1)} %copy-done.10, bf16[1024,1536]{1,0:T(8,128)(2,1)} %collective-permute-done.8.b_ref.a_oth), custom_call_target="tpu_custom_call" | custom-call | flops 2147483648 | bytes 3145728 | tf_op jit(solution)/shard_map/pallas_call | solution.py:490
  233.2 5.8 %shard_map.130 = f32[12,384,128]{2,1,0:T(8,128)S(1)} custom-call(s32[1]{0:T(128)} %bitcast.ids_ref, bf16[384,2048]{1,0:T(8,128)(2,1)S(1)} %shard_map.129.a_ref, bf16[2048,768]{1,0:T(8,128)(2,1)S(1)} %copy-done.12, bf16[2048,768]{1,0:T(8,128)(2,1)} %collective-permute-done.10.b_ref.c_ref), custom_call_target="tpu_custom_call" | custom-call | flops 2415919104 | bytes 10485760 | tf_op jit(solution)/shard_map/pallas_call | solution.py:509
  240.5 8.7 %out_y.1 = bf16[1024,1536]{1,0:T(8,128)(2,1)} custom-call(s32[2]{0:T(128)S(1)} %pad_add_fusion.1.ids_ref.refs_1_, bf16[2048,768]{1,0:T(8,128)(2,1)S(1)} %copy-done.12, bf16[2048,768]{1,0:T(8,128)(2,1)} %collective-permute-done.10.b_ref.c_ref, bf16[12,1536,128]{2,1,0:T(8,128)(2,1)S(1)} %bitcast.29, bf16[12,1536,128]{2,1,0:T(8,128)(2,1)S(1)} %bitcast.30), custom_call_target="tpu_custom_call" | custom-call | flops 4831838208 | bytes 14680064 | tf_op jit(solution)/shard_map/out_y/pallas_call | solution.py:475
  249.2 10.3 %grad_x.1 = bf16[1024,1536]{1,0:T(8,128)(2,1)} custom-call(s32[2]{0:T(128)S(1)} %pad_add_fusion.1.ids_ref.refs_1_, bf16[2048,768]{1,0:T(8,128)(2,1)} %get-tuple-element.111.a_ref.b_ref, bf16[2048,768]{1,0:T(8,128)(2,1)S(1)} %collective-permute-done.9.b_ref.c_ref, bf16[12,1536,128]{2,1,0:T(8,128)(2,1)S(1)} %bitcast.36, bf16[12,1536,128]{2,1,0:T(8,128)(2,1)S(1)} %bitcast.37, ...), custom_call_target="tpu_custom_call" | custom-call | flops 4831838208 | bytes 14680064 | tf_op jit(solution)/shard_map/grad_x/pallas_call | solution.py:475
  259.6 64.7 %collective-permute-done.17 = f32[6,384,128]{2,1,0:T(8,128)S(1)} collective-permute-done((f32[6,384,128]{2,1,0:T(8,128)S(1)}, f32[6,384,128]{2,1,0:T(8,128)S(1)}, u32[]{:S(2)}, u32[]{:S(2)}) %collective-permute-start.17) | collective-permute-done | bytes 1179680 | tf_op jit(solution)/shard_map/ppermute | solution.py:555
  (96 shorter events, 29.8 us)
Async XLA Ops:
  0.7 23.9 %slice-start.4 = ((s8[4718592]{0:T(1024)(128)(4,1)}), s8[524288]{0:T(1024)(128)(4,1)S(1)}, s32[]{:S(2)}) async-start(s8[4718592]{0:T(1024)(128)(4,1)} %bitcast.31), calls=%async_computation.4 | async-start | bytes 1048576
  6.4 12.7 %collective-permute-start.8 = (bf16[1024,1536]{1,0:T(8,128)(2,1)}, bf16[1024,1536]{1,0:T(8,128)(2,1)}, u32[]{:S(2)}, u32[]{:S(2)}) collective-permute-start(bf16[1024,1536]{1,0:T(8,128)(2,1)} %a_ref.7), channel_id=1, source_target_pairs={{0,1},{1,0},{2,3},{3,2},{4,5},{5,4},{6,7},{7,6}} | collective-permute-start | bytes 9437192 | tf_op jit(solution)/shard_map/ppermute | solution.py:555
  7.3 17.3 %collective-permute-start.4 = (bf16[1024,1536]{1,0:T(8,128)(2,1)}, bf16[1024,1536]{1,0:T(8,128)(2,1)}, u32[]{:S(2)}, u32[]{:S(2)}) collective-permute-start(bf16[1024,1536]{1,0:T(8,128)(2,1)} %a_ref.6), channel_id=1, source_target_pairs={{0,1},{1,0},{2,3},{3,2},{4,5},{5,4},{6,7},{7,6}} | collective-permute-start | bytes 9437192 | tf_op jit(solution)/shard_map/ppermute | solution.py:555
  7.3 6.3 %collective-permute-start.1 = (s32[1024]{0:T(1024)S(1)}, s32[1024]{0:T(1024)S(1)}, u32[]{:S(2)}, u32[]{:S(2)}) collective-permute-start(s32[1024]{0:T(1024)S(1)} %copy-done.13), channel_id=1, source_target_pairs={{0,2},{1,3},{4,6},{5,7}} | collective-permute-start | bytes 12296 | tf_op jit(solution)/shard_map/ppermute | solution.py:555
  12.1 5.5 %collective-permute-start.2 = (s32[1024]{0:T(1024)S(1)}, s32[1024]{0:T(1024)S(1)}, u32[]{:S(2)}, u32[]{:S(2)}) collective-permute-start(s32[1024]{0:T(1024)S(1)} %copy-done.13), channel_id=1, source_target_pairs={{0,3},{1,2},{4,7},{5,6}} | collective-permute-start | bytes 12296 | tf_op jit(solution)/shard_map/ppermute | solution.py:555
  13.4 5.6 %collective-permute-start.3 = (s32[1024]{0:T(1024)S(1)}, s32[1024]{0:T(1024)S(1)}, u32[]{:S(2)}, u32[]{:S(2)}) collective-permute-start(s32[1024]{0:T(1024)S(1)} %copy-done.13), channel_id=1, source_target_pairs={{0,1},{1,0},{2,3},{3,2},{4,5},{5,4},{6,7},{7,6}} | collective-permute-start | bytes 12296 | tf_op jit(solution)/shard_map/ppermute | solution.py:555
  13.6 19.6 %collective-permute-start.5 = (bf16[1024,256]{1,0:T(8,128)(2,1)S(1)}, bf16[1024,256]{1,0:T(8,128)(2,1)S(1)}, u32[]{:S(2)}, u32[]{:S(2)}) collective-permute-start(bf16[1024,256]{1,0:T(8,128)(2,1)S(1)} %get-tuple-element.95.kv_own), channel_id=1, source_target_pairs={{0,2},{1,3},{4,6},{5,7}} | collective-permute-start | bytes 1572872 | tf_op jit(solution)/shard_map/ppermute | solution.py:555
  17.7 21.5 %collective-permute-start.6 = (bf16[1024,256]{1,0:T(8,128)(2,1)}, bf16[1024,256]{1,0:T(8,128)(2,1)S(1)}, u32[]{:S(2)}, u32[]{:S(2)}) collective-permute-start(bf16[1024,256]{1,0:T(8,128)(2,1)} %get-tuple-element.98), channel_id=1, source_target_pairs={{0,3},{1,2},{4,7},{5,6}} | collective-permute-start | bytes 1572872 | tf_op jit(solution)/shard_map/ppermute | solution.py:555
  19.1 20.1 %collective-permute-start.7 = (bf16[1024,256]{1,0:T(8,128)(2,1)}, bf16[1024,256]{1,0:T(8,128)(2,1)S(1)}, u32[]{:S(2)}, u32[]{:S(2)}) collective-permute-start(bf16[1024,256]{1,0:T(8,128)(2,1)} %get-tuple-element.98), channel_id=1, source_target_pairs={{0,1},{1,0},{2,3},{3,2},{4,5},{5,4},{6,7},{7,6}} | collective-permute-start | bytes 1572872 | tf_op jit(solution)/shard_map/ppermute | solution.py:555
  24.6 94.3 %copy-start = (bf16[384,2048]{1,0:T(8,128)(2,1)}, bf16[384,2048]{1,0:T(8,128)(2,1)S(1)}, u32[]{:S(2)}) copy-start(bf16[384,2048]{1,0:T(8,128)(2,1)S(1)} %shard_map.120.a_ref) | copy-start | bytes 4718596
  24.6 97.3 %slice-start = ((s8[4718592]{0:T(1024)(128)(4,1)}), s8[4194304]{0:T(1024)(128)(4,1)S(1)}, s32[]{:S(2)}) async-start(s8[4718592]{0:T(1024)(128)(4,1)} %bitcast.24), calls=%async_computation | async-start | bytes 8388608
  33.1 88.8 %slice-start.1 = ((s8[4718592]{0:T(1024)(128)(4,1)}), s8[524288]{0:T(1024)(128)(4,1)S(1)}, s32[]{:S(2)}) async-start(s8[4718592]{0:T(1024)(128)(4,1)} %bitcast.24), calls=%async_computation.1 | async-start | bytes 1048576
  118.8 16.6 %copy-start.11 = (bf16[2048,768]{1,0:T(8,128)(2,1)}, bf16[2048,768]{1,0:T(8,128)(2,1)S(1)}, u32[]{:S(2)}) copy-start(bf16[2048,768]{1,0:T(8,128)(2,1)S(1)} %get-tuple-element.107.b_ref.refs_4_.a_ref) | copy-start | bytes 9437188
  133.5 57.1 %collective-permute-start.11 = (f32[1024,256]{1,0:T(8,128)}, f32[1024,256]{1,0:T(8,128)}, u32[]{:S(2)}, u32[]{:S(2)}) collective-permute-start(f32[1024,256]{1,0:T(8,128)} %get-tuple-element.110), channel_id=1, source_target_pairs={{2,0},{3,1},{6,4},{7,5}} | collective-permute-start | bytes 3145736 | tf_op jit(solution)/shard_map/ppermute | solution.py:555
  135.5 51.5 %collective-permute-start = (f32[1024,256]{1,0:T(8,128)S(1)}, f32[1024,256]{1,0:T(8,128)}, u32[]{:S(2)}, u32[]{:S(2)}) collective-permute-start(f32[1024,256]{1,0:T(8,128)S(1)} %get-tuple-element.66), channel_id=1, source_target_pairs={{2,0},{3,1},{6,4},{7,5}} | collective-permute-start | bytes 3145736 | tf_op jit(solution)/shard_map/cond/branch_1_fun/ppermute | solution.py:555
  187.0 22.0 %collective-permute-start.9 = (bf16[2048,768]{1,0:T(8,128)(2,1)}, bf16[2048,768]{1,0:T(8,128)(2,1)S(1)}, u32[]{:S(2)}, u32[]{:S(2)}) collective-permute-start(bf16[2048,768]{1,0:T(8,128)(2,1)} %get-tuple-element.111.a_ref.b_ref), channel_id=1, source_target_pairs={{0,1},{1,0},{2,3},{3,2},{4,5},{5,4},{6,7},{7,6}} | collective-permute-start | bytes 9437192 | tf_op jit(solution)/shard_map/ppermute | solution.py:555
  190.6 22.4 %collective-permute-start.10 = (bf16[2048,768]{1,0:T(8,128)(2,1)}, bf16[2048,768]{1,0:T(8,128)(2,1)}, u32[]{:S(2)}, u32[]{:S(2)}) collective-permute-start(bf16[2048,768]{1,0:T(8,128)(2,1)} %copy-done.11), channel_id=1, source_target_pairs={{0,1},{1,0},{2,3},{3,2},{4,5},{5,4},{6,7},{7,6}} | collective-permute-start | bytes 9437192 | tf_op jit(solution)/shard_map/ppermute | solution.py:555
  194.1 8.0 %collective-permute-start.12 = (bf16[2048,256]{1,0:T(8,128)(2,1)S(1)}, bf16[2048,256]{1,0:T(8,128)(2,1)S(1)}, u32[]{:S(2)}, u32[]{:S(2)}) collective-permute-start(bf16[2048,256]{1,0:T(8,128)(2,1)S(1)} %pad_maximum_fusion.b_ref.c_ref), channel_id=1, source_target_pairs={{0,1},{1,0},{2,3},{3,2},{4,5},{5,4},{6,7},{7,6}} | collective-permute-start | bytes 3145736 | tf_op jit(solution)/shard_map/ppermute | solution.py:555
  203.3 20.4 %collective-permute-start.15 = (f32[4,384,128]{2,1,0:T(8,128)S(1)}, f32[4,384,128]{2,1,0:T(8,128)S(1)}, u32[]{:S(2)}, u32[]{:S(2)}) collective-permute-start(f32[4,384,128]{2,1,0:T(8,128)S(1)} %shard_map.124), channel_id=1, source_target_pairs={{0,2},{2,0},{1,3},{3,1},{4,6},{6,4},{5,7},{7,5}} | collective-permute-start | bytes 2359304 | tf_op jit(solution)/shard_map/ppermute | solution.py:555
  203.3 56.2 %collective-permute-start.16 = (f32[6,384,128]{2,1,0:T(8,128)S(1)}, f32[6,384,128]{2,1,0:T(8,128)S(1)}, u32[]{:S(2)}, u32[]{:S(2)}) collective-permute-start(f32[6,384,128]{2,1,0:T(8,128)S(1)} %copy-done.5), channel_id=1, source_target_pairs={{0,2},{2,0},{1,3},{3,1},{4,6},{6,4},{5,7},{7,5}} | collective-permute-start | bytes 3538952 | tf_op jit(solution)/shard_map/ppermute | solution.py:555
  209.0 116.9 %collective-permute-start.13 = (f32[6,384,128]{2,1,0:T(8,128)S(1)}, f32[6,384,128]{2,1,0:T(8,128)S(1)}, u32[]{:S(2)}, u32[]{:S(2)}) collective-permute-start(f32[6,384,128]{2,1,0:T(8,128)S(1)} %shard_map.127), channel_id=1, source_target_pairs={{0,2},{2,0},{1,3},{3,1},{4,6},{6,4},{5,7},{7,5}} | collective-permute-start | bytes 3538952 | tf_op jit(solution)/shard_map/ppermute | solution.py:555
  211.0 114.9 %collective-permute-start.14 = (f32[6,384,128]{2,1,0:T(8,128)S(1)}, f32[6,384,128]{2,1,0:T(8,128)S(1)}, u32[]{:S(2)}, u32[]{:S(2)}) collective-permute-start(f32[6,384,128]{2,1,0:T(8,128)S(1)} %shard_map.123), channel_id=1, source_target_pairs={{0,2},{2,0},{1,3},{3,1},{4,6},{6,4},{5,7},{7,5}} | collective-permute-start | bytes 3538952 | tf_op jit(solution)/shard_map/ppermute | solution.py:555
  216.7 107.6 %collective-permute-start.17 = (f32[6,384,128]{2,1,0:T(8,128)S(1)}, f32[6,384,128]{2,1,0:T(8,128)S(1)}, u32[]{:S(2)}, u32[]{:S(2)}) collective-permute-start(f32[6,384,128]{2,1,0:T(8,128)S(1)} %shard_map.131), channel_id=1, source_target_pairs={{0,2},{2,0},{1,3},{3,1},{4,6},{6,4},{5,7},{7,5}} | collective-permute-start | bytes 3538952 | tf_op jit(solution)/shard_map/ppermute | solution.py:555
  229.7 10.8 %slice-start.2 = ((s8[4718592]{0:T(1024)(128)(4,1)}), s8[4194304]{0:T(1024)(128)(4,1)S(1)}, s32[]{:S(2)}) async-start(s8[4718592]{0:T(1024)(128)(4,1)} %bitcast.27), calls=%async_computation.2 | async-start | bytes 8388608
  (16 other events, 83.6 us)

commit v5 on v4

--- a/solution.py
+++ b/solution.py
@@ -83,8 +83,8 @@
     def _():
         spread_segments(rows_ref, segk, 0, 2 * HALF)
         first = jnp.where(ids_ref[1] == 0, HALF, 0)
-        ends = [seg_ref[store_block(first + p, core) * BLK + BLK - 1] for p in (HALF // 2 - 1, HALF - 1)]
-        reach_ref[0] = (ends[0] == ends[1]).astype(jnp.int32)
+        ends = [seg_ref[store_block(first + p, core) * BLK + BLK - 1] for p in (3, 5, 7)]
+        reach_ref[0] = (ends[0] == ends[2]).astype(jnp.int32) + (ends[1] == ends[2]).astype(jnp.int32)
 
         for i, part in enumerate((kv_far0, kv_far1, kv_own, kv_oth)):
             kv_ref[i * tok:(i + 1) * tok, :] = part[...]
@@ -179,7 +179,7 @@
 def bwd_kernel(remote, *refs):
     if remote:
         (seg_ref, ids_ref, q_ref, do_ref, o_ref, kv_own, kv_oth,
-         rows_ref, lse_ref, dq_out, dkv_first, dkv_second,
+         rows_ref, lse_ref, dq_out, dkv_first, dkv_second, dkv_third,
          segk, kv_ref, qs, qt, ds_, dt, delta, pm, sm, dqt, dkv_ref) = refs
     else:
         (seg_ref, ids_ref, q_ref, do_ref, o_ref, kv_own, kv_oth,
@@ -249,9 +249,10 @@
 
         @pl.when(step == pl.num_programs(0) - 1)
         def _():
-            tok = dkv_first.shape[0]
-            dkv_first[...] = dkv_ref[:tok, :]
-            dkv_second[...] = dkv_ref[tok:, :]
+            at = 0
+            for part in (dkv_first, dkv_second, dkv_third):
+                part[...] = dkv_ref[at:at + part.shape[0], :]
+                at += part.shape[0]
     else:
         for h in range(HEADS):
             cols = slice(h * BLK, (h + 1) * BLK)
@@ -395,9 +396,10 @@
     kv_spec = pl.BlockSpec((tok, 2 * HD), whole)
     extra = []
     if remote:
-        shard = jax.ShapeDtypeStruct((tok // 2, 2 * HD), jnp.float32)
-        out_shape = [jax.ShapeDtypeStruct((grid, HD, WIDE), jnp.float32), shard, shard]
-        out_specs = [dqt_spec] + [pl.BlockSpec((tok // 2, 2 * HD), whole)] * 2
+        parts = [(n, 2 * HD) for n in (tok // 2, tok // 4, tok // 4)]
+        out_shape = [jax.ShapeDtypeStruct((grid, HD, WIDE), jnp.float32)]
+        out_shape += [jax.ShapeDtypeStruct(part, jnp.float32) for part in parts]
+        out_specs = [dqt_spec] + [pl.BlockSpec(part, whole) for part in parts]
         extra = [pltpu.VMEM((tok, 2 * HD), jnp.float32)]
     else:
         in_specs.append(dqt_spec)
@@ -590,22 +592,23 @@
         dwo_in2 = send(dwo_far2, chip_pairs)
 
         do = project(ids, after(dy, dwo_far), dy_o, w_o)
-        dq_part, dkv_far0, dkv_far1 = attend_grad(True, seg_all, ids, q, do, o, kv_far, seg_rows, lse)
-        dkv_in1 = send(dkv_far1, down_pairs)
-
+        dq_part, *far = attend_grad(True, seg_all, ids, q, do, o, kv_far, seg_rows, lse)
+        last_in = send(far[2], down_pairs)
         local = (seg_all, ids, q, do, o, kv_near, seg_rows, lse, dq_part)
 
-        def sent(first, args):
-            got = send(first, down_pairs)
-            return *attend_grad(False, *args), got
-
-        def kept(first, args):
-            return *attend_grad(False, *args), jnp.zeros_like(first)
-
-        dq, dkv_near, dkv_in0 = lax.cond(reach[0] != 0, sent, kept, dkv_far0, local)
+        def near_pass(level):
+            def run(first, second, x_far, args):
+                second_in = send(second, down_pairs) if level > 0 else jnp.zeros_like(second)
+                first_in = send(first, down_pairs) if level > 1 else jnp.zeros_like(first)
+                dq, dkv = attend_grad(False, *args)
+                return dq, dkv, wgrad_one(x_far, dq, False), first_in, second_in
+
+            return run
+
+        dq, dkv_near, dwq_far1, first_in, second_in = lax.switch(
+            reach[0], [near_pass(level) for level in range(3)], far[0], far[1], x_far, local)
+        dwq_in = send(dwq_far1, chip_pairs)
         dq_p = send(dq, core_pairs)
-        dwq_far1 = wgrad_one(x_far, dq, False)
-        dwq_in = send(dwq_far1, chip_pairs)
         dwq_far = wgrad_one(x_far, dq_p, True)
         dwq_in2 = send(dwq_far, chip_pairs)
 
@@ -615,8 +618,8 @@
         dwo_near = wgrad(core, dy_near, o, o_p)
         dwq_near = wgrad(core, x_near, dq, dq_p)
 
-        dkv = dkv_near + jnp.where(core == 0, jnp.concatenate([dkv_in0, dkv_in1]),
-                                   jnp.concatenate([dkv_in1, dkv_in0]))
+        dkv = dkv_near + jnp.where(core == 0, jnp.concatenate([first_in, second_in, last_in]),
+                                   jnp.concatenate([second_in, last_in, first_in]))
         dkv = jnp.concatenate([dkv[:, :HD] * HD ** -0.5, dkv[:, HD:]], axis=1).astype(jnp.bfloat16)
         dkv_p = send(dkv, core_pairs)
         dwkv_far = wgrad(core, x_far, dkv, dkv_p)

time: 328 us -> 336 us (1.024)
  waiting for transfers between devices: 77.9 us -> 83.5 us
  Pallas kernels: 212 us -> 216 us
    ppermute x18 -> x19, waiting for transfers between devices: 77.9 us -> 83.5 us  [send(): return lax.ppermute(a, 'cp', pairs)]
    ppermute x18 -> x19, starting transfers between devices: 23.5 us -> 21.3 us  [send(): return lax.ppermute(a, 'cp', pairs)]
  transfers between devices with their start and end apart: 18 -> 19, of which waited for: 5 -> 4; matrix products, arithmetic and copies ran while one was open for 2% -> 2% of each run, Pallas kernels for 34% -> 35%
where the time goes in v5:
time: 336 us
  Pallas kernels  216 us (64%)
  waiting for transfers between devices  83.5 us (25%)
  starting transfers between devices  21.3 us (6%)
  other arithmetic  6.86 us (2%)
  local copies, waits for them, and re-layouts  5.79 us (2%)
    ppermute x19, waiting for transfers between devices, send(): return lax.ppermute(a, 'cp', pairs)  83.5 us
    pallas_call x1, Pallas kernels, attend(): pl.pallas_call(fwd_kernel, grid_spec=pltpu.PrefetchScalarGridSpec(num_sca...  79.7 us
    pallas_call x2, Pallas kernels, attend_grad(): pl.pallas_call(functools.partial(bwd_kernel, remote), grid_spec=pltpu.Pre...  53.5 us
    ppermute x19, starting transfers between devices, send(): return lax.ppermute(a, 'cp', pairs)  21.3 us
    pallas_call x2, Pallas kernels, expand(): pl.pallas_call(expand_kv_kernel if extra else expand_kernel, grid_spec=pl...  19 us
    pallas_call x2, Pallas kernels, project(): pl.pallas_call(project_kernel, grid_spec=pltpu.PrefetchScalarGridSpec(num...  16.2 us
    pallas_call x4, Pallas kernels, wgrad(): pl.pallas_call(wgrad_kernel, grid_spec=pltpu.PrefetchScalarGridSpec(num_s...  15.3 us
    pallas_call x4, Pallas kernels, turn(): pl.pallas_call(turn_kernel, grid_spec=pltpu.PrefetchScalarGridSpec(num_sc...  13.5 us
  transfers between devices with their start and end apart: 19, of which 4 were waited for; matrix products, arithmetic and copies ran while one was open for 2% of the time, Pallas kernels for 35%

profile of v5, /device:TPU:0, one launch (start us, length us, event | category | flops | bytes accessed | tf_op | source)
XLA Modules:
  0.0 335.6 jit_solution(7131636083994856463)
XLA Ops:
  0.7 5.7 %project_kv.1 = (bf16[1024,256]{1,0:T(8,128)(2,1)S(1)}, bf16[1024,256]{1,0:T(8,128)(2,1)}, bf16[1536,256]{1,0:T(8,128)(2,1)}, bf16[1536,256]{1,0:T(8,128)(2,1)}) custom-call(s32[2]{0:T(128)S(1)} %pad_add_fusion.1.ids_ref.refs_1_, bf16[1024,1536]{1,0:T(8,128)(2,1)} %a_ref.6, bf16[3072,128]{1,0:T(8,128)(2,1)} %bitcast.39, bf16[3072,128]{1,0:T(8,128)(2,1)} %bitcast.40), custom_call_target="tpu_custom_call" | custom-call | flops 805306368 | bytes 6291456 | tf_op jit(solution)/shard_map/project_kv/pallas_call | solution.py:444
  7.3 4.9 %collective-permute-start.3 = (s32[1024]{0:T(1024)S(1)}, s32[1024]{0:T(1024)S(1)}, u32[]{:S(2)}, u32[]{:S(2)}) collective-permute-start(s32[1024]{0:T(1024)S(1)} %copy-done.15), channel_id=1, source_target_pairs={{0,2},{1,3},{4,6},{5,7}} | collective-permute-start | bytes 12296 | tf_op jit(solution)/shard_map/ppermute | solution.py:557
  13.6 4.1 %collective-permute-start.7 = (bf16[1024,256]{1,0:T(8,128)(2,1)S(1)}, bf16[1024,256]{1,0:T(8,128)(2,1)S(1)}, u32[]{:S(2)}, u32[]{:S(2)}) collective-permute-start(bf16[1024,256]{1,0:T(8,128)(2,1)S(1)} %get-tuple-element.145.kv_own), channel_id=1, source_target_pairs={{0,2},{1,3},{4,6},{5,7}} | collective-permute-start | bytes 1572872 | tf_op jit(solution)/shard_map/ppermute | solution.py:557
  21.1 3.5 %shard_map.120.a_ref = bf16[384,2048]{1,0:T(8,128)(2,1)S(1)} custom-call(s32[1]{0:T(128)} %bitcast.9.ids_ref, bf16[1024,1536]{1,0:T(8,128)(2,1)S(1)} %copy-done.8, bf16[1024,1536]{1,0:T(8,128)(2,1)} %collective-permute-done.10.b_ref.a_oth), custom_call_target="tpu_custom_call" | custom-call | flops 2147483648 | bytes 3145728 | tf_op jit(solution)/shard_map/pallas_call | solution.py:492
  24.6 8.5 %shard_map.118.q_ref.refs_2_ = bf16[2048,768]{1,0:T(8,128)(2,1)S(1)} custom-call(s32[2]{0:T(128)S(1)} %pad_add_fusion.1.ids_ref.refs_1_, bf16[1024,1536]{1,0:T(8,128)(2,1)S(1)} %copy-done.2, bf16[1024,1536]{1,0:T(8,128)(2,1)} %collective-permute-done.6.a_oth.b_ref, bf16[12,1536,128]{2,1,0:T(8,128)(2,1)S(1)} %bitcast.33), custom_call_target="tpu_custom_call" | custom-call | flops 4831838208 | bytes 12582912 | tf_op jit(solution)/shard_map/pallas_call | solution.py:427
  33.1 6.0 %collective-permute-done.8.kv_far1.refs_6_ = bf16[1024,256]{1,0:T(8,128)(2,1)S(1)} collective-permute-done((bf16[1024,256]{1,0:T(8,128)(2,1)}, bf16[1024,256]{1,0:T(8,128)(2,1)S(1)}, u32[]{:S(2)}, u32[]{:S(2)}) %collective-permute-start.8) | collective-permute-done | bytes 524320 | tf_op jit(solution)/shard_map/ppermute | solution.py:557
  39.2 79.7 %attend.1 = (bf16[2048,768]{1,0:T(8,128)(2,1)S(1)}, f32[8,1,1536]{2,1,0:T(1,128)S(1)}, s32[1]{0:T(128)}) custom-call(s32[4096]{0:T(1024)S(1)} %constant_dynamic-update-slice_fusion.seg_ref.refs_0_, s32[2]{0:T(128)S(1)} %pad_add_fusion.1.ids_ref.refs_1_, bf16[2048,768]{1,0:T(8,128)(2,1)S(1)} %shard_map.118.q_ref.refs_2_, ...), custom_call_target="tpu_custom_call" | custom-call | flops 8053063680 | bytes 12582912 | tf_op jit(solution)/shard_map/attend/pallas_call | solution.py:369
  122.0 7.7 %shard_map.122.refs_3_ = bf16[2048,768]{1,0:T(8,128)(2,1)S(1)} custom-call(s32[2]{0:T(128)S(1)} %pad_add_fusion.1.ids_ref.refs_1_, bf16[1024,1536]{1,0:T(8,128)(2,1)S(1)} %copy-done.9, bf16[1024,1536]{1,0:T(8,128)(2,1)} %collective-permute-done.10.b_ref.a_oth, bf16[12,1536,128]{2,1,0:T(8,128)(2,1)S(1)} %bitcast.26), custom_call_target="tpu_custom_call" | custom-call | flops 4831838208 | bytes 12582912 | tf_op jit(solution)/shard_map/pallas_call | solution.py:427
  129.7 3.6 %attend_grad_remote.1 = (f32[8,128,1536]{2,1,0:T(8,128)S(1)}, f32[1024,256]{1,0:T(8,128)S(1)}, f32[512,256]{1,0:T(8,128)S(1)}, f32[512,256]{1,0:T(8,128)}) custom-call(s32[4096]{0:T(1024)S(1)} %constant_dynamic-update-slice_fusion.seg_ref.refs_0_, s32[2]{0:T(128)S(1)} %pad_add_fusion.1.ids_ref.refs_1_, bf16[2048,768]{1,0:T(8,128)(2,1)S(1)} %shard_map.118.q_ref.refs_2_, ...), custom_call_target="tpu_custom_call" | custom-call | flops 10066329600 | bytes 20971520 | tf_op jit(solution)/shard_map/attend_grad_remote/pallas_call | solution.py:412
  134.6 3.9 %shard_map.119.a_ref = bf16[384,2048]{1,0:T(8,128)(2,1)} custom-call(s32[1]{0:T(128)} %bitcast.9.ids_ref, bf16[1024,1536]{1,0:T(8,128)(2,1)S(1)} %copy-done.2, bf16[1024,1536]{1,0:T(8,128)(2,1)} %collective-permute-done.6.a_oth.b_ref), custom_call_target="tpu_custom_call" | custom-call | flops 2147483648 | bytes 3145728 | tf_op jit(solution)/shard_map/pallas_call | solution.py:492
  139.2 56.9 %conditional.1 = (bf16[2048,768]{1,0:T(8,128)(2,1)}, f32[2048,256]{1,0:T(8,128)}, f32[6,384,128]{2,1,0:T(8,128)S(1)}, f32[1024,256]{1,0:T(8,128)}, f32[512,256]{1,0:T(8,128)}) conditional(s32[]{:T(128)} %bitcast.10, (s32[4096]{0:T(1024)S(1)}, s32[2]{0:T(128)S(1)}, bf16[2048,768]{1,0:T(8,128)(2,1)S(1)}, ...), branch_computations={%region_0.1_spmd, %region_1.2_spmd, %region_2.3_spmd} | conditional | flops 11274289152 | bytes 33554552 | solution.py:608
  141.8 49.9 %attend_grad_local.5 = (bf16[2048,768]{1,0:T(8,128)(2,1)}, f32[2048,256]{1,0:T(8,128)}) custom-call(s32[4096]{0:T(1024)S(1)} %get-tuple-element.99.refs_0_, s32[2]{0:T(128)S(1)} %get-tuple-element.100.refs_1_, bf16[2048,768]{1,0:T(8,128)(2,1)S(1)} %get-tuple-element.101.refs_2_, bf16[2048,768]{1,0:T(8,128)(2,1)S(1)} %get-tuple-element.102.refs_3_, ...), custom_call_target="tpu_custom_call" | custom-call | flops 10066329600 | bytes 20971520 | tf_op jit(solution)/shard_map/cond/branch_2_fun/attend_grad_local/pallas_call | solution.py:412
  191.7 4.1 %branch_2_fun.1 = f32[6,384,128]{2,1,0:T(8,128)S(1)} custom-call(bf16[384,2048]{1,0:T(8,128)(2,1)} %get-tuple-element.111.a_ref, bf16[2048,768]{1,0:T(8,128)(2,1)} %get-tuple-element.184.b_ref), custom_call_target="tpu_custom_call" | custom-call | flops 1207959552 | bytes 6291456 | tf_op jit(solution)/shard_map/cond/branch_2_fun/pallas_call | solution.py:530
  197.6 3.2 fusion.4
  201.2 7.8 %collective-permute-done.14.c_ref.d_ref = bf16[2048,256]{1,0:T(8,128)(2,1)S(1)} collective-permute-done((bf16[2048,256]{1,0:T(8,128)(2,1)S(1)}, bf16[2048,256]{1,0:T(8,128)(2,1)S(1)}, u32[]{:S(2)}, u32[]{:S(2)}) %collective-permute-start.14) | collective-permute-done | bytes 1048608 | tf_op jit(solution)/shard_map/ppermute | solution.py:557
  213.7 3.4 %shard_map.123 = f32[6,384,128]{2,1,0:T(8,128)S(1)} custom-call(bf16[384,2048]{1,0:T(8,128)(2,1)} %shard_map.119.a_ref, bf16[2048,768]{1,0:T(8,128)(2,1)S(1)} %collective-permute-done.11.b_ref.c_ref), custom_call_target="tpu_custom_call" | custom-call | flops 1207959552 | bytes 6291456 | tf_op jit(solution)/shard_map/pallas_call | solution.py:530
  219.0 3.6 %shard_map.130 = f32[6,384,128]{2,1,0:T(8,128)S(1)} custom-call(bf16[384,2048]{1,0:T(8,128)(2,1)S(1)} %copy-done.1, bf16[2048,768]{1,0:T(8,128)(2,1)} %collective-permute-done.12.b_ref.c_ref), custom_call_target="tpu_custom_call" | custom-call | flops 1207959552 | bytes 6291456 | tf_op jit(solution)/shard_map/pallas_call | solution.py:530
  226.9 5.2 %collective-permute-done.17 = f32[4,384,128]{2,1,0:T(8,128)S(1)} collective-permute-done((f32[4,384,128]{2,1,0:T(8,128)S(1)}, f32[4,384,128]{2,1,0:T(8,128)S(1)}, u32[]{:S(2)}, u32[]{:S(2)}) %collective-permute-start.17) | collective-permute-done | bytes 786464 | tf_op jit(solution)/shard_map/ppermute | solution.py:557
  232.2 5.8 %shard_map.126 = f32[12,384,128]{2,1,0:T(8,128)S(1)} custom-call(s32[1]{0:T(128)} %bitcast.ids_ref, bf16[384,2048]{1,0:T(8,128)(2,1)S(1)} %shard_map.125.a_ref, bf16[2048,768]{1,0:T(8,128)(2,1)} %get-tuple-element.163.a_ref.b_ref, bf16[2048,768]{1,0:T(8,128)(2,1)S(1)} %collective-permute-done.11.b_ref.c_ref), custom_call_target="tpu_custom_call" | custom-call | flops 2415919104 | bytes 10485760 | tf_op jit(solution)/shard_map/pallas_call | solution.py:511
  238.0 3.4 %shard_map.128.a_ref = bf16[384,2048]{1,0:T(8,128)(2,1)S(1)} custom-call(s32[1]{0:T(128)} %bitcast.12.ids_ref, bf16[1024,1536]{1,0:T(8,128)(2,1)S(1)} %copy-done.10, bf16[1024,1536]{1,0:T(8,128)(2,1)} %collective-permute-done.10.b_ref.a_oth), custom_call_target="tpu_custom_call" | custom-call | flops 2147483648 | bytes 3145728 | tf_op jit(solution)/shard_map/pallas_call | solution.py:492
  241.5 5.7 %shard_map.129 = f32[12,384,128]{2,1,0:T(8,128)S(1)} custom-call(s32[1]{0:T(128)} %bitcast.ids_ref, bf16[384,2048]{1,0:T(8,128)(2,1)S(1)} %shard_map.128.a_ref, bf16[2048,768]{1,0:T(8,128)(2,1)S(1)} %copy-done.12, bf16[2048,768]{1,0:T(8,128)(2,1)} %collective-permute-done.12.b_ref.c_ref), custom_call_target="tpu_custom_call" | custom-call | flops 2415919104 | bytes 10485760 | tf_op jit(solution)/shard_map/pallas_call | solution.py:511
  248.8 8.7 %out_y.1 = bf16[1024,1536]{1,0:T(8,128)(2,1)} custom-call(s32[2]{0:T(128)S(1)} %pad_add_fusion.1.ids_ref.refs_1_, bf16[2048,768]{1,0:T(8,128)(2,1)S(1)} %copy-done.12, bf16[2048,768]{1,0:T(8,128)(2,1)} %collective-permute-done.12.b_ref.c_ref, bf16[12,1536,128]{2,1,0:T(8,128)(2,1)S(1)} %bitcast.29, bf16[12,1536,128]{2,1,0:T(8,128)(2,1)S(1)} %bitcast.30), custom_call_target="tpu_custom_call" | custom-call | flops 4831838208 | bytes 14680064 | tf_op jit(solution)/shard_map/out_y/pallas_call | solution.py:477
  257.5 10.3 %grad_x.1 = bf16[1024,1536]{1,0:T(8,128)(2,1)} custom-call(s32[2]{0:T(128)S(1)} %pad_add_fusion.1.ids_ref.refs_1_, bf16[2048,768]{1,0:T(8,128)(2,1)} %get-tuple-element.163.a_ref.b_ref, bf16[2048,768]{1,0:T(8,128)(2,1)S(1)} %collective-permute-done.11.b_ref.c_ref, bf16[12,1536,128]{2,1,0:T(8,128)(2,1)S(1)} %bitcast.36, bf16[12,1536,128]{2,1,0:T(8,128)(2,1)S(1)} %bitcast.37, ...), custom_call_target="tpu_custom_call" | custom-call | flops 4831838208 | bytes 14680064 | tf_op jit(solution)/shard_map/grad_x/pallas_call | solution.py:477
  267.8 64.5 %collective-permute-done.19 = f32[6,384,128]{2,1,0:T(8,128)S(1)} collective-permute-done((f32[6,384,128]{2,1,0:T(8,128)S(1)}, f32[6,384,128]{2,1,0:T(8,128)S(1)}, u32[]{:S(2)}, u32[]{:S(2)}) %collective-permute-start.19) | collective-permute-done | bytes 1179680 | tf_op jit(solution)/shard_map/ppermute | solution.py:557
  (102 shorter events, 30.3 us)
Async XLA Ops:
  0.7 23.9 %slice-start.4 = ((s8[4718592]{0:T(1024)(128)(4,1)}), s8[524288]{0:T(1024)(128)(4,1)S(1)}, s32[]{:S(2)}) async-start(s8[4718592]{0:T(1024)(128)(4,1)} %bitcast.31), calls=%async_computation.4 | async-start | bytes 1048576
  6.4 12.7 %collective-permute-start.10 = (bf16[1024,1536]{1,0:T(8,128)(2,1)}, bf16[1024,1536]{1,0:T(8,128)(2,1)}, u32[]{:S(2)}, u32[]{:S(2)}) collective-permute-start(bf16[1024,1536]{1,0:T(8,128)(2,1)} %a_ref.7), channel_id=1, source_target_pairs={{0,1},{1,0},{2,3},{3,2},{4,5},{5,4},{6,7},{7,6}} | collective-permute-start | bytes 9437192 | tf_op jit(solution)/shard_map/ppermute | solution.py:557
  7.3 17.3 %collective-permute-start.6 = (bf16[1024,1536]{1,0:T(8,128)(2,1)}, bf16[1024,1536]{1,0:T(8,128)(2,1)}, u32[]{:S(2)}, u32[]{:S(2)}) collective-permute-start(bf16[1024,1536]{1,0:T(8,128)(2,1)} %a_ref.6), channel_id=1, source_target_pairs={{0,1},{1,0},{2,3},{3,2},{4,5},{5,4},{6,7},{7,6}} | collective-permute-start | bytes 9437192 | tf_op jit(solution)/shard_map/ppermute | solution.py:557
  7.3 6.3 %collective-permute-start.3 = (s32[1024]{0:T(1024)S(1)}, s32[1024]{0:T(1024)S(1)}, u32[]{:S(2)}, u32[]{:S(2)}) collective-permute-start(s32[1024]{0:T(1024)S(1)} %copy-done.15), channel_id=1, source_target_pairs={{0,2},{1,3},{4,6},{5,7}} | collective-permute-start | bytes 12296 | tf_op jit(solution)/shard_map/ppermute | solution.py:557
  12.1 5.5 %collective-permute-start.4 = (s32[1024]{0:T(1024)S(1)}, s32[1024]{0:T(1024)S(1)}, u32[]{:S(2)}, u32[]{:S(2)}) collective-permute-start(s32[1024]{0:T(1024)S(1)} %copy-done.15), channel_id=1, source_target_pairs={{0,3},{1,2},{4,7},{5,6}} | collective-permute-start | bytes 12296 | tf_op jit(solution)/shard_map/ppermute | solution.py:557
  13.4 5.6 %collective-permute-start.5 = (s32[1024]{0:T(1024)S(1)}, s32[1024]{0:T(1024)S(1)}, u32[]{:S(2)}, u32[]{:S(2)}) collective-permute-start(s32[1024]{0:T(1024)S(1)} %copy-done.15), channel_id=1, source_target_pairs={{0,1},{1,0},{2,3},{3,2},{4,5},{5,4},{6,7},{7,6}} | collective-permute-start | bytes 12296 | tf_op jit(solution)/shard_map/ppermute | solution.py:557
  13.6 19.6 %collective-permute-start.7 = (bf16[1024,256]{1,0:T(8,128)(2,1)S(1)}, bf16[1024,256]{1,0:T(8,128)(2,1)S(1)}, u32[]{:S(2)}, u32[]{:S(2)}) collective-permute-start(bf16[1024,256]{1,0:T(8,128)(2,1)S(1)} %get-tuple-element.145.kv_own), channel_id=1, source_target_pairs={{0,2},{1,3},{4,6},{5,7}} | collective-permute-start | bytes 1572872 | tf_op jit(solution)/shard_map/ppermute | solution.py:557
  17.7 21.5 %collective-permute-start.8 = (bf16[1024,256]{1,0:T(8,128)(2,1)}, bf16[1024,256]{1,0:T(8,128)(2,1)S(1)}, u32[]{:S(2)}, u32[]{:S(2)}) collective-permute-start(bf16[1024,256]{1,0:T(8,128)(2,1)} %get-tuple-element.148), channel_id=1, source_target_pairs={{0,3},{1,2},{4,7},{5,6}} | collective-permute-start | bytes 1572872 | tf_op jit(solution)/shard_map/ppermute | solution.py:557
  19.1 20.1 %collective-permute-start.9 = (bf16[1024,256]{1,0:T(8,128)(2,1)}, bf16[1024,256]{1,0:T(8,128)(2,1)S(1)}, u32[]{:S(2)}, u32[]{:S(2)}) collective-permute-start(bf16[1024,256]{1,0:T(8,128)(2,1)} %get-tuple-element.148), channel_id=1, source_target_pairs={{0,1},{1,0},{2,3},{3,2},{4,5},{5,4},{6,7},{7,6}} | collective-permute-start | bytes 1572872 | tf_op jit(solution)/shard_map/ppermute | solution.py:557
  24.6 94.3 %copy-start = (bf16[384,2048]{1,0:T(8,128)(2,1)}, bf16[384,2048]{1,0:T(8,128)(2,1)S(1)}, u32[]{:S(2)}) copy-start(bf16[384,2048]{1,0:T(8,128)(2,1)S(1)} %shard_map.120.a_ref) | copy-start | bytes 4718596
  24.6 97.3 %slice-start = ((s8[4718592]{0:T(1024)(128)(4,1)}), s8[4194304]{0:T(1024)(128)(4,1)S(1)}, s32[]{:S(2)}) async-start(s8[4718592]{0:T(1024)(128)(4,1)} %bitcast.24), calls=%async_computation | async-start | bytes 8388608
  33.1 88.8 %slice-start.1 = ((s8[4718592]{0:T(1024)(128)(4,1)}), s8[524288]{0:T(1024)(128)(4,1)S(1)}, s32[]{:S(2)}) async-start(s8[4718592]{0:T(1024)(128)(4,1)} %bitcast.24), calls=%async_computation.1 | async-start | bytes 1048576
  118.8 20.3 %copy-start.11 = (bf16[2048,768]{1,0:T(8,128)(2,1)}, bf16[2048,768]{1,0:T(8,128)(2,1)S(1)}, u32[]{:S(2)}) copy-start(bf16[2048,768]{1,0:T(8,128)(2,1)S(1)} %get-tuple-element.158.b_ref.refs_4_.a_ref) | copy-start | bytes 9437188
  133.4 64.3 %collective-permute-start.13 = (f32[512,256]{1,0:T(8,128)}, f32[512,256]{1,0:T(8,128)}, u32[]{:S(2)}, u32[]{:S(2)}) collective-permute-start(f32[512,256]{1,0:T(8,128)} %get-tuple-element.162), channel_id=1, source_target_pairs={{2,0},{3,1},{6,4},{7,5}} | collective-permute-start | bytes 1572872 | tf_op jit(solution)/shard_map/ppermute | solution.py:557
  139.2 56.6 %collective-permute-start.1 = (f32[1024,256]{1,0:T(8,128)S(1)}, f32[1024,256]{1,0:T(8,128)}, u32[]{:S(2)}, u32[]{:S(2)}) collective-permute-start(f32[1024,256]{1,0:T(8,128)S(1)} %get-tuple-element.112), channel_id=1, source_target_pairs={{2,0},{3,1},{6,4},{7,5}} | collective-permute-start | bytes 3145736 | tf_op jit(solution)/shard_map/cond/branch_2_fun/ppermute | solution.py:557
  140.5 55.3 %collective-permute-start.2 = (f32[512,256]{1,0:T(8,128)S(1)}, f32[512,256]{1,0:T(8,128)}, u32[]{:S(2)}, u32[]{:S(2)}) collective-permute-start(f32[512,256]{1,0:T(8,128)S(1)} %get-tuple-element.113), channel_id=1, source_target_pairs={{2,0},{3,1},{6,4},{7,5}} | collective-permute-start | bytes 1572872 | tf_op jit(solution)/shard_map/cond/branch_2_fun/ppermute | solution.py:557
  197.1 16.6 %collective-permute-start.11 = (bf16[2048,768]{1,0:T(8,128)(2,1)}, bf16[2048,768]{1,0:T(8,128)(2,1)S(1)}, u32[]{:S(2)}, u32[]{:S(2)}) collective-permute-start(bf16[2048,768]{1,0:T(8,128)(2,1)} %get-tuple-element.163.a_ref.b_ref), channel_id=1, source_target_pairs={{0,1},{1,0},{2,3},{3,2},{4,5},{5,4},{6,7},{7,6}} | collective-permute-start | bytes 9437192 | tf_op jit(solution)/shard_map/ppermute | solution.py:557
  197.1 21.9 %collective-permute-start.12 = (bf16[2048,768]{1,0:T(8,128)(2,1)}, bf16[2048,768]{1,0:T(8,128)(2,1)}, u32[]{:S(2)}, u32[]{:S(2)}) collective-permute-start(bf16[2048,768]{1,0:T(8,128)(2,1)} %copy-done.11), channel_id=1, source_target_pairs={{0,1},{1,0},{2,3},{3,2},{4,5},{5,4},{6,7},{7,6}} | collective-permute-start | bytes 9437192 | tf_op jit(solution)/shard_map/ppermute | solution.py:557
  201.1 7.8 %collective-permute-start.14 = (bf16[2048,256]{1,0:T(8,128)(2,1)S(1)}, bf16[2048,256]{1,0:T(8,128)(2,1)S(1)}, u32[]{:S(2)}, u32[]{:S(2)}) collective-permute-start(bf16[2048,256]{1,0:T(8,128)(2,1)S(1)} %pad_maximum_fusion.b_ref.c_ref), channel_id=1, source_target_pairs={{0,1},{1,0},{2,3},{3,2},{4,5},{5,4},{6,7},{7,6}} | collective-permute-start | bytes 3145736 | tf_op jit(solution)/shard_map/ppermute | solution.py:557
  211.6 20.4 %collective-permute-start.17 = (f32[4,384,128]{2,1,0:T(8,128)S(1)}, f32[4,384,128]{2,1,0:T(8,128)S(1)}, u32[]{:S(2)}, u32[]{:S(2)}) collective-permute-start(f32[4,384,128]{2,1,0:T(8,128)S(1)} %shard_map.124), channel_id=1, source_target_pairs={{0,2},{2,0},{1,3},{3,1},{4,6},{6,4},{5,7},{7,5}} | collective-permute-start | bytes 2359304 | tf_op jit(solution)/shard_map/ppermute | solution.py:557
  211.6 56.2 %collective-permute-start.18 = (f32[6,384,128]{2,1,0:T(8,128)S(1)}, f32[6,384,128]{2,1,0:T(8,128)S(1)}, u32[]{:S(2)}, u32[]{:S(2)}) collective-permute-start(f32[6,384,128]{2,1,0:T(8,128)S(1)} %copy-done.5), channel_id=1, source_target_pairs={{0,2},{2,0},{1,3},{3,1},{4,6},{6,4},{5,7},{7,5}} | collective-permute-start | bytes 3538952 | tf_op jit(solution)/shard_map/ppermute | solution.py:557
  213.6 120.3 %collective-permute-start.15 = (f32[6,384,128]{2,1,0:T(8,128)S(1)}, f32[6,384,128]{2,1,0:T(8,128)S(1)}, u32[]{:S(2)}, u32[]{:S(2)}) collective-permute-start(f32[6,384,128]{2,1,0:T(8,128)S(1)} %copy-done.14), channel_id=1, source_target_pairs={{0,2},{2,0},{1,3},{3,1},{4,6},{6,4},{5,7},{7,5}} | collective-permute-start | bytes 3538952 | tf_op jit(solution)/shard_map/ppermute | solution.py:557
  217.1 116.8 %collective-permute-start.16 = (f32[6,384,128]{2,1,0:T(8,128)S(1)}, f32[6,384,128]{2,1,0:T(8,128)S(1)}, u32[]{:S(2)}, u32[]{:S(2)}) collective-permute-start(f32[6,384,128]{2,1,0:T(8,128)S(1)} %shard_map.123), channel_id=1, source_target_pairs={{0,2},{2,0},{1,3},{3,1},{4,6},{6,4},{5,7},{7,5}} | collective-permute-start | bytes 3538952 | tf_op jit(solution)/shard_map/ppermute | solution.py:557
  222.7 109.6 %collective-permute-start.19 = (f32[6,384,128]{2,1,0:T(8,128)S(1)}, f32[6,384,128]{2,1,0:T(8,128)S(1)}, u32[]{:S(2)}, u32[]{:S(2)}) collective-permute-start(f32[6,384,128]{2,1,0:T(8,128)S(1)} %shard_map.130), channel_id=1, source_target_pairs={{0,2},{2,0},{1,3},{3,1},{4,6},{6,4},{5,7},{7,5}} | collective-permute-start | bytes 3538952 | tf_op jit(solution)/shard_map/ppermute | solution.py:557
  (19 other events, 118.7 us)

commit v6 on v5

--- a/solution.py
+++ b/solution.py
@@ -21,11 +21,6 @@
 
 def dot_nt(a, b):
     return lax.dot_general(a, b, (((1,), (1,)), ((), ())), preferred_element_type=jnp.float32)
-
-
-def stack_heads(src, dst):
-    for h in range(HEADS):
-        dst[h * BLK:(h + 1) * BLK, :] = src[:, h * HD:(h + 1) * HD]
 
 
 def flip_heads(src, dst):
@@ -180,11 +175,11 @@
     if remote:
         (seg_ref, ids_ref, q_ref, do_ref, o_ref, kv_own, kv_oth,
          rows_ref, lse_ref, dq_out, dkv_first, dkv_second, dkv_third,
-         segk, kv_ref, qs, qt, ds_, dt, delta, pm, sm, dqt, dkv_ref) = refs
+         segk, kv_ref, qt, dt, delta, pmt, smt, sm, dqt, dkvt) = refs
     else:
         (seg_ref, ids_ref, q_ref, do_ref, o_ref, kv_own, kv_oth,
          rows_ref, lse_ref, dq_in, dq_out, dkv_ref,
-         segk, kv_ref, qs, qt, ds_, dt, delta, pm, sm, dqt) = refs
+         segk, kv_ref, qt, dt, delta, pmt, smt, sm, dqt, dkvt) = refs
     step = pl.program_id(0)
     core = ids_ref[0]
     scale = HD ** -0.5
@@ -192,7 +187,7 @@
 
     @pl.when(step == 0)
     def _():
-        dkv_ref[...] = jnp.zeros_like(dkv_ref)
+        dkvt[...] = jnp.zeros_like(dkvt)
         spread_segments(rows_ref, segk, 0 if remote else HALF, HALF)
         tok = kv_own.shape[0]
         kv_ref[:tok, :] = kv_own[...]
@@ -209,9 +204,7 @@
 
     @pl.when(count > 0)
     def _():
-        stack_heads(q_ref, qs)
         flip_heads(q_ref, qt)
-        stack_heads(do_ref, ds_)
         flip_heads(do_ref, dt)
         for h in range(HEADS):
             hc = slice(h * HD, (h + 1) * HD)
@@ -235,24 +228,28 @@
             w = jnp.where(mask, jnp.exp2(s * scale2 - lse_ref[0, :, cols]), 0.0)
             dp = dot(v_blk, dt[:, cols])
             dsv = w * (dp - delta[:, cols])
-            pm[:, cols] = w.astype(jnp.bfloat16)
-            sm[:, cols] = dsv.astype(jnp.bfloat16)
+            pmt[cols, :] = w.astype(jnp.bfloat16).T
+            ds_half = dsv.astype(jnp.bfloat16)
+            sm[:, cols] = ds_half
+            smt[cols, :] = ds_half.T
         put = pl.multiple_of(p * BLK, BLK) if remote else key_start
-        dkv_ref[pl.ds(put, BLK), HD:] += dot(pm[...], ds_[...])
-        dkv_ref[pl.ds(put, BLK), :HD] += dot(sm[...], qs[...])
+        dkvt[HD:, pl.ds(put, BLK)] += dot(dt[...], pmt[...])
+        dkvt[:HD, pl.ds(put, BLK)] += dot(qt[...], smt[...])
         dqt[...] += dot(k_blk.T, sm[...])
         return carry
 
     lax.fori_loop(0, count, body, 0)
+
+    @pl.when(step == pl.num_programs(0) - 1)
+    def _():
+        at = 0
+        for part in (dkv_first, dkv_second, dkv_third) if remote else (dkv_ref,):
+            for t in range(0, part.shape[0], BLK):
+                part[t:t + BLK, :] = dkvt[:, at + t:at + t + BLK].T
+            at += part.shape[0]
+
     if remote:
         dq_out[0] = dqt[...]
-
-        @pl.when(step == pl.num_programs(0) - 1)
-        def _():
-            at = 0
-            for part in (dkv_first, dkv_second, dkv_third):
-                part[...] = dkv_ref[at:at + part.shape[0], :]
-                at += part.shape[0]
     else:
         for h in range(HEADS):
             cols = slice(h * BLK, (h + 1) * BLK)
@@ -394,28 +391,26 @@
     dqt_spec = pl.BlockSpec((1, HD, WIDE), lead)
     kv_grad = jax.ShapeDtypeStruct((tok, 2 * HD), jnp.float32)
     kv_spec = pl.BlockSpec((tok, 2 * HD), whole)
-    extra = []
     if remote:
         parts = [(n, 2 * HD) for n in (tok // 2, tok // 4, tok // 4)]
         out_shape = [jax.ShapeDtypeStruct((grid, HD, WIDE), jnp.float32)]
         out_shape += [jax.ShapeDtypeStruct(part, jnp.float32) for part in parts]
         out_specs = [dqt_spec] + [pl.BlockSpec(part, whole) for part in parts]
-        extra = [pltpu.VMEM((tok, 2 * HD), jnp.float32)]
     else:
         in_specs.append(dqt_spec)
         args.append(dq_in)
         out_shape = [jax.ShapeDtypeStruct((tok, HEADS * HD), jnp.bfloat16), kv_grad]
         out_specs = [block, kv_spec]
-    stack = pltpu.VMEM((WIDE, HD), jnp.bfloat16)
     flip = pltpu.VMEM((HD, WIDE), jnp.bfloat16)
-    tile = pltpu.VMEM((BLK, WIDE), jnp.bfloat16)
+    turned = pltpu.VMEM((WIDE, BLK), jnp.bfloat16)
     return pl.pallas_call(
         functools.partial(bwd_kernel, remote),
         grid_spec=pltpu.PrefetchScalarGridSpec(
             num_scalar_prefetch=2, grid=(grid,), in_specs=in_specs, out_specs=out_specs,
             scratch_shapes=[pltpu.VMEM((tok, 128), jnp.int32), pltpu.VMEM((tok, 2 * HD), jnp.bfloat16),
-                            stack, flip, stack, flip, pltpu.VMEM((1, WIDE), jnp.float32),
-                            tile, tile, pltpu.VMEM((HD, WIDE), jnp.float32)] + extra),
+                            flip, flip, pltpu.VMEM((1, WIDE), jnp.float32), turned, turned,
+                            pltpu.VMEM((BLK, WIDE), jnp.bfloat16), pltpu.VMEM((HD, WIDE), jnp.float32),
+                            pltpu.VMEM((2 * HD, tok), jnp.float32)]),
         out_shape=out_shape, compiler_params=params(28),
         name='attend_grad_remote' if remote else 'attend_grad_local',
         cost_estimate=pl.CostEstimate(flops=20 * 10 * WIDE * BLK * HD, bytes_accessed=20 << 20, transcendentals=0),

time: 336 us -> 332 us (0.988)
  Pallas kernels: 216 us -> 212 us
    pallas_call x2, Pallas kernels: 53.5 us -> 49.2 us  [attend_grad(): pl.pallas_call(functools.partial(bwd_kernel, remote), grid_spec=pltpu.Pre...]
  transfers between devices with their start and end apart: 19 -> 19, of which waited for: 4 -> 4; matrix products, arithmetic and copies ran while one was open for 2% -> 2% of each run, Pallas kernels for 35% -> 34%
where the time goes in v6:
time: 332 us; the launch traced here: 331 us
  Pallas kernels  212 us (64%)
  waiting for transfers between devices  83.5 us (25%)
  starting transfers between devices  21.3 us (6%)
  other arithmetic  6.86 us (2%)
  local copies, waits for them, and re-layouts  5.79 us (2%)
    ppermute x19, waiting for transfers between devices, send(): return lax.ppermute(a, 'cp', pairs)  83.5 us
    pallas_call x1, Pallas kernels, attend(): pl.pallas_call(fwd_kernel, grid_spec=pltpu.PrefetchScalarGridSpec(num_sca...  79.7 us
    pallas_call x2, Pallas kernels, attend_grad(): pl.pallas_call(functools.partial(bwd_kernel, remote), grid_spec=pltpu.Pre...  49.2 us
    ppermute x19, starting transfers between devices, send(): return lax.ppermute(a, 'cp', pairs)  21.3 us
    pallas_call x2, Pallas kernels, expand(): pl.pallas_call(expand_kv_kernel if extra else expand_kernel, grid_spec=pl...  19 us
    pallas_call x2, Pallas kernels, project(): pl.pallas_call(project_kernel, grid_spec=pltpu.PrefetchScalarGridSpec(num...  16.2 us
    pallas_call x4, Pallas kernels, wgrad(): pl.pallas_call(wgrad_kernel, grid_spec=pltpu.PrefetchScalarGridSpec(num_s...  15.3 us
    pallas_call x4, Pallas kernels, turn(): pl.pallas_call(turn_kernel, grid_spec=pltpu.PrefetchScalarGridSpec(num_sc...  13.5 us
  transfers between devices with their start and end apart: 19, of which 4 were waited for; matrix products, arithmetic and copies ran while one was open for 2% of the time, Pallas kernels for 34%

profile of v6, /device:TPU:0, one launch (start us, length us, event | category | flops | bytes accessed | tf_op | source)
XLA Modules:
  0.0 331.3 jit_solution(6108756138788478552)
XLA Ops:
  0.7 5.7 %project_kv.1 = (bf16[1024,256]{1,0:T(8,128)(2,1)S(1)}, bf16[1024,256]{1,0:T(8,128)(2,1)}, bf16[1536,256]{1,0:T(8,128)(2,1)}, bf16[1536,256]{1,0:T(8,128)(2,1)}) custom-call(s32[2]{0:T(128)S(1)} %pad_add_fusion.1.ids_ref.refs_1_, bf16[1024,1536]{1,0:T(8,128)(2,1)} %a_ref.6, bf16[3072,128]{1,0:T(8,128)(2,1)} %bitcast.39, bf16[3072,128]{1,0:T(8,128)(2,1)} %bitcast.40), custom_call_target="tpu_custom_call" | custom-call | flops 805306368 | bytes 6291456 | tf_op jit(solution)/shard_map/project_kv/pallas_call | solution.py:439
  7.3 4.9 %collective-permute-start.3 = (s32[1024]{0:T(1024)S(1)}, s32[1024]{0:T(1024)S(1)}, u32[]{:S(2)}, u32[]{:S(2)}) collective-permute-start(s32[1024]{0:T(1024)S(1)} %copy-done.15), channel_id=1, source_target_pairs={{0,2},{1,3},{4,6},{5,7}} | collective-permute-start | bytes 12296 | tf_op jit(solution)/shard_map/ppermute | solution.py:552
  13.6 4.1 %collective-permute-start.7 = (bf16[1024,256]{1,0:T(8,128)(2,1)S(1)}, bf16[1024,256]{1,0:T(8,128)(2,1)S(1)}, u32[]{:S(2)}, u32[]{:S(2)}) collective-permute-start(bf16[1024,256]{1,0:T(8,128)(2,1)S(1)} %get-tuple-element.145.kv_own), channel_id=1, source_target_pairs={{0,2},{1,3},{4,6},{5,7}} | collective-permute-start | bytes 1572872 | tf_op jit(solution)/shard_map/ppermute | solution.py:552
  21.1 3.5 %shard_map.120.a_ref = bf16[384,2048]{1,0:T(8,128)(2,1)S(1)} custom-call(s32[1]{0:T(128)} %bitcast.9.ids_ref, bf16[1024,1536]{1,0:T(8,128)(2,1)S(1)} %copy-done.8, bf16[1024,1536]{1,0:T(8,128)(2,1)} %collective-permute-done.10.b_ref.a_oth), custom_call_target="tpu_custom_call" | custom-call | flops 2147483648 | bytes 3145728 | tf_op jit(solution)/shard_map/pallas_call | solution.py:487
  24.6 8.5 %shard_map.118.q_ref.refs_2_ = bf16[2048,768]{1,0:T(8,128)(2,1)S(1)} custom-call(s32[2]{0:T(128)S(1)} %pad_add_fusion.1.ids_ref.refs_1_, bf16[1024,1536]{1,0:T(8,128)(2,1)S(1)} %copy-done.2, bf16[1024,1536]{1,0:T(8,128)(2,1)} %collective-permute-done.6.a_oth.b_ref, bf16[12,1536,128]{2,1,0:T(8,128)(2,1)S(1)} %bitcast.33), custom_call_target="tpu_custom_call" | custom-call | flops 4831838208 | bytes 12582912 | tf_op jit(solution)/shard_map/pallas_call | solution.py:422
  33.1 6.0 %collective-permute-done.8.kv_far1.refs_6_ = bf16[1024,256]{1,0:T(8,128)(2,1)S(1)} collective-permute-done((bf16[1024,256]{1,0:T(8,128)(2,1)}, bf16[1024,256]{1,0:T(8,128)(2,1)S(1)}, u32[]{:S(2)}, u32[]{:S(2)}) %collective-permute-start.8) | collective-permute-done | bytes 524320 | tf_op jit(solution)/shard_map/ppermute | solution.py:552
  39.2 79.7 %attend.1 = (bf16[2048,768]{1,0:T(8,128)(2,1)S(1)}, f32[8,1,1536]{2,1,0:T(1,128)S(1)}, s32[1]{0:T(128)}) custom-call(s32[4096]{0:T(1024)S(1)} %constant_dynamic-update-slice_fusion.seg_ref.refs_0_, s32[2]{0:T(128)S(1)} %pad_add_fusion.1.ids_ref.refs_1_, bf16[2048,768]{1,0:T(8,128)(2,1)S(1)} %shard_map.118.q_ref.refs_2_, ...), custom_call_target="tpu_custom_call" | custom-call | flops 8053063680 | bytes 12582912 | tf_op jit(solution)/shard_map/attend/pallas_call | solution.py:366
  122.0 7.7 %shard_map.122.refs_3_ = bf16[2048,768]{1,0:T(8,128)(2,1)S(1)} custom-call(s32[2]{0:T(128)S(1)} %pad_add_fusion.1.ids_ref.refs_1_, bf16[1024,1536]{1,0:T(8,128)(2,1)S(1)} %copy-done.9, bf16[1024,1536]{1,0:T(8,128)(2,1)} %collective-permute-done.10.b_ref.a_oth, bf16[12,1536,128]{2,1,0:T(8,128)(2,1)S(1)} %bitcast.26), custom_call_target="tpu_custom_call" | custom-call | flops 4831838208 | bytes 12582912 | tf_op jit(solution)/shard_map/pallas_call | solution.py:422
  129.7 4.1 %attend_grad_remote.1 = (f32[8,128,1536]{2,1,0:T(8,128)S(1)}, f32[1024,256]{1,0:T(8,128)S(1)}, f32[512,256]{1,0:T(8,128)S(1)}, f32[512,256]{1,0:T(8,128)}) custom-call(s32[4096]{0:T(1024)S(1)} %constant_dynamic-update-slice_fusion.seg_ref.refs_0_, s32[2]{0:T(128)S(1)} %pad_add_fusion.1.ids_ref.refs_1_, bf16[2048,768]{1,0:T(8,128)(2,1)S(1)} %shard_map.118.q_ref.refs_2_, ...), custom_call_target="tpu_custom_call" | custom-call | flops 10066329600 | bytes 20971520 | tf_op jit(solution)/shard_map/attend_grad_remote/pallas_call | solution.py:406
  135.1 3.9 %shard_map.119.a_ref = bf16[384,2048]{1,0:T(8,128)(2,1)} custom-call(s32[1]{0:T(128)} %bitcast.9.ids_ref, bf16[1024,1536]{1,0:T(8,128)(2,1)S(1)} %copy-done.2, bf16[1024,1536]{1,0:T(8,128)(2,1)} %collective-permute-done.6.a_oth.b_ref), custom_call_target="tpu_custom_call" | custom-call | flops 2147483648 | bytes 3145728 | tf_op jit(solution)/shard_map/pallas_call | solution.py:487
  139.6 52.1 %conditional.1 = (bf16[2048,768]{1,0:T(8,128)(2,1)}, f32[2048,256]{1,0:T(8,128)}, f32[6,384,128]{2,1,0:T(8,128)S(1)}, f32[1024,256]{1,0:T(8,128)}, f32[512,256]{1,0:T(8,128)}) conditional(s32[]{:T(128)} %bitcast.10, (s32[4096]{0:T(1024)S(1)}, s32[2]{0:T(128)S(1)}, bf16[2048,768]{1,0:T(8,128)(2,1)S(1)}, ...), branch_computations={%region_0.1_spmd, %region_1.2_spmd, %region_2.3_spmd} | conditional | flops 11274289152 | bytes 33554552 | solution.py:603
  142.2 45.1 %attend_grad_local.5 = (bf16[2048,768]{1,0:T(8,128)(2,1)}, f32[2048,256]{1,0:T(8,128)}) custom-call(s32[4096]{0:T(1024)S(1)} %get-tuple-element.99.refs_0_, s32[2]{0:T(128)S(1)} %get-tuple-element.100.refs_1_, bf16[2048,768]{1,0:T(8,128)(2,1)S(1)} %get-tuple-element.101.refs_2_, bf16[2048,768]{1,0:T(8,128)(2,1)S(1)} %get-tuple-element.102.refs_3_, ...), custom_call_target="tpu_custom_call" | custom-call | flops 10066329600 | bytes 20971520 | tf_op jit(solution)/shard_map/cond/branch_2_fun/attend_grad_local/pallas_call | solution.py:406
  187.3 4.1 %branch_2_fun.1 = f32[6,384,128]{2,1,0:T(8,128)S(1)} custom-call(bf16[384,2048]{1,0:T(8,128)(2,1)} %get-tuple-element.111.a_ref, bf16[2048,768]{1,0:T(8,128)(2,1)} %get-tuple-element.184.b_ref), custom_call_target="tpu_custom_call" | custom-call | flops 1207959552 | bytes 6291456 | tf_op jit(solution)/shard_map/cond/branch_2_fun/pallas_call | solution.py:525
  193.3 3.2 fusion.4
  196.8 7.8 %collective-permute-done.14.c_ref.d_ref = bf16[2048,256]{1,0:T(8,128)(2,1)S(1)} collective-permute-done((bf16[2048,256]{1,0:T(8,128)(2,1)S(1)}, bf16[2048,256]{1,0:T(8,128)(2,1)S(1)}, u32[]{:S(2)}, u32[]{:S(2)}) %collective-permute-start.14) | collective-permute-done | bytes 1048608 | tf_op jit(solution)/shard_map/ppermute | solution.py:552
  209.3 3.4 %shard_map.123 = f32[6,384,128]{2,1,0:T(8,128)S(1)} custom-call(bf16[384,2048]{1,0:T(8,128)(2,1)} %shard_map.119.a_ref, bf16[2048,768]{1,0:T(8,128)(2,1)S(1)} %collective-permute-done.11.b_ref.c_ref), custom_call_target="tpu_custom_call" | custom-call | flops 1207959552 | bytes 6291456 | tf_op jit(solution)/shard_map/pallas_call | solution.py:525
  214.7 3.6 %shard_map.130 = f32[6,384,128]{2,1,0:T(8,128)S(1)} custom-call(bf16[384,2048]{1,0:T(8,128)(2,1)S(1)} %copy-done.1, bf16[2048,768]{1,0:T(8,128)(2,1)} %collective-permute-done.12.b_ref.c_ref), custom_call_target="tpu_custom_call" | custom-call | flops 1207959552 | bytes 6291456 | tf_op jit(solution)/shard_map/pallas_call | solution.py:525
  222.5 5.1 %collective-permute-done.17 = f32[4,384,128]{2,1,0:T(8,128)S(1)} collective-permute-done((f32[4,384,128]{2,1,0:T(8,128)S(1)}, f32[4,384,128]{2,1,0:T(8,128)S(1)}, u32[]{:S(2)}, u32[]{:S(2)}) %collective-permute-start.17) | collective-permute-done | bytes 786464 | tf_op jit(solution)/shard_map/ppermute | solution.py:552
  227.8 5.8 %shard_map.126 = f32[12,384,128]{2,1,0:T(8,128)S(1)} custom-call(s32[1]{0:T(128)} %bitcast.ids_ref, bf16[384,2048]{1,0:T(8,128)(2,1)S(1)} %shard_map.125.a_ref, bf16[2048,768]{1,0:T(8,128)(2,1)} %get-tuple-element.163.a_ref.b_ref, bf16[2048,768]{1,0:T(8,128)(2,1)S(1)} %collective-permute-done.11.b_ref.c_ref), custom_call_target="tpu_custom_call" | custom-call | flops 2415919104 | bytes 10485760 | tf_op jit(solution)/shard_map/pallas_call | solution.py:506
  233.6 3.4 %shard_map.128.a_ref = bf16[384,2048]{1,0:T(8,128)(2,1)S(1)} custom-call(s32[1]{0:T(128)} %bitcast.12.ids_ref, bf16[1024,1536]{1,0:T(8,128)(2,1)S(1)} %copy-done.10, bf16[1024,1536]{1,0:T(8,128)(2,1)} %collective-permute-done.10.b_ref.a_oth), custom_call_target="tpu_custom_call" | custom-call | flops 2147483648 | bytes 3145728 | tf_op jit(solution)/shard_map/pallas_call | solution.py:487
  237.1 5.7 %shard_map.129 = f32[12,384,128]{2,1,0:T(8,128)S(1)} custom-call(s32[1]{0:T(128)} %bitcast.ids_ref, bf16[384,2048]{1,0:T(8,128)(2,1)S(1)} %shard_map.128.a_ref, bf16[2048,768]{1,0:T(8,128)(2,1)S(1)} %copy-done.12, bf16[2048,768]{1,0:T(8,128)(2,1)} %collective-permute-done.12.b_ref.c_ref), custom_call_target="tpu_custom_call" | custom-call | flops 2415919104 | bytes 10485760 | tf_op jit(solution)/shard_map/pallas_call | solution.py:506
  244.4 8.7 %out_y.1 = bf16[1024,1536]{1,0:T(8,128)(2,1)} custom-call(s32[2]{0:T(128)S(1)} %pad_add_fusion.1.ids_ref.refs_1_, bf16[2048,768]{1,0:T(8,128)(2,1)S(1)} %copy-done.12, bf16[2048,768]{1,0:T(8,128)(2,1)} %collective-permute-done.12.b_ref.c_ref, bf16[12,1536,128]{2,1,0:T(8,128)(2,1)S(1)} %bitcast.29, bf16[12,1536,128]{2,1,0:T(8,128)(2,1)S(1)} %bitcast.30), custom_call_target="tpu_custom_call" | custom-call | flops 4831838208 | bytes 14680064 | tf_op jit(solution)/shard_map/out_y/pallas_call | solution.py:472
  253.1 10.3 %grad_x.1 = bf16[1024,1536]{1,0:T(8,128)(2,1)} custom-call(s32[2]{0:T(128)S(1)} %pad_add_fusion.1.ids_ref.refs_1_, bf16[2048,768]{1,0:T(8,128)(2,1)} %get-tuple-element.163.a_ref.b_ref, bf16[2048,768]{1,0:T(8,128)(2,1)S(1)} %collective-permute-done.11.b_ref.c_ref, bf16[12,1536,128]{2,1,0:T(8,128)(2,1)S(1)} %bitcast.36, bf16[12,1536,128]{2,1,0:T(8,128)(2,1)S(1)} %bitcast.37, ...), custom_call_target="tpu_custom_call" | custom-call | flops 4831838208 | bytes 14680064 | tf_op jit(solution)/shard_map/grad_x/pallas_call | solution.py:472
  263.5 64.5 %collective-permute-done.19 = f32[6,384,128]{2,1,0:T(8,128)S(1)} collective-permute-done((f32[6,384,128]{2,1,0:T(8,128)S(1)}, f32[6,384,128]{2,1,0:T(8,128)S(1)}, u32[]{:S(2)}, u32[]{:S(2)}) %collective-permute-start.19) | collective-permute-done | bytes 1179680 | tf_op jit(solution)/shard_map/ppermute | solution.py:552
  (102 shorter events, 30.3 us)
Async XLA Ops:
  0.7 23.9 %slice-start.4 = ((s8[4718592]{0:T(1024)(128)(4,1)}), s8[524288]{0:T(1024)(128)(4,1)S(1)}, s32[]{:S(2)}) async-start(s8[4718592]{0:T(1024)(128)(4,1)} %bitcast.31), calls=%async_computation.4 | async-start | bytes 1048576
  6.4 12.7 %collective-permute-start.10 = (bf16[1024,1536]{1,0:T(8,128)(2,1)}, bf16[1024,1536]{1,0:T(8,128)(2,1)}, u32[]{:S(2)}, u32[]{:S(2)}) collective-permute-start(bf16[1024,1536]{1,0:T(8,128)(2,1)} %a_ref.7), channel_id=1, source_target_pairs={{0,1},{1,0},{2,3},{3,2},{4,5},{5,4},{6,7},{7,6}} | collective-permute-start | bytes 9437192 | tf_op jit(solution)/shard_map/ppermute | solution.py:552
  7.3 17.3 %collective-permute-start.6 = (bf16[1024,1536]{1,0:T(8,128)(2,1)}, bf16[1024,1536]{1,0:T(8,128)(2,1)}, u32[]{:S(2)}, u32[]{:S(2)}) collective-permute-start(bf16[1024,1536]{1,0:T(8,128)(2,1)} %a_ref.6), channel_id=1, source_target_pairs={{0,1},{1,0},{2,3},{3,2},{4,5},{5,4},{6,7},{7,6}} | collective-permute-start | bytes 9437192 | tf_op jit(solution)/shard_map/ppermute | solution.py:552
  7.3 6.3 %collective-permute-start.3 = (s32[1024]{0:T(1024)S(1)}, s32[1024]{0:T(1024)S(1)}, u32[]{:S(2)}, u32[]{:S(2)}) collective-permute-start(s32[1024]{0:T(1024)S(1)} %copy-done.15), channel_id=1, source_target_pairs={{0,2},{1,3},{4,6},{5,7}} | collective-permute-start | bytes 12296 | tf_op jit(solution)/shard_map/ppermute | solution.py:552
  12.1 5.5 %collective-permute-start.4 = (s32[1024]{0:T(1024)S(1)}, s32[1024]{0:T(1024)S(1)}, u32[]{:S(2)}, u32[]{:S(2)}) collective-permute-start(s32[1024]{0:T(1024)S(1)} %copy-done.15), channel_id=1, source_target_pairs={{0,3},{1,2},{4,7},{5,6}} | collective-permute-start | bytes 12296 | tf_op jit(solution)/shard_map/ppermute | solution.py:552
  13.4 5.6 %collective-permute-start.5 = (s32[1024]{0:T(1024)S(1)}, s32[1024]{0:T(1024)S(1)}, u32[]{:S(2)}, u32[]{:S(2)}) collective-permute-start(s32[1024]{0:T(1024)S(1)} %copy-done.15), channel_id=1, source_target_pairs={{0,1},{1,0},{2,3},{3,2},{4,5},{5,4},{6,7},{7,6}} | collective-permute-start | bytes 12296 | tf_op jit(solution)/shard_map/ppermute | solution.py:552
  13.6 19.6 %collective-permute-start.7 = (bf16[1024,256]{1,0:T(8,128)(2,1)S(1)}, bf16[1024,256]{1,0:T(8,128)(2,1)S(1)}, u32[]{:S(2)}, u32[]{:S(2)}) collective-permute-start(bf16[1024,256]{1,0:T(8,128)(2,1)S(1)} %get-tuple-element.145.kv_own), channel_id=1, source_target_pairs={{0,2},{1,3},{4,6},{5,7}} | collective-permute-start | bytes 1572872 | tf_op jit(solution)/shard_map/ppermute | solution.py:552
  17.7 21.5 %collective-permute-start.8 = (bf16[1024,256]{1,0:T(8,128)(2,1)}, bf16[1024,256]{1,0:T(8,128)(2,1)S(1)}, u32[]{:S(2)}, u32[]{:S(2)}) collective-permute-start(bf16[1024,256]{1,0:T(8,128)(2,1)} %get-tuple-element.148), channel_id=1, source_target_pairs={{0,3},{1,2},{4,7},{5,6}} | collective-permute-start | bytes 1572872 | tf_op jit(solution)/shard_map/ppermute | solution.py:552
  19.1 20.1 %collective-permute-start.9 = (bf16[1024,256]{1,0:T(8,128)(2,1)}, bf16[1024,256]{1,0:T(8,128)(2,1)S(1)}, u32[]{:S(2)}, u32[]{:S(2)}) collective-permute-start(bf16[1024,256]{1,0:T(8,128)(2,1)} %get-tuple-element.148), channel_id=1, source_target_pairs={{0,1},{1,0},{2,3},{3,2},{4,5},{5,4},{6,7},{7,6}} | collective-permute-start | bytes 1572872 | tf_op jit(solution)/shard_map/ppermute | solution.py:552
  24.6 94.3 %copy-start = (bf16[384,2048]{1,0:T(8,128)(2,1)}, bf16[384,2048]{1,0:T(8,128)(2,1)S(1)}, u32[]{:S(2)}) copy-start(bf16[384,2048]{1,0:T(8,128)(2,1)S(1)} %shard_map.120.a_ref) | copy-start | bytes 4718596
  24.6 97.3 %slice-start = ((s8[4718592]{0:T(1024)(128)(4,1)}), s8[4194304]{0:T(1024)(128)(4,1)S(1)}, s32[]{:S(2)}) async-start(s8[4718592]{0:T(1024)(128)(4,1)} %bitcast.24), calls=%async_computation | async-start | bytes 8388608
  33.1 88.8 %slice-start.1 = ((s8[4718592]{0:T(1024)(128)(4,1)}), s8[524288]{0:T(1024)(128)(4,1)S(1)}, s32[]{:S(2)}) async-start(s8[4718592]{0:T(1024)(128)(4,1)} %bitcast.24), calls=%async_computation.1 | async-start | bytes 1048576
  118.8 20.8 %copy-start.11 = (bf16[2048,768]{1,0:T(8,128)(2,1)}, bf16[2048,768]{1,0:T(8,128)(2,1)S(1)}, u32[]{:S(2)}) copy-start(bf16[2048,768]{1,0:T(8,128)(2,1)S(1)} %get-tuple-element.158.b_ref.refs_4_.a_ref) | copy-start | bytes 9437188
  133.8 59.5 %collective-permute-start.13 = (f32[512,256]{1,0:T(8,128)}, f32[512,256]{1,0:T(8,128)}, u32[]{:S(2)}, u32[]{:S(2)}) collective-permute-start(f32[512,256]{1,0:T(8,128)} %get-tuple-element.162), channel_id=1, source_target_pairs={{2,0},{3,1},{6,4},{7,5}} | collective-permute-start | bytes 1572872 | tf_op jit(solution)/shard_map/ppermute | solution.py:552
  139.6 51.9 %collective-permute-start.1 = (f32[1024,256]{1,0:T(8,128)S(1)}, f32[1024,256]{1,0:T(8,128)}, u32[]{:S(2)}, u32[]{:S(2)}) collective-permute-start(f32[1024,256]{1,0:T(8,128)S(1)} %get-tuple-element.112), channel_id=1, source_target_pairs={{2,0},{3,1},{6,4},{7,5}} | collective-permute-start | bytes 3145736 | tf_op jit(solution)/shard_map/cond/branch_2_fun/ppermute | solution.py:552
  140.9 50.5 %collective-permute-start.2 = (f32[512,256]{1,0:T(8,128)S(1)}, f32[512,256]{1,0:T(8,128)}, u32[]{:S(2)}, u32[]{:S(2)}) collective-permute-start(f32[512,256]{1,0:T(8,128)S(1)} %get-tuple-element.113), channel_id=1, source_target_pairs={{2,0},{3,1},{6,4},{7,5}} | collective-permute-start | bytes 1572872 | tf_op jit(solution)/shard_map/cond/branch_2_fun/ppermute | solution.py:552
  192.8 16.6 %collective-permute-start.11 = (bf16[2048,768]{1,0:T(8,128)(2,1)}, bf16[2048,768]{1,0:T(8,128)(2,1)S(1)}, u32[]{:S(2)}, u32[]{:S(2)}) collective-permute-start(bf16[2048,768]{1,0:T(8,128)(2,1)} %get-tuple-element.163.a_ref.b_ref), channel_id=1, source_target_pairs={{0,1},{1,0},{2,3},{3,2},{4,5},{5,4},{6,7},{7,6}} | collective-permute-start | bytes 9437192 | tf_op jit(solution)/shard_map/ppermute | solution.py:552
  192.8 21.9 %collective-permute-start.12 = (bf16[2048,768]{1,0:T(8,128)(2,1)}, bf16[2048,768]{1,0:T(8,128)(2,1)}, u32[]{:S(2)}, u32[]{:S(2)}) collective-permute-start(bf16[2048,768]{1,0:T(8,128)(2,1)} %copy-done.11), channel_id=1, source_target_pairs={{0,1},{1,0},{2,3},{3,2},{4,5},{5,4},{6,7},{7,6}} | collective-permute-start | bytes 9437192 | tf_op jit(solution)/shard_map/ppermute | solution.py:552
  196.8 7.8 %collective-permute-start.14 = (bf16[2048,256]{1,0:T(8,128)(2,1)S(1)}, bf16[2048,256]{1,0:T(8,128)(2,1)S(1)}, u32[]{:S(2)}, u32[]{:S(2)}) collective-permute-start(bf16[2048,256]{1,0:T(8,128)(2,1)S(1)} %pad_maximum_fusion.b_ref.c_ref), channel_id=1, source_target_pairs={{0,1},{1,0},{2,3},{3,2},{4,5},{5,4},{6,7},{7,6}} | collective-permute-start | bytes 3145736 | tf_op jit(solution)/shard_map/ppermute | solution.py:552
  207.2 20.4 %collective-permute-start.17 = (f32[4,384,128]{2,1,0:T(8,128)S(1)}, f32[4,384,128]{2,1,0:T(8,128)S(1)}, u32[]{:S(2)}, u32[]{:S(2)}) collective-permute-start(f32[4,384,128]{2,1,0:T(8,128)S(1)} %shard_map.124), channel_id=1, source_target_pairs={{0,2},{2,0},{1,3},{3,1},{4,6},{6,4},{5,7},{7,5}} | collective-permute-start | bytes 2359304 | tf_op jit(solution)/shard_map/ppermute | solution.py:552
  207.3 56.2 %collective-permute-start.18 = (f32[6,384,128]{2,1,0:T(8,128)S(1)}, f32[6,384,128]{2,1,0:T(8,128)S(1)}, u32[]{:S(2)}, u32[]{:S(2)}) collective-permute-start(f32[6,384,128]{2,1,0:T(8,128)S(1)} %copy-done.5), channel_id=1, source_target_pairs={{0,2},{2,0},{1,3},{3,1},{4,6},{6,4},{5,7},{7,5}} | collective-permute-start | bytes 3538952 | tf_op jit(solution)/shard_map/ppermute | solution.py:552
  209.3 120.3 %collective-permute-start.15 = (f32[6,384,128]{2,1,0:T(8,128)S(1)}, f32[6,384,128]{2,1,0:T(8,128)S(1)}, u32[]{:S(2)}, u32[]{:S(2)}) collective-permute-start(f32[6,384,128]{2,1,0:T(8,128)S(1)} %copy-done.14), channel_id=1, source_target_pairs={{0,2},{2,0},{1,3},{3,1},{4,6},{6,4},{5,7},{7,5}} | collective-permute-start | bytes 3538952 | tf_op jit(solution)/shard_map/ppermute | solution.py:552
  212.8 116.8 %collective-permute-start.16 = (f32[6,384,128]{2,1,0:T(8,128)S(1)}, f32[6,384,128]{2,1,0:T(8,128)S(1)}, u32[]{:S(2)}, u32[]{:S(2)}) collective-permute-start(f32[6,384,128]{2,1,0:T(8,128)S(1)} %shard_map.123), channel_id=1, source_target_pairs={{0,2},{2,0},{1,3},{3,1},{4,6},{6,4},{5,7},{7,5}} | collective-permute-start | bytes 3538952 | tf_op jit(solution)/shard_map/ppermute | solution.py:552
  218.3 109.6 %collective-permute-start.19 = (f32[6,384,128]{2,1,0:T(8,128)S(1)}, f32[6,384,128]{2,1,0:T(8,128)S(1)}, u32[]{:S(2)}, u32[]{:S(2)}) collective-permute-start(f32[6,384,128]{2,1,0:T(8,128)S(1)} %shard_map.130), channel_id=1, source_target_pairs={{0,2},{2,0},{1,3},{3,1},{4,6},{6,4},{5,7},{7,5}} | collective-permute-start | bytes 3538952 | tf_op jit(solution)/shard_map/ppermute | solution.py:552
  (19 other events, 118.7 us)
